TPU v7x, 32 devices: a whole 2x2x4 slice. The times are simulated.
32 devices in a mesh: tower: 2 (over x), dp: 16 (over z, y, core).
Axes of the slice: x: 2, y: 2, z: 4, core: 2. Of those that a mesh axis runs over, the one named last changes fastest.
Arguments:
- images: bfloat16 [288, 50, 768], P('dp'), may hold values from -6 to 6
- captions: bfloat16 [864, 16, 768], P('dp'), may hold values from -6 to 6
- token_ids: int32 [864, 16], P('dp'), may hold values from 0 to 31999, as said below
- counts: int32 [288], P('dp'), may hold values from 1 to 5, as said below
- matches: int32 [864], P('dp'), may hold values from 0 to 287, as said below
- image_weights: bfloat16 [9216, 768], P('dp')
- image_norms: float32 [4, 768], replicated, may hold values from -1.2 to 1.2, as said below
- weights: float32 [9216, 768], P(('tower', 'dp'))
- norm_params: float32 [4, 768], replicated, may hold values from -1.2 to 1.2, as said below
- momentum: float32 [9216, 768], P(('tower', 'dp'))
- norm_momentum: float32 [4, 768], replicated
- averages: float32 [9216, 768], P(('tower', 'dp'))
- norm_averages: float32 [4, 768], replicated, may hold values from -1.2 to 1.2
Outputs:
- grads: float32 [9216, 768], P(('tower', 'dp'))
- norm_grads: float32 [4, 768], replicated
- input_grad: float32 [864, 16, 768], P('dp', None, 'tower')
- new_weights: float32 [9216, 768], P(('tower', 'dp'))
- new_momentum: float32 [9216, 768], P(('tower', 'dp'))
- new_averages: float32 [9216, 768], P(('tower', 'dp'))
- new_norm_params: float32 [4, 768], replicated
- new_norm_momentum: float32 [4, 768], replicated
- new_norm_averages: float32 [4, 768], replicated
- grad_norm: float32 [], replicated
Inputs may be any that keep to these rules, and one draw needn't show every extreme that they name: `token_ids`: in each caption the ids are nonzero on a leading run of 4 to 16 positions and 0 after it. counts[i] is the number of captions c with matches[c] = i; the counts sum to 864. `matches`: image i is named by exactly counts[i] captions. `norm_params`: rows 0 and 2 are gains, rows 1 and 3 biases. `image_norms`: rows 0 and 2 are gains, rows 1 and 3 biases.
All inputs are finite; a program needn't handle non-finite values.
Results may differ from a plain program's by a relative error of at most 0.014.
The roundings to bfloat16 on the way count: a program that leaves them out, or rounds other values in their place, can miss the bound.
Values may be sent and summed in bfloat16 or wider, within the bound.
No kernel may reach another device: no remote copies, remote signals or barrier semaphores. Data moves between devices by JAX's collectives and lax.ppermute only.
A program may use at most 320 MiB of HBM per device.

v0:
```python
from functools import partial
import math

import jax
import jax.numpy as jnp
from jax import lax
from jax.sharding import PartitionSpec as P

HEADS = 12


EPSILON = 1e-06
LOGIT_SCALE = 50.0
CLIP_NORM = 1.0
MOMENTUM_RATE = 0.9
DECAY_RATE = 0.0001
AVERAGE_RATE = 0.7


def passed_along(block, axis, distance):
    devices = range(lax.axis_size(axis))
    route = [(i - distance, i) for i in devices if i - distance in devices]
    return lax.ppermute(block, axis, route)


def layer_norm(rows_in, scaling, offset):
    middle = jnp.mean(rows_in, axis=-1, keepdims=True)
    centred = rows_in - middle
    spread = jnp.mean(centred * centred, axis=-1, keepdims=True)
    return centred * lax.rsqrt(spread + EPSILON) * scaling + offset


def split_packed(packed):
    features = packed.shape[1]
    hidden_units = (packed.shape[0] - 4 * features) // 2
    return (
        packed[: 3 * features],
        packed[3 * features : 4 * features],
        packed[4 * features : 4 * features + hidden_units],
        packed[4 * features + hidden_units :],
    )


def masked_scores(queries, key_rows, causal):
    scores = jnp.einsum(
        "nqhd,nkhd->nhqk", queries, key_rows, preferred_element_type=jnp.float32
    ) * queries.shape[-1] ** (-0.5)
    if causal:
        seq_length = queries.shape[1]
        causal_mask = lax.broadcasted_iota(
            jnp.int32, (seq_length, seq_length), 0
        ) >= lax.broadcasted_iota(jnp.int32, (seq_length, seq_length), 1)
        scores = jnp.where(causal_mask, scores, -1e30)
    return scores


def block_forward(rows_in, packed, norms, causal):
    qkv_matrix, out_matrix, up_matrix, down_matrix = split_packed(packed)
    seq_count, seq_length, features = rows_in.shape
    normed = layer_norm(rows_in, norms[0], norms[1]).astype(jnp.bfloat16)
    joined = jnp.einsum(
        "nld,ed->nle", normed, qkv_matrix, preferred_element_type=jnp.float32
    ).astype(jnp.bfloat16)
    joined = joined.reshape(seq_count, seq_length, 3, HEADS, features // HEADS)
    scores = masked_scores(joined[:, :, 0], joined[:, :, 1], causal)
    highest = jnp.max(scores, axis=-1, keepdims=True)
    exponent = jnp.exp(scores - highest)
    totals = jnp.sum(exponent, axis=-1, keepdims=True)
    attn_probs = (exponent / totals).astype(jnp.bfloat16)
    log_total = highest + jnp.log(totals)
    attended = jnp.einsum(
        "nhqk,nkhd->nqhd", attn_probs, joined[:, :, 2], preferred_element_type=jnp.float32
    )
    attended = attended.astype(jnp.bfloat16).reshape(seq_count, seq_length, features)
    hidden = rows_in + jnp.einsum(
        "nld,ed->nle", attended, out_matrix, preferred_element_type=jnp.float32
    )
    normed_mid = layer_norm(hidden, norms[2], norms[3]).astype(jnp.bfloat16)
    pre_act = jnp.einsum("nld,fd->nlf", normed_mid, up_matrix, preferred_element_type=jnp.float32)
    activated = jax.nn.gelu(pre_act, approximate=True).astype(jnp.bfloat16)
    block_out = hidden + jnp.einsum(
        "nlf,fd->nld", activated, down_matrix, preferred_element_type=jnp.float32
    )
    return (
        (normed, joined, log_total, attended, hidden, normed_mid, pre_act, activated),
        block_out,
    )


def block_backward(grad_rows, rows_in, packed, norms, kept):
    normed, joined, log_total, attended, hidden, normed_mid, pre_act, activated = kept
    qkv_matrix, out_matrix, up_matrix, down_matrix = split_packed(packed)
    seq_count, seq_length, features = rows_in.shape
    queries, key_rows, values = (joined[:, :, 0], joined[:, :, 1], joined[:, :, 2])
    grad_branch = grad_rows.astype(jnp.bfloat16)
    grad_down_matrix = jnp.einsum(
        "nlf,nld->fd", activated, grad_branch, preferred_element_type=jnp.float32
    )
    grad_act = jnp.einsum(
        "nld,fd->nlf", grad_branch, down_matrix, preferred_element_type=jnp.float32
    ).astype(jnp.bfloat16)
    gelu_pull = jax.vjp(partial(jax.nn.gelu, approximate=True), pre_act)[1]
    grad_pre = gelu_pull(grad_act.astype(jnp.float32))[0].astype(jnp.bfloat16)
    grad_up_matrix = jnp.einsum(
        "nlf,nld->fd", grad_pre, normed_mid, preferred_element_type=jnp.float32
    )
    grad_normed_mid = jnp.einsum(
        "nlf,fd->nld", grad_pre, up_matrix, preferred_element_type=jnp.float32
    )
    mid_pull = jax.vjp(layer_norm, hidden, norms[2], norms[3])[1]
    grad_mid_part, grad_gain_mid, grad_shift_mid = mid_pull(grad_normed_mid)
    grad_hidden = grad_rows + grad_mid_part
    grad_mixed = grad_hidden.astype(jnp.bfloat16)
    grad_out_matrix = jnp.einsum(
        "nle,nld->ed", grad_mixed, attended, preferred_element_type=jnp.float32
    )
    grad_att = jnp.einsum(
        "nle,ed->nld", grad_mixed, out_matrix, preferred_element_type=jnp.float32
    ).astype(jnp.bfloat16)
    grad_att = grad_att.reshape(seq_count, seq_length, HEADS, features // HEADS)
    attn_probs = jnp.exp(masked_scores(queries, key_rows, True) - log_total)
    grad_probs = jnp.einsum("nqhd,nkhd->nhqk", grad_att, values, preferred_element_type=jnp.float32)
    grad_values = jnp.einsum(
        "nhqk,nqhd->nkhd",
        attn_probs.astype(jnp.bfloat16),
        grad_att,
        preferred_element_type=jnp.float32,
    )
    grad_scores = attn_probs * (
        grad_probs - jnp.sum(attn_probs * grad_probs, axis=-1, keepdims=True)
    )
    grad_raw = (grad_scores * queries.shape[-1] ** (-0.5)).astype(jnp.bfloat16)
    grad_queries = jnp.einsum(
        "nhqk,nkhd->nqhd", grad_raw, key_rows, preferred_element_type=jnp.float32
    )
    grad_keys = jnp.einsum("nhqk,nqhd->nkhd", grad_raw, queries, preferred_element_type=jnp.float32)
    grad_joined = jnp.stack([grad_queries, grad_keys, grad_values], axis=2).astype(jnp.bfloat16)
    grad_joined = grad_joined.reshape(seq_count, seq_length, 3 * features)
    grad_qkv_matrix = jnp.einsum(
        "nle,nld->ed", grad_joined, normed, preferred_element_type=jnp.float32
    )
    grad_normed = jnp.einsum(
        "nle,ed->nld", grad_joined, qkv_matrix, preferred_element_type=jnp.float32
    )
    first_pull = jax.vjp(layer_norm, rows_in, norms[0], norms[1])[1]
    grad_first, grad_gain_first, grad_shift_first = first_pull(grad_normed)
    matrix_grads = jnp.concatenate(
        [grad_qkv_matrix, grad_out_matrix, grad_up_matrix, grad_down_matrix], axis=0
    )
    small_grads = jnp.stack([grad_gain_first, grad_shift_first, grad_gain_mid, grad_shift_mid])
    return (matrix_grads, small_grads, grad_hidden + grad_first)


def text_blank(seq_count, seq_length, features, hidden_units):
    return (
        jnp.zeros((seq_count, seq_length, features), jnp.bfloat16),
        jnp.zeros((seq_count, seq_length, 3, HEADS, features // HEADS), jnp.bfloat16),
        jnp.zeros((seq_count, HEADS, seq_length, 1), jnp.float32),
        jnp.zeros((seq_count, seq_length, features), jnp.bfloat16),
        jnp.zeros((seq_count, seq_length, features), jnp.float32),
        jnp.zeros((seq_count, seq_length, features), jnp.bfloat16),
        jnp.zeros((seq_count, seq_length, hidden_units), jnp.float32),
        jnp.zeros((seq_count, seq_length, hidden_units), jnp.bfloat16),
        jnp.zeros((seq_count, features), jnp.float32),
        jnp.zeros((seq_count, 1), jnp.float32),
    )


def local(
    images,
    captions,
    token_ids,
    counts,
    matches,
    image_weights,
    image_norms,
    weights,
    norm_params,
    momentum,
    norm_momentum,
    averages,
    norm_averages,
):
    tower_index = lax.axis_index("tower")
    seq_count, seq_length, features = captions.shape
    frozen = lax.all_gather(image_weights, "dp", axis=0, tiled=True)
    low_shard = weights.astype(jnp.bfloat16)
    packed = lax.all_gather(low_shard, ("tower", "dp"), axis=0, tiled=True)
    hidden_units = (packed.shape[0] - 4 * features) // 2

    def image_side(operand):
        block_out = block_forward(images.astype(jnp.float32), frozen, image_norms, False)[1]
        top_rows = block_out[:, 0]
        return (
            top_rows * lax.rsqrt(jnp.sum(top_rows * top_rows, axis=-1, keepdims=True) + EPSILON)
        ).astype(jnp.bfloat16)

    def image_blank(operand):
        return jnp.zeros((images.shape[0], features), jnp.bfloat16)

    pooled_image = lax.cond(tower_index == 0, image_side, image_blank, 0)
    crossed = passed_along(pooled_image, "tower", 1)
    every_image, every_count = (
        lax.all_gather(crossed, "dp", axis=0, tiled=True),
        lax.all_gather(counts.astype(jnp.bfloat16), "dp", axis=0, tiled=True),
    )
    tokens = captions.astype(jnp.float32)
    lengths = jnp.sum((token_ids != 0).astype(jnp.int32), axis=1)
    pool_mask = (
        lax.broadcasted_iota(jnp.int32, (seq_count, seq_length), 1) == (lengths - 1)[:, None]
    ).astype(jnp.float32)

    def text_side(operand):
        kept, block_out = block_forward(tokens, packed, norm_params, True)
        pooled_rows = jnp.sum(block_out * pool_mask[:, :, None], axis=1)
        inverse = lax.rsqrt(jnp.sum(pooled_rows * pooled_rows, axis=-1, keepdims=True) + EPSILON)
        return kept + (pooled_rows, inverse)

    def text_skip(operand):
        return text_blank(seq_count, seq_length, features, hidden_units)

    forward = lax.cond(tower_index == 1, text_side, text_skip, 0)
    pooled_rows, inverse = (forward[8], forward[9])
    text_emb = (pooled_rows * inverse).astype(jnp.bfloat16)
    logits = LOGIT_SCALE * jnp.einsum(
        "cd,id->ci", text_emb, every_image, preferred_element_type=jnp.float32
    )
    row_top = jnp.max(logits, axis=1, keepdims=True)
    row_lse = row_top + jnp.log(jnp.sum(jnp.exp(logits - row_top), axis=1, keepdims=True))
    all_text = lax.all_gather(text_emb, "dp", axis=0, tiled=True)
    own_logits = LOGIT_SCALE * jnp.einsum(
        "cd,id->ci", all_text, crossed, preferred_element_type=jnp.float32
    )
    own_top = jnp.max(own_logits, axis=0)
    own_lse = own_top + jnp.log(jnp.sum(jnp.exp(own_logits - own_top[None, :]), axis=0))
    column_lse = lax.all_gather(own_lse, "dp", axis=0, tiled=True)
    target = (matches[:, None] == lax.broadcasted_iota(jnp.int32, logits.shape, 1)).astype(
        jnp.float32
    )
    grad_logits = 0.5 * (jnp.exp(logits - row_lse) - target) + 0.5 * (
        jnp.exp(logits - column_lse[None, :]) - target / every_count.astype(jnp.float32)[None, :]
    )
    scaled_grad = (LOGIT_SCALE * grad_logits).astype(jnp.bfloat16)
    grad_embed = jnp.einsum(
        "ci,id->cd", scaled_grad, every_image, preferred_element_type=jnp.float32
    )
    projection = jnp.sum(pooled_rows * grad_embed, axis=-1, keepdims=True)
    grad_pooled = inverse * grad_embed - inverse * inverse * inverse * projection * pooled_rows
    grad_rows = pool_mask[:, :, None] * grad_pooled[:, None, :]

    def text_back(operand):
        return block_backward(grad_rows, tokens, packed, norm_params, forward[:8])

    def back_skip(operand):
        return (
            jnp.zeros(packed.shape, jnp.float32),
            jnp.zeros(norm_params.shape, jnp.float32),
            jnp.zeros(tokens.shape, jnp.float32),
        )

    raw_grads, raw_norm_grads, input_full = lax.cond(tower_index == 1, text_back, back_skip, 0)
    own_grads = lax.psum_scatter(raw_grads, ("tower", "dp"), scatter_dimension=0, tiled=True)
    total_norm_grads, square_total = lax.psum(
        (raw_norm_grads, jnp.sum(own_grads * own_grads)), ("tower", "dp")
    )
    grad_norm = jnp.sqrt(square_total + jnp.sum(total_norm_grads * total_norm_grads))
    factor = jnp.minimum(1.0, CLIP_NORM / (grad_norm + 1e-06))
    grads = own_grads * factor
    norm_grads = total_norm_grads * factor
    step_rate = 0.4 * math.sqrt(packed.shape[0])
    decayed = grads + DECAY_RATE * weights
    new_momentum = MOMENTUM_RATE * momentum + decayed
    new_weights = weights - step_rate * (decayed + MOMENTUM_RATE * new_momentum)
    new_averages = AVERAGE_RATE * averages + (1.0 - AVERAGE_RATE) * new_weights
    new_norm_momentum = MOMENTUM_RATE * norm_momentum + norm_grads
    new_norm_params = norm_params - step_rate * (norm_grads + MOMENTUM_RATE * new_norm_momentum)
    new_norm_averages = AVERAGE_RATE * norm_averages + (1.0 - AVERAGE_RATE) * new_norm_params
    half_width = features // 2
    given_half = passed_along(
        input_full[:, :, :half_width].astype(jnp.bfloat16), "tower", -1
    ).astype(jnp.float32)
    input_grad = jnp.where(tower_index == 0, given_half, input_full[:, :, half_width:])
    return (
        grads,
        norm_grads,
        input_grad,
        new_weights,
        new_momentum,
        new_averages,
        new_norm_params,
        new_norm_momentum,
        new_norm_averages,
        grad_norm,
    )


def solution(mesh):
    return jax.shard_map(
        local,
        mesh=mesh,
        in_specs=(
            P("dp", None, None),
            P("dp", None, None),
            P("dp", None),
            P("dp"),
            P("dp"),
            P("dp", None),
            P(),
            P(("tower", "dp"), None),
            P(),
            P(("tower", "dp"), None),
            P(),
            P(("tower", "dp"), None),
            P(),
        ),
        out_specs=(
            P(("tower", "dp"), None),
            P(),
            P("dp", None, "tower"),
            P(("tower", "dp"), None),
            P(("tower", "dp"), None),
            P(("tower", "dp"), None),
            P(),
            P(),
            P(),
            P(),
        ),
        check_vma=False,
    )
```

profile of v0, /device:TPU:0, one launch (start us, length us, event | category | flops | bytes accessed | tf_op | source)
XLA Modules:
  0.0 870.2 jit_solution(6323068292886722784)
XLA Ops:
  7.2 2.0 convert_element_type.135
  11.8 105.6 %all-gather.6.cloned.1.call-done = bf16[9216,768]{1,0:T(8,128)(2,1)} async-done(((bf16[288,768]{1,0:T(8,128)(2,1)}), bf16[9216,768]{1,0:T(8,128)(2,1)}) %all-gather.6.cloned.1.call-update) | async-done | bytes 14155792 | tf_op jit(solution)/shard_map/all_gather | solution.py:188
  117.4 28.0 %conditional.3 = (bf16[54,16,768]{2,1,0:T(8,128)(2,1)}, bf16[54,16,3,12,64]{4,3,2,1,0:T(8,128)(2,1)}, f32[54,12,16,1]{2,1,0,3:T(8,128)S(1)}, bf16[54,16,768]{2,1...) conditional(s32[]{:T(128)} %convert_element_type.133, () %tuple.33, ...), branch_computations={%region_1.2_spmd, %region_2.11_spmd} | conditional | flops 12316222464 | bytes 96540504 | solution.py:222
  121.6 1.8 broadcast.285
  123.4 3.0 broadcast.287
  126.5 6.4 broadcast.283
  132.9 5.2 broadcast.286
  147.4 81.1 %all-gather.8.cloned.1.call-done = bf16[9216,768]{1,0:T(8,128)(2,1)} async-done(((bf16[576,768]{1,0:T(8,128)(2,1)}), bf16[9216,768]{1,0:T(8,128)(2,1)}) %all-gather.8.cloned.1.call-update) | async-done | bytes 14155792 | tf_op jit(solution)/shard_map/all_gather | solution.py:186
  228.5 75.8 %conditional.4 = (bf16[18,768]{1,0:T(8,128)(2,1)S(1)}) conditional(s32[]{:T(128)} %convert_element_type.140, () %tuple.35, (bf16[18,50,768]{2,1,0:T(8,128)(2,1)}, f32[4,768]{1,0:T(4,128)S(1)}, bf16[9216,768]{1,0:T(8,128)(2,1)}) %tuple.93), branch_computations={%region_11.12_spmd, %region_12.20_spmd} | conditional | flops 12925296640 | bytes 90307072 | solution.py:201
  228.6 1.8 convert_reduce_fusion
  230.4 2.0 fusion.53
  232.4 8.0 convolution_convert_fusion.1
  240.4 11.5 %reshape.256 = bf16[18,50,3,12,64]{4,3,2,1,0:T(8,128)(2,1)} reshape(bf16[18,50,2304]{2,1,0:T(8,128)(2,1)} %convolution_convert_fusion.1) | data formatting | bytes 8294400 | tf_op jit(solution)/shard_map/cond/branch_1_fun/reshape | solution.py:64
  251.8 5.5 fusion.164
  259.1 10.1 %fusion.165 = (f32[18,12,50]{2,1,0:T(8,128)S(1)}, f32[18,12,50,50]{2,3,1,0:T(8,128)S(1)}) fusion(f32[18,12,50,50]{2,3,1,0:T(8,128)S(1)} %fusion.58), kind=kOutput, calls=%fused_computation.269 | output fusion | flops 2160049 | bytes 4363200 | tf_op jit(solution)/shard_map/cond/branch_1_fun/sub | solution.py:67
  269.2 1.8 convert_bitcast_fusion.1
  271.0 2.6 copy.79
  273.6 5.9 reshape.257
  279.5 3.8 fusion.166
  285.5 17.2 %fusion.39 = f32[18,50,768]{2,1,0:T(8,128)} fusion(bf16[9216,768]{1,0:T(8,128)(2,1)} %get-tuple-element.113, f32[18,50,768]{2,1,0:T(8,128)} %copy-done.10, f32[768]{0:T(1024)S(1)} %get-tuple-element.225, f32[768]{0:T(1024)S(1)} %get-tuple-element.222, f32[18,50]{1,0:T(8,128)S(1)} %add_rsqrt_fusion.2, f32[18,50]{1,0:T(8,128)S(1)} %broadcast_multiply_fusion.2), kind=kOutput, calls=%fused_computation.67 | convolution fusion | flops 8521804800 | bytes 15311904 | tf_op jit(solution)/shard_map/cond/branch_1_fun/nlf,fd->nld/dot_general | solution.py:81
  307.8 30.5 %all-reduce.1 = bf16[288]{0:T(512)(128)(2,1)S(1)} all-reduce(bf16[288]{0:T(512)(128)(2,1)S(1)} %dynamic-update-slice.1), channel_id=1, replica_groups=mesh['tower'=2,'dp'=16] {'dp'}, use_global_device_ids=true, to_apply=%add.1 | all-reduce | flops 288 | bytes 1152
  338.9 19.0 %all-gather = bf16[16,18,768]{2,1,0:T(8,128)(2,1)S(1)} all-gather(bf16[1,18,768]{2,1,0:T(8,128)(2,1)S(1)} %bitcast.168), channel_id=1, replica_groups=mesh['tower'=2,'dp'=16] {'dp'}, dimensions={0}, use_global_device_ids=true | all-gather | bytes 470016 | tf_op jit(solution)/shard_map/all_gather | solution.py:204
  361.7 2.4 reshape.268
  364.1 1.9 fusion.167
  366.3 31.7 %all-reduce = f32[288]{0:T(512)} all-reduce(f32[288]{0:T(512)S(1)} %add_dynamic-update-slice_fusion), channel_id=1, replica_groups=mesh['tower'=2,'dp'=16] {'dp'}, use_global_device_ids=true, to_apply=%add | all-reduce | flops 288 | bytes 2304
  400.0 12.9 %conditional.5 = (f32[9216,768]{1,0:T(8,128)}, f32[4,768]{1,0:T(4,128)}, f32[54,16,768]{2,1,0:T(8,128)S(1)}) conditional(s32[]{:T(128)} %convert_element_type.133, () %tuple.32, (bf16[54,16,3,12,64]{4,3,2,1,0:T(8,128)(2,1)}, f32[54,12,16,1]{2,1,0,3:T(8,128)S(1)}, f32[54,16,1]{1,0,2:T(8,128)}, f32[54,768]{1,0:T(8,128)S(1)}, ...), branch_computations={%region_24.25_spmd, %region_25.40_spmd} | conditional | flops 24696150016 | bytes 398636160 | solution.py:261
  400.9 9.5 %broadcast.307 = f32[9216,768]{1,0:T(8,128)} broadcast(f32[]{:T(128)} %constant.88.clone), dimensions={} | broadcast | bytes 28311556 | tf_op jit(solution)/shard_map/broadcast.59
  414.4 154.4 %collective-permute-done.1 = bf16[54,16,384]{2,1,0:T(8,128)(2,1)S(1)} collective-permute-done((bf16[54,16,384]{2,1,0:T(8,128)(2,1)S(1)}, bf16[54,16,384]{2,1,0:T(8,128)(2,1)S(1)}, u32[]{:S(2)}, u32[]{:S(2)}) %collective-permute-start.1) | collective-permute-done | bytes 663584 | tf_op jit(solution)/shard_map/ppermute | solution.py:23
  570.0 242.4 %reduce-scatter.2.cloned.1.call-done = f32[288,768]{1,0:T(8,128)} async-done(((f32[9216,768]{1,0:T(8,128)}), f32[288,768]{1,0:T(8,128)}) %reduce-scatter.2.cloned.1.call-update) | async-done | bytes 884752 | tf_op jit(solution)/shard_map/reduce_scatter | solution.py:262
  812.4 2.0 multiply_reduce_fusion.14
  814.4 40.6 %all-reduce.2 = (f32[]{:T(128)}, f32[4,768]{1,0:T(4,128)S(1)}) all-reduce(f32[]{:T(128)} %multiply_reduce_fusion.14, f32[4,768]{1,0:T(4,128)} %get-tuple-element.164), channel_id=1, replica_groups=mesh['tower'=2,'dp'=16] {'tower','dp'}, use_global_device_ids=true, to_apply=%region_42.0 | all-reduce | flops 3073 | bytes 24584 | tf_op jit(solution)/shard_map/psum | solution.py:263
  858.4 3.7 multiply_add_fusion.3
  (83 shorter events, 29.2 us)
Async XLA Ops:
  7.2 4.6 copy-start.23
  7.2 110.2 %copy-start.18 = (f32[4,768]{1,0:T(4,128)S(1)}, f32[4,768]{1,0:T(4,128)}, u32[]{:S(2)}) copy-start(f32[4,768]{1,0:T(4,128)} %param.27) | copy-start | bytes 36868
  7.2 110.2 %all-gather.6.cloned.1.call-start = ((), (), s32[]{:S(2)}) async-start(), calls=%async_computation.1 | async-start | bytes 14598144 | tf_op jit(solution)/shard_map/all_gather | solution.py:188
  9.2 219.3 %all-gather.8.cloned.1.call-start = ((), (), s32[]{:S(2)}) async-start(), calls=%async_computation.2 | async-start | bytes 15040512 | tf_op jit(solution)/shard_map/all_gather | solution.py:186
  10.0 351.7 %all-gather.10.cloned.1.call-start = ((), (), s32[]{:S(2)}) async-start(), calls=%async_computation.4 | async-start | bytes 1462272 | tf_op jit(solution)/shard_map/all_gather | solution.py:230
  117.4 111.1 %copy-start.20 = (f32[4,768]{1,0:T(4,128)S(1)}, f32[4,768]{1,0:T(4,128)}, u32[]{:S(2)}) copy-start(f32[4,768]{1,0:T(4,128)} %param.25) | copy-start | bytes 36868
  145.5 83.0 %copy-start.13 = (f32[54,12,16,1]{2,1,0,3:T(8,128)}, f32[54,12,16,1]{2,1,0,3:T(8,128)S(1)}, u32[]{:S(2)}) copy-start(f32[54,12,16,1]{2,1,0,3:T(8,128)S(1)} %get-tuple-element.154) | copy-start | bytes 124420
  145.5 213.3 %copy-start.24 = (f32[54,1]{0,1:T(1,128)}, f32[54,1]{0,1:T(1,128)S(1)}, u32[]{:S(2)}) copy-start(f32[54,1]{0,1:T(1,128)S(1)} %get-tuple-element.155) | copy-start | bytes 652
  147.3 665.1 %reduce-scatter.2.cloned.1.call-start = ((), (), s32[]{:S(2)}) async-start(), calls=%async_computation.3 | async-start | bytes 29196288 | tf_op jit(solution)/shard_map/reduce_scatter | solution.py:262
  228.5 77.8 %copy-start.25 = (s32[18]{0:T(128)S(1)}, s32[18]{0:T(128)}, u32[]{:S(2)}) copy-start(s32[18]{0:T(128)} %param.22) | copy-start | bytes 220
  228.5 77.8 %copy-start.26 = (u32[32]{0:T(128)S(1)}, u32[32]{0:T(128)}, u32[]{:S(2)}) copy-start(u32[32]{0:T(128)} %constant.158) | copy-start | bytes 388
  228.5 3.9 copy-start.7
  283.3 1.7 copy-start.10
  304.3 34.6 %collective-permute-start = (bf16[18,768]{1,0:T(8,128)(2,1)S(1)}, bf16[18,768]{1,0:T(8,128)(2,1)S(1)}, u32[]{:S(2)}, u32[]{:S(2)}) collective-permute-start(bf16[18,768]{1,0:T(8,128)(2,1)S(1)} %get-tuple-element.300), channel_id=1, source_target_pairs={{0,16},{1,17},{2,18},{3,19},{4,20},{5,21},{6,22},{7,23},{8,24},{9,... | collective-permute-start | bytes 82952 | tf_op jit(solution)/shard_map/ppermute | solution.py:23
  338.9 19.0 %copy-start.16 = (bf16[18,768]{1,0:T(8,128)(2,1)}, bf16[18,768]{1,0:T(8,128)(2,1)S(1)}, u32[]{:S(2)}) copy-start(bf16[18,768]{1,0:T(8,128)(2,1)S(1)} %collective-permute-done) | copy-start | bytes 82948
  358.8 39.2 %copy-start.12 = (bf16[288,768]{1,0:T(8,128)(2,1)S(1)}, bf16[288,768]{1,0:T(8,128)(2,1)}, u32[]{:S(2)}) copy-start(bf16[288,768]{1,0:T(8,128)(2,1)} %reshape.266) | copy-start | bytes 1327108
  358.8 41.2 %copy-start.14 = (f32[54,12,16,1]{2,1,0,3:T(8,128)S(1)}, f32[54,12,16,1]{2,1,0,3:T(8,128)}, u32[]{:S(2)}) copy-start(f32[54,12,16,1]{2,1,0,3:T(8,128)} %copy-done.13) | copy-start | bytes 124420
  360.4 0.6 copy-start.15
  412.9 445.5 %copy-start.9 = (f32[288,768]{1,0:T(8,128)S(1)}, f32[288,768]{1,0:T(8,128)}, u32[]{:S(2)}) copy-start(f32[288,768]{1,0:T(8,128)} %param.26) | copy-start | bytes 2654212
  413.0 155.8 %collective-permute-start.1 = (bf16[54,16,384]{2,1,0:T(8,128)(2,1)S(1)}, bf16[54,16,384]{2,1,0:T(8,128)(2,1)S(1)}, u32[]{:S(2)}, u32[]{:S(2)}) collective-permute-start(bf16[54,16,384]{2,1,0:T(8,128)(2,1)S(1)} %slice.206), channel_id=1, source_target_pairs={{16,0},{17,1},{18,2},{19,3},{20,4},{21,5},{22,6},{23,7},{24,8},{25... | collective-permute-start | bytes 1990664 | tf_op jit(solution)/shard_map/ppermute | solution.py:23
Sparse Core Ops, SparseCore 0:
  11.5 105.8 all-gather.5
  119.7 108.7 all-gather.7
  230.7 37.1 all-gather.9
  413.0 399.3 reduce-scatter.1
where the time goes:
time: 877 us; the launch traced here: 870 us
  waiting for transfers between devices  584 us (67%)
  blocking collectives  122 us (14%)
  local copies, waits for them, and re-layouts  63.9 us (7%)
  matrix products  37.2 us (4%)
  other arithmetic  32.5 us (4%)
  between operations  17.6 us (2%)
  loops' own time  10.1 us (1%)
    reduce_scatter x1, waiting for transfers between devices, local(): lax.psum_scatter(raw_grads, ('tower', 'dp'), scatter_dimension=0, tiled=T...  242 us
    ppermute x2, waiting for transfers between devices, passed_along(): return lax.ppermute(block, axis, route)  154 us
    all_gather x1, waiting for transfers between devices, local(): packed = lax.all_gather(low_shard, ('tower', 'dp'), axis=0, tiled=True)  106 us
    all_gather x1, waiting for transfers between devices, local(): frozen = lax.all_gather(image_weights, 'dp', axis=0, tiled=True)  81.1 us
    unnamed x2, blocking collectives  62.2 us
    psum x1, blocking collectives, local(): lax.psum((raw_norm_grads, jnp.sum(own_grads * own_grads)), ('tower', 'dp'))  40.6 us
    another operation x13, local copies, waits for them, and re-layouts  31.1 us
    all_gather x1, blocking collectives, local(): lax.all_gather(crossed, 'dp', axis=0, tiled=True)  19 us
  transfers between devices with their start and end apart: 6, of which 4 were waited for; matrix products, arithmetic and copies ran while one was open for 12% of the time, Pallas kernels for 0%

commit v1 on v0

v1 whole, which is shorter than its diff:
```python
from functools import partial
import math

import jax
import jax.numpy as jnp
import numpy as np
from jax import lax
from jax.experimental import pallas as pl
from jax.experimental.pallas import tpu as pltpu
from jax.sharding import PartitionSpec as P

HEAD_DIM = 64
GROUP = 4

EPSILON = 1e-06
LOGIT_SCALE = 50.0
CLIP_NORM = 1.0
MOMENTUM_RATE = 0.9
DECAY_RATE = 0.0001
AVERAGE_RATE = 0.7
MASKED = -1e30
GELU_A = 0.044715
GELU_C = math.sqrt(2.0 / math.pi)

f32 = jnp.float32
bf16 = jnp.bfloat16


def round_up(value, step):
    return (value + step - 1) // step * step


def dot_nn(left, right, **kw):
    return lax.dot_general(
        left, right, (((1,), (0,)), ((), ())), preferred_element_type=f32, **kw
    )


def dot_nt(left, right):
    return lax.dot_general(left, right, (((1,), (1,)), ((), ())), preferred_element_type=f32)


def dot_tn(left, right):
    return lax.dot_general(left, right, (((0,), (0,)), ((), ())), preferred_element_type=f32)


def call(kernel, outs, *args, scratch=(), name=None, flops=0):
    whole = pl.BlockSpec(memory_space=pltpu.VMEM)
    return pl.pallas_call(
        kernel,
        out_shape=outs,
        in_specs=[whole] * len(args),
        out_specs=jax.tree.map(lambda _: whole, outs),
        scratch_shapes=list(scratch),
        name=name,
    )(*args)


def sds(shape, dtype):
    return jax.ShapeDtypeStruct(shape, dtype)


def normalize(rows):
    middle = jnp.mean(rows, axis=-1, keepdims=True)
    centred = rows - middle
    spread = jnp.mean(centred * centred, axis=-1, keepdims=True)
    scale = lax.rsqrt(spread + EPSILON)
    return centred * scale, scale


def norm_pull(grad, rows, gain):
    unit, scale = normalize(rows)
    scaled = grad * gain
    pulled = scale * (
        scaled
        - jnp.mean(scaled, axis=-1, keepdims=True)
        - unit * jnp.mean(scaled * unit, axis=-1, keepdims=True)
    )
    return pulled, grad * unit


def lanes_of_heads(count):
    return lax.broadcasted_iota(jnp.int32, (count, GROUP * HEAD_DIM), 1) // HEAD_DIM


def stack_heads(block):
    lanes = lanes_of_heads(block.shape[0])
    zero = jnp.zeros_like(block)
    return jnp.concatenate([jnp.where(lanes == h, block, zero) for h in range(GROUP)], axis=0)


def unstack_heads(block):
    count = block.shape[0] // GROUP
    lanes = lanes_of_heads(count)
    total = jnp.where(lanes == 0, block[:count], 0.0)
    for h in range(1, GROUP):
        total = jnp.where(lanes == h, block[h * count : (h + 1) * count], total)
    return total


def group_slice(index, base=0):
    return pl.ds(pl.multiple_of(base + index * 256, 256), 256)


def rows_kernel(step, x_ref, pos_ref, norms_ref, normed_ref, npool_ref, xpool_ref):
    gain, offset = norms_ref[0:1, :], norms_ref[1:2, :]

    @pl.loop(0, x_ref.shape[0] // step)
    def _(i):
        here = pl.ds(pl.multiple_of(i * step, step), step)
        unit, _ = normalize(x_ref[here, :].astype(f32))
        normed_ref[here, :] = (unit * gain + offset).astype(bf16)

    count = npool_ref.shape[0]
    pick = (
        lax.broadcasted_iota(jnp.int32, (count, x_ref.shape[0]), 1) == pos_ref[...]
    ).astype(bf16)
    npool_ref[...] = dot_nn(pick, normed_ref[...]).astype(bf16)
    xpool_ref[...] = dot_nn(pick, x_ref[...])


def attend_kernel(
    normed_ref, npool_ref, xpool_ref, norms_ref, low_ref, high_ref, w_ref,
    q_ref, k_ref, v_ref, probs_ref, att_ref, hidden_ref, nm_ref,
):
    count, features = npool_ref.shape
    total = normed_ref.shape[0]
    keys = lax.broadcasted_iota(jnp.int32, (count, total), 1)
    allowed = ((keys >= low_ref[...]) & (keys < high_ref[...]))[None]

    @pl.loop(0, features // 256)
    def _(i):
        cols = group_slice(i)
        queries = dot_nt(npool_ref[...], w_ref[group_slice(i), :]).astype(bf16)
        key_rows = dot_nt(normed_ref[...], w_ref[group_slice(i, features), :]).astype(bf16)
        values = dot_nt(normed_ref[...], w_ref[group_slice(i, 2 * features), :]).astype(bf16)
        q_ref[:, cols] = queries
        k_ref[:, cols] = key_rows
        v_ref[:, cols] = values
        scores = dot_nt(stack_heads(queries), key_rows) * HEAD_DIM**-0.5
        scores = jnp.where(allowed, scores.reshape(GROUP, count, total), MASKED)
        exponent = jnp.exp(scores - jnp.max(scores, axis=-1, keepdims=True))
        probs = exponent / jnp.sum(exponent, axis=-1, keepdims=True)
        probs = probs.reshape(GROUP * count, total)
        probs_ref[i] = probs
        att_ref[:, cols] = unstack_heads(dot_nn(probs.astype(bf16), values)).astype(bf16)

    hidden = xpool_ref[...] + dot_nt(
        att_ref[...], w_ref[pl.ds(3 * features, features), :]
    )
    hidden_ref[...] = hidden
    unit, _ = normalize(hidden)
    nm_ref[...] = (unit * norms_ref[2:3, :] + norms_ref[3:4, :]).astype(bf16)


def gelu_parts(pre):
    tanh = jnp.tanh(GELU_C * (pre + GELU_A * pre * pre * pre))
    return 0.5 * (1.0 + tanh), tanh


def feed_kernel(
    nm_ref, hidden_ref, up_ref, down_ref,
    pre_ref, act_ref, pooled_ref, inverse_ref, emb_ref, total_ref,
):
    step = pl.program_id(0)
    pre = dot_nt(nm_ref[...], up_ref[...])
    pre_ref[...] = pre
    act = (pre * gelu_parts(pre)[0]).astype(bf16)
    act_ref[...] = act
    part = dot_nn(act, down_ref[...])

    @pl.when(step == 0)
    def _():
        total_ref[...] = part

    @pl.when(step > 0)
    def _():
        total_ref[...] += part

    @pl.when(step == pl.num_programs(0) - 1)
    def _():
        pooled = hidden_ref[...] + total_ref[...]
        inverse = lax.rsqrt(jnp.sum(pooled * pooled, axis=-1, keepdims=True) + EPSILON)
        pooled_ref[...] = pooled
        inverse_ref[...] = jnp.broadcast_to(inverse, inverse_ref.shape)
        emb_ref[...] = (pooled * inverse).astype(bf16)


def loss_kernel(
    chunk, slots, text_ref, img_ref, row_bias_ref, col_bias_ref, emb_ref, pooled_ref, inverse_ref,
    place_ref, count_place_ref, slot_ref, real_ref, grad_ref, branch_ref,
):
    images = img_ref.shape[0]
    count = emb_ref.shape[0]

    def body(j, carry):
        top, acc = carry
        here = pl.ds(pl.multiple_of(j * chunk, chunk), chunk)
        logits = LOGIT_SCALE * dot_nt(text_ref[here, :], img_ref[...]) + row_bias_ref[here, :]
        higher = jnp.maximum(top, jnp.max(logits, axis=0, keepdims=True))
        acc = acc * jnp.exp(top - higher) + jnp.sum(
            jnp.exp(logits - higher), axis=0, keepdims=True
        )
        return higher, acc

    top, acc = lax.fori_loop(
        0,
        text_ref.shape[0] // chunk,
        body,
        (jnp.full((1, images), MASKED, f32), jnp.zeros((1, images), f32)),
    )
    column_lse = top + jnp.log(acc)
    logits = LOGIT_SCALE * dot_nt(emb_ref[...], img_ref[...])
    masked = logits + col_bias_ref[...]
    row_top = jnp.max(masked, axis=1, keepdims=True)
    row_exp = jnp.exp(masked - row_top)
    by_row = row_exp / jnp.sum(row_exp, axis=1, keepdims=True)
    by_column = jnp.exp(masked - column_lse)
    columns = lax.broadcasted_iota(jnp.int32, (count, images), 1)
    target = (columns == place_ref[...]).astype(f32)
    listed = dot_nn((columns == count_place_ref[...]).astype(bf16), img_ref[...])
    at = lax.broadcasted_iota(jnp.int32, listed.shape, 1) == slot_ref[...]
    named = jnp.maximum(jnp.sum(jnp.where(at, listed, 0.0), axis=1, keepdims=True), 1.0)
    grad_logits = 0.5 * (by_row - target) + 0.5 * (by_column - target / named)
    scaled = jnp.where(
        (col_bias_ref[...] == 0.0) & (real_ref[...] > 0.0), LOGIT_SCALE * grad_logits, 0.0
    ).astype(bf16)
    grad_embed = dot_nn(scaled, img_ref[...])
    pooled = pooled_ref[...]
    inverse = inverse_ref[:, 0:1]
    projection = jnp.sum(pooled * grad_embed, axis=-1, keepdims=True)
    grad_pooled = inverse * grad_embed - inverse * inverse * inverse * projection * pooled
    grad_ref[...] = grad_pooled
    branch_ref[...] = grad_pooled.astype(bf16)


def feed_back_kernel(
    branch_ref, grad_ref, hidden_ref, norms_ref, pre_ref, up_ref, down_ref,
    gpre_ref, ghidden_ref, mixed_ref, sums_ref, total_ref,
):
    step = pl.program_id(0)
    pre = pre_ref[...]
    cdf, tanh = gelu_parts(pre)
    slope = cdf + pre * 0.5 * (1.0 - tanh * tanh) * GELU_C * (1.0 + 3.0 * GELU_A * pre * pre)
    grad_act = dot_nt(branch_ref[...], down_ref[...]).astype(bf16)
    gpre = (grad_act.astype(f32) * slope).astype(bf16)
    gpre_ref[...] = gpre
    part = dot_nn(gpre, up_ref[...])

    @pl.when(step == 0)
    def _():
        total_ref[...] = part

    @pl.when(step > 0)
    def _():
        total_ref[...] += part

    @pl.when(step == pl.num_programs(0) - 1)
    def _():
        grad = total_ref[...]
        pulled, by_gain = norm_pull(grad, hidden_ref[...], norms_ref[2:3, :])
        ghidden = grad_ref[...] + pulled
        ghidden_ref[...] = ghidden
        mixed_ref[...] = ghidden.astype(bf16)
        sums_ref[...] = jnp.zeros_like(sums_ref)
        sums_ref[2:3, :] = jnp.sum(by_gain, axis=0, keepdims=True)
        sums_ref[3:4, :] = jnp.sum(grad, axis=0, keepdims=True)


def attend_back_kernel(
    step, half, mixed_ref, ghidden_ref, probs_ref, q_ref, k_ref, v_ref, x_ref, pos_ref, norms_ref,
    sums_in_ref, fold_ref, w_ref,
    gatt_ref, gq_ref, craw_ref, cprob_ref, left_ref, right_ref, sums_ref, grad_ref,
):
    count, features = mixed_ref.shape
    gatt_ref[...] = dot_nn(mixed_ref[...], w_ref[pl.ds(3 * features, features), :]).astype(bf16)

    @pl.loop(0, features // 256)
    def _(i):
        cols = group_slice(i)
        gatt = stack_heads(gatt_ref[:, cols])
        queries = stack_heads(q_ref[:, cols])
        key_rows, values = k_ref[:, cols], v_ref[:, cols]
        probs = probs_ref[i]
        grad_probs = dot_nt(gatt, values)
        mean = jnp.sum(probs * grad_probs, axis=-1, keepdims=True)
        raw = (probs * (grad_probs - mean) * HEAD_DIM**-0.5).astype(bf16)
        low = probs.astype(bf16)
        gq_ref[:, cols] = unstack_heads(dot_nn(raw, key_rows)).astype(bf16)
        gk = dot_tn(raw, queries).astype(bf16)
        gv = dot_tn(low, gatt).astype(bf16)
        part = dot_nn(gk, w_ref[group_slice(i, features), :]) + dot_nn(
            gv, w_ref[group_slice(i, 2 * features), :]
        )

        @pl.when(i == 0)
        def _():
            grad_ref[...] = part

        @pl.when(i > 0)
        def _():
            grad_ref[...] += part

        fold = fold_ref[...]
        craw_ref[i] = lax.dot_general(
            fold, raw, (((0,), (1,)), ((), ())), preferred_element_type=f32
        ).astype(bf16)
        cprob_ref[i] = lax.dot_general(
            fold, low, (((0,), (1,)), ((), ())), preferred_element_type=f32
        ).astype(bf16)

    gpool = dot_nn(gq_ref[...], w_ref[pl.ds(0, features), :])
    gain = norms_ref[0:1, :]

    def body(j, carry):
        dgain, doffset = carry
        here = pl.ds(pl.multiple_of(j * step, step), step)
        pick = (
            lax.broadcasted_iota(jnp.int32, (step, count), 0) + j * step == pos_ref[...]
        ).astype(f32)
        grad = grad_ref[here, :] + dot_nn(pick, gpool, precision=lax.Precision.HIGHEST)
        pulled, by_gain = norm_pull(grad, x_ref[here, :].astype(f32), gain)
        pulled = pulled + dot_nn(pick, ghidden_ref[...], precision=lax.Precision.HIGHEST)
        left_ref[here, :] = pulled[:, :half].astype(bf16)
        right_ref[here, :] = pulled[:, half:]
        return (
            dgain + jnp.sum(by_gain, axis=0, keepdims=True),
            doffset + jnp.sum(grad, axis=0, keepdims=True),
        )

    none = jnp.zeros((1, features), f32)
    dgain, doffset = lax.fori_loop(0, left_ref.shape[0] // step, body, (none, none))
    sums_ref[...] = sums_in_ref[...]
    sums_ref[0:1, :] = dgain
    sums_ref[1:2, :] = doffset


def key_grad_kernel(compact_ref, factor_ref, normed_ref, spread_ref, row_ref, col_ref, out_ref):
    features = factor_ref.shape[1]

    @pl.loop(0, features // 256)
    def _(i):
        factor = stack_heads(factor_ref[:, group_slice(i)])
        wide = dot_nn(spread_ref[...], compact_ref[i])
        wide = jnp.where(row_ref[...] == col_ref[...], wide, 0.0).astype(bf16)
        joined = dot_nn(wide, factor).astype(bf16)
        out_ref[group_slice(i), :] = dot_tn(joined, normed_ref[...])


def owner_kernel(info_ref, a_ref, b0_ref, b1_ref, out_ref, square_ref):
    first = dot_tn(a_ref[...], b0_ref[0])
    second = dot_tn(a_ref[...], b1_ref[0])
    rows = lax.broadcasted_iota(jnp.int32, first.shape, 0)
    grad = jnp.where(rows < info_ref[2], first, second)
    place = rows + info_ref[3]
    grad = jnp.where((place < info_ref[4]) | (place >= info_ref[5]), grad, 0.0)
    out_ref[...] = grad
    square_ref[...] = jnp.sum(grad * grad, axis=0, keepdims=True)


def bits_of(axis):
    size = lax.axis_size(axis)
    return [1 << b for b in range(size.bit_length() - 1)]


def swapped(block, axis, bit):
    return lax.ppermute(block, axis, [(i, i ^ bit) for i in range(lax.axis_size(axis))])


def gathered(block, axis):
    for bit in reversed(bits_of(axis)):
        block = jnp.concatenate([block, swapped(block, axis, bit)], axis=0)
    return block


def place_in_gathered(device, axis):
    other = lax.axis_index(axis) ^ device
    order = list(reversed(bits_of(axis)))
    return sum(((other & bit) // bit) << s for s, bit in enumerate(order))


def summed_slice(block, axis):
    index = lax.axis_index(axis)
    for bit in bits_of(axis):
        half = block.shape[0] // 2
        upper = (index & bit) != 0
        sent = jnp.where(upper, block[:half], block[half:])
        kept = jnp.where(upper, block[half:], block[:half])
        block = kept + swapped(sent, axis, bit)
    return block


def share_of(index, size):
    bits = [1 << b for b in range(size.bit_length() - 1)]
    return sum(((index & bit) // bit) << (len(bits) - 1 - s) for s, bit in enumerate(bits))


def summed(block):
    for axis in ("dp", "tower"):
        for bit in bits_of(axis):
            block = block + swapped(block, axis, bit)
    return block


def local(
    images,
    captions,
    token_ids,
    counts,
    matches,
    image_weights,
    image_norms,
    weights,
    norm_params,
    momentum,
    norm_momentum,
    averages,
    norm_averages,
):
    text = lax.axis_index("tower") == 1
    index = lax.axis_index("dp")
    n = lax.axis_size("dp")
    both = ("tower", "dp")
    caps, length, features = captions.shape
    imgs, img_rows = images.shape[:2]
    text_rows = caps * length
    own_rows = weights.shape[0]
    all_rows = 2 * n * own_rows
    hidden_units = (all_rows - 4 * features) // 2
    count = round_up(max(caps, imgs), 8)
    total = round_up(max(text_rows, imgs * img_rows), 48)
    wide = GROUP * count

    low_shard = weights.astype(bf16)
    even = lax.ppermute(low_shard, both, [(2 * k, n + k) for k in range(n)])
    odd = lax.ppermute(low_shard, both, [(2 * k + 1, n + k) for k in range(n)])
    shard = jnp.where(text, jnp.concatenate([even, odd], axis=0), image_weights)
    packed = lax.all_gather(shard, "dp", axis=0, tiled=True)

    def padded(rows):
        return jnp.pad(rows.reshape(-1, features), ((0, total - rows.shape[0] * rows.shape[1]), (0, 0)))

    caption_x = padded(captions)
    lengths = jnp.sum((token_ids != 0).astype(jnp.int32), axis=1)
    start_t = jnp.arange(caps, dtype=jnp.int32) * length
    start_i = jnp.arange(imgs, dtype=jnp.int32) * img_rows

    def column(values, fill):
        return jnp.pad(values, (0, count - values.shape[0]), constant_values=fill)[:, None]

    low_t, high_t, pos_t = column(start_t, 0), column(start_t + lengths, 1), column(start_t + lengths - 1, 0)
    low_i, high_i, pos_i = column(start_i, 0), column(start_i + img_rows, 1), column(start_i, 0)
    rows_out = (
        sds((total, features), bf16),
        sds((count, features), bf16),
        sds((count, features), f32),
    )
    normed_t, npool_t, xpool_t = call(
        partial(rows_kernel, 48), rows_out, caption_x, pos_t, norm_params, name="rows"
    )
    normed_i, npool_i, xpool_i = call(
        partial(rows_kernel, 48), rows_out, padded(images), pos_i, image_norms, name="rows"
    )

    def mine(of_text, of_image):
        return jnp.where(text, of_text, of_image)

    normed, npool, xpool = mine(normed_t, normed_i), mine(npool_t, npool_i), mine(xpool_t, xpool_i)
    norms = mine(norm_params, image_norms)

    queries, key_rows, values, probs, attended, hidden, normed_mid = call(
        attend_kernel,
        (
            sds((count, features), bf16),
            sds((total, features), bf16),
            sds((total, features), bf16),
            sds((features // 256, wide, total), f32),
            sds((count, features), bf16),
            sds((count, features), f32),
            sds((count, features), bf16),
        ),
        normed, npool, xpool, norms, mine(low_t, low_i), mine(high_t, high_i),
        packed[: 4 * features],
        name="attend",
    )
    block = hidden_units // 8
    up_at, down_at = 4 * features // block, (4 * features + hidden_units) // block
    fixed = pl.BlockSpec((count, features), lambda i: (0, 0))
    up_spec = pl.BlockSpec((block, features), lambda i: (up_at + i, 0))
    down_spec = pl.BlockSpec((block, features), lambda i: (down_at + i, 0))
    slab = pl.BlockSpec((count, block), lambda i: (0, i))
    pre_act, activated, pooled, inverse, emb = pl.pallas_call(
        feed_kernel,
        grid=(8,),
        in_specs=[fixed, fixed, up_spec, down_spec],
        out_specs=(slab, slab, fixed, pl.BlockSpec((count, 128), lambda i: (0, 0)), fixed),
        out_shape=(
            sds((count, hidden_units), f32),
            sds((count, hidden_units), bf16),
            sds((count, features), f32),
            sds((count, 128), f32),
            sds((count, features), bf16),
        ),
        scratch_shapes=[pltpu.VMEM((count, features), f32)],
        name="feed",
    )(normed_mid, hidden, packed, packed)

    img_slots = round_up(imgs + 1, 8)
    count_row = jnp.pad(counts.astype(bf16), (0, features - imgs))[None]
    image_block = jnp.concatenate(
        [emb[:imgs], count_row, jnp.zeros((img_slots - imgs - 1, features), bf16)], axis=0
    )
    crossed = lax.ppermute(image_block, "tower", [(0, 1)])
    all_text = gathered(emb, "dp")
    all_images = gathered(crossed, "dp")
    owner_place = place_in_gathered(matches // imgs, "dp")
    place = column(owner_place * img_slots + matches % imgs, 0)
    count_place = column(owner_place * img_slots + imgs, 0)
    slot = column(matches % imgs, 0)
    real = (np.arange(count) < caps).astype(np.float32)[:, None]
    row_bias = np.tile(np.where(np.arange(count) < caps, 0.0, MASKED), n)[:, None]
    col_bias = np.tile(np.where(np.arange(img_slots) < imgs, 0.0, MASKED), n)[None]
    chunk = count * min(8, n)
    grad_rows, grad_branch = call(
        partial(loss_kernel, chunk, imgs),
        (sds((count, features), f32), sds((count, features), bf16)),
        all_text, all_images, jnp.asarray(row_bias, f32), jnp.asarray(col_bias, f32),
        emb, pooled, inverse, place, count_place, slot, jnp.asarray(real),
        name="loss",
    )

    grad_pre, grad_hidden, grad_mixed, sums = pl.pallas_call(
        feed_back_kernel,
        grid=(8,),
        in_specs=[
            fixed, fixed, fixed, pl.BlockSpec((4, features), lambda i: (0, 0)), slab,
            up_spec, down_spec,
        ],
        out_specs=(slab, fixed, fixed, pl.BlockSpec((8, features), lambda i: (0, 0))),
        out_shape=(
            sds((count, hidden_units), bf16),
            sds((count, features), f32),
            sds((count, features), bf16),
            sds((8, features), f32),
        ),
        scratch_shapes=[pltpu.VMEM((count, features), f32)],
        name="feed_back",
    )(grad_branch, grad_rows, hidden, norms, pre_act, packed, packed)
    half = features // 2
    groups = features // 256
    fold = (np.arange(total)[:, None] % length == np.arange(length)[None]).astype(np.float32)
    fold = jnp.asarray(fold, bf16)
    grad_att, grad_q, compact_raw, compact_prob, left, right, sums = call(
        partial(attend_back_kernel, 48, half),
        (
            sds((count, features), bf16),
            sds((count, features), bf16),
            sds((groups, length, wide), bf16),
            sds((groups, length, wide), bf16),
            sds((text_rows, half), bf16),
            sds((text_rows, features - half), f32),
            sds((8, features), f32),
        ),
        grad_mixed, grad_hidden, probs, queries, key_rows, values, caption_x,
        pos_t.reshape(1, count), norms, sums, fold, packed[: 4 * features],
        scratch=[pltpu.VMEM((total, features), f32)],
        name="attend_back",
    )

    lower = all_rows // 2 - 4 * features
    to_image = [(1, 0)]
    early = lax.ppermute(
        jnp.concatenate([queries, attended, normed_mid], axis=1), "tower", to_image
    )
    raw_x = lax.ppermute(compact_raw, "tower", to_image)
    late = lax.ppermute(
        jnp.concatenate([grad_q, grad_mixed, grad_pre[:, :lower]], axis=1), "tower", to_image
    )
    left_x = lax.ppermute(left, "tower", to_image)
    queries_x, attended_x = early[:, :features], early[:, features : 2 * features]
    mid_x = early[:, 2 * features :]
    columns = mine(
        jnp.concatenate([grad_pre[:, lower:], activated], axis=1),
        jnp.concatenate(
            [late[:, :features], jnp.zeros((count, 2 * features), bf16), late[:, features:]], axis=1
        ),
    )
    spread = columns.reshape(count, n, own_rows).transpose(1, 0, 2)
    own_columns = lax.all_to_all(spread, "dp", 0, 0, tiled=True).reshape(n * count, own_rows)
    others = jnp.stack(
        [mine(grad_branch, npool_t), mine(grad_branch, attended_x), mine(normed_mid, mid_x)]
    )
    others = lax.all_gather(others, "dp", axis=1, tiled=True)

    row_cap = jnp.asarray(np.arange(total)[:, None] // length, jnp.int32)
    col_cap = jnp.asarray(np.tile(np.arange(count), GROUP)[None], jnp.int32)
    kv_part = call(
        key_grad_kernel,
        sds((features, features), f32),
        mine(compact_prob, raw_x), mine(grad_att, queries_x), normed_t, fold, row_cap, col_cap,
        name="key_grad",
    )
    kv_share = summed_slice(kv_part, "dp")
    share_rows = features // n
    slots = own_rows // share_rows
    holder = {share_of(i, n): i for i in range(n)}
    placed = []
    for s in range(slots):
        route = []
        for owner in range(2 * n):
            row = owner * own_rows + s * share_rows
            if features <= row < 3 * features:
                tower, at = divmod((row - features) // share_rows, n)
                route.append((tower * n + holder[at], owner))
        placed.append(lax.ppermute(kv_share, both, route))
    kv_rows = jnp.concatenate(placed, axis=0)

    first_row = (lax.axis_index("tower") * n + index) * own_rows
    last_row = first_row + own_rows - 1
    up_row, down_row = 4 * features, 4 * features + hidden_units

    def other_of(row):
        in_low = jnp.where(row < 3 * features, 0, jnp.where(row < up_row, 1, 2))
        return jnp.where(row >= down_row, 0, in_low)

    edges = jnp.array([features, 3 * features, up_row, down_row], jnp.int32)
    inside = (edges > first_row) & (edges <= last_row)
    edge = jnp.min(jnp.where(inside, edges - first_row, own_rows))
    info = jnp.stack(
        [
            other_of(first_row), other_of(last_row), edge, first_row,
            jnp.int32(features), jnp.int32(3 * features),
        ]
    ).astype(jnp.int32)
    own_grads, squares = pl.pallas_call(
        owner_kernel,
        grid_spec=pltpu.PrefetchScalarGridSpec(
            num_scalar_prefetch=1,
            grid=(1,),
            in_specs=[
                pl.BlockSpec((n * count, own_rows), lambda i, s: (0, 0)),
                pl.BlockSpec((1, n * count, features), lambda i, s: (s[0], 0, 0)),
                pl.BlockSpec((1, n * count, features), lambda i, s: (s[1], 0, 0)),
            ],
            out_specs=(
                pl.BlockSpec((own_rows, features), lambda i, s: (0, 0)),
                pl.BlockSpec((1, features), lambda i, s: (0, 0)),
            ),
        ),
        out_shape=(sds((own_rows, features), f32), sds((1, features), f32)),
        name="owner",
    )(info, own_columns, others, others)

    squares = squares + jnp.sum(kv_share * kv_share, axis=0, keepdims=True)
    sums = jnp.where(text, sums, 0.0)
    sums = summed(jnp.concatenate([sums[:4], squares, sums[5:]], axis=0))
    total_norm_grads = sums[:4]
    grad_norm = jnp.sqrt(jnp.sum(sums[4]) + jnp.sum(total_norm_grads * total_norm_grads))
    factor = jnp.minimum(1.0, CLIP_NORM / (grad_norm + 1e-06))
    grads = (own_grads + kv_rows) * factor
    norm_grads = total_norm_grads * factor
    step_rate = 0.4 * math.sqrt(all_rows)
    decayed = grads + DECAY_RATE * weights
    new_momentum = MOMENTUM_RATE * momentum + decayed
    new_weights = weights - step_rate * (decayed + MOMENTUM_RATE * new_momentum)
    new_averages = AVERAGE_RATE * averages + (1.0 - AVERAGE_RATE) * new_weights
    new_norm_momentum = MOMENTUM_RATE * norm_momentum + norm_grads
    new_norm_params = norm_params - step_rate * (norm_grads + MOMENTUM_RATE * new_norm_momentum)
    new_norm_averages = AVERAGE_RATE * norm_averages + (1.0 - AVERAGE_RATE) * new_norm_params
    input_grad = jnp.where(text, right, left_x.astype(f32)).reshape(caps, length, half)
    return (
        grads,
        norm_grads,
        input_grad,
        new_weights,
        new_momentum,
        new_averages,
        new_norm_params,
        new_norm_momentum,
        new_norm_averages,
        grad_norm,
    )


def solution(mesh):
    return jax.shard_map(
        local,
        mesh=mesh,
        in_specs=(
            P("dp", None, None),
            P("dp", None, None),
            P("dp", None),
            P("dp"),
            P("dp"),
            P("dp", None),
            P(),
            P(("tower", "dp"), None),
            P(),
            P(("tower", "dp"), None),
            P(),
            P(("tower", "dp"), None),
            P(),
        ),
        out_specs=(
            P(("tower", "dp"), None),
            P(),
            P("dp", None, "tower"),
            P(("tower", "dp"), None),
            P(("tower", "dp"), None),
            P(("tower", "dp"), None),
            P(),
            P(),
            P(),
            P(),
        ),
        check_vma=False,
    )
```

time: 877 us -> 372 us (0.42)
  waiting for transfers between devices: 584 us -> 168 us
  blocking collectives: 122 us -> 0 us
  Pallas kernels: 0 us -> 81.2 us
  starting transfers between devices: 2.88 us -> 43.4 us
  matrix products: 37.2 us -> 0 us
  local copies, waits for them, and re-layouts: 63.9 us -> 31.3 us
  loops' own time: 10.1 us -> 0 us
    reduce_scatter x1 -> x0, waiting for transfers between devices: 242 us -> none  [local(): lax.psum_scatter(raw_grads, ('tower', 'dp'), scatter_dimension=0, tiled=T...]
    all_gather x3 -> x2, waiting for transfers between devices: 187 us -> 83.4 us  [the longest x1 83.4 us: local(): packed = lax.all_gather(shard, 'dp', axis=0, tiled=True)]
    pallas_call x0 -> x9, Pallas kernels: none -> 81.2 us  [the longest x6 57.1 us: call(): pl.pallas_call(kernel, out_shape=outs, in_specs=[whole] * len(args), out_...]
    ppermute x2 -> x30, waiting for transfers between devices: 154 us -> 84.5 us  [the longest x17 55 us: swapped(): lax.ppermute(block, axis, [(i, i ^ bit) for i in range(lax.axis_size(axis...]
    unnamed x2 -> x0, blocking collectives: 62.2 us -> none
    psum x1 -> x0, blocking collectives: 40.6 us -> none  [local(): lax.psum((raw_norm_grads, jnp.sum(own_grads * own_grads)), ('tower', 'dp'))]
    dot_general x8 -> x0, matrix products: 37.2 us -> none  [the longest x1 17.2 us: block_forward(): jnp.einsum('nlf,fd->nld', activated, down_matrix, preferred_element_type=...]
    ppermute x2 -> x30, starting transfers between devices: 2.72 us -> 39.5 us  [the longest x17 13.1 us: swapped(): lax.ppermute(block, axis, [(i, i ^ bit) for i in range(lax.axis_size(axis...]
  transfers between devices with their start and end apart: 6 -> 33, of which waited for: 4 -> 19; matrix products, arithmetic and copies ran while one was open for 12% -> 11% of each run, Pallas kernels for 0% -> 17%
where the time goes in v1:
time: 372 us; the launch traced here: 370 us
  waiting for transfers between devices  168 us (45%)
  Pallas kernels  81.2 us (22%)
  starting transfers between devices  43.4 us (12%)
  local copies, waits for them, and re-layouts  31.3 us (8%)
  other arithmetic  29.1 us (8%)
  between operations  17.3 us (5%)
    all_gather x1, waiting for transfers between devices, local(): packed = lax.all_gather(shard, 'dp', axis=0, tiled=True)  83.4 us
    pallas_call x6, Pallas kernels, call(): pl.pallas_call(kernel, out_shape=outs, in_specs=[whole] * len(args), out_...  57.1 us
    ppermute x17, waiting for transfers between devices, swapped(): lax.ppermute(block, axis, [(i, i ^ bit) for i in range(lax.axis_size(axis...  55 us
    ppermute x1, waiting for transfers between devices, local(): even = lax.ppermute(low_shard, both, [(2 * k, n + k) for k in range(n)])  17.4 us
    ppermute x17, starting transfers between devices, swapped(): lax.ppermute(block, axis, [(i, i ^ bit) for i in range(lax.axis_size(axis...  13.1 us
    ppermute x6, starting transfers between devices, local(): placed.append(lax.ppermute(kv_share, both, route))  10.9 us
    pallas_call x1, Pallas kernels, local(): pl.pallas_call(feed_back_kernel, grid=(8,), in_specs=[fixed, fixed, fixed...  9.79 us
    pallas_call x1, Pallas kernels, local(): pl.pallas_call(feed_kernel, grid=(8,), in_specs=[fixed, fixed, up_spec, d...  9.54 us
  transfers between devices with their start and end apart: 33, of which 19 were waited for; matrix products, arithmetic and copies ran while one was open for 11% of the time, Pallas kernels for 17%

profile of v1, /device:TPU:0, one launch (start us, length us, event | category | flops | bytes accessed | tf_op | source)
XLA Modules:
  0.0 370.1 jit_solution(15416286916546979024)
XLA Ops:
  9.2 6.2 %collective-permute-start = (bf16[288,768]{1,0:T(8,128)(2,1)S(1)}, bf16[288,768]{1,0:T(8,128)(2,1)}, u32[]{:S(2)}, u32[]{:S(2)}) collective-permute-start(bf16[288,768]{1,0:T(8,128)(2,1)S(1)} %convert_element_type.19), channel_id=1, source_target_pairs={{0,16},{2,17},{4,18},{6,19},{8,20},{10,21},{12,22},{14,23},{16,24}... | collective-permute-start | bytes 1327112 | tf_op jit(solution)/shard_map/ppermute | solution.py:435
  15.4 17.4 %collective-permute-done = bf16[288,768]{1,0:T(8,128)(2,1)} collective-permute-done((bf16[288,768]{1,0:T(8,128)(2,1)S(1)}, bf16[288,768]{1,0:T(8,128)(2,1)}, u32[]{:S(2)}, u32[]{:S(2)}) %collective-permute-start) | collective-permute-done | bytes 442400 | tf_op jit(solution)/shard_map/ppermute | solution.py:435
  32.8 2.2 maximum_select_fusion
  36.7 2.6 pad.39.x_ref
  44.9 6.6 %rows.2 = (bf16[912,768]{1,0:T(8,128)(2,1)}, bf16[56,768]{1,0:T(8,128)(2,1)}, f32[56,768]{1,0:T(8,128)}) custom-call(bf16[912,768]{1,0:T(8,128)(2,1)} %pad.39.x_ref, s32[56,1]{1,0:T(8,128)} %copy.30.pos_ref, f32[4,768]{1,0:T(4,128)} %norms_ref.2), custom_call_target="tpu_custom_call" | custom-call | tf_op jit(solution)/shard_map/rows/pallas_call | solution.py:49
  51.6 6.6 %rows.3 = (bf16[912,768]{1,0:T(8,128)(2,1)}, bf16[56,768]{1,0:T(8,128)(2,1)}, f32[56,768]{1,0:T(8,128)}) custom-call(bf16[912,768]{1,0:T(8,128)(2,1)} %pad.41.x_ref, s32[56,1]{1,0:T(8,128)} %copy.31.pos_ref, f32[4,768]{1,0:T(4,128)} %norms_ref.3), custom_call_target="tpu_custom_call" | custom-call | tf_op jit(solution)/shard_map/rows/pallas_call | solution.py:49
  61.9 2.6 broadcast_select_fusion.normed_ref
  64.5 83.4 %all-gather.3.cloned.1.call-done.up_ref.down_ref = bf16[9216,768]{1,0:T(8,128)(2,1)} async-done(((bf16[576,768]{1,0:T(8,128)(2,1)}), bf16[9216,768]{1,0:T(8,128)(2,1)}) %all-gather.3.cloned.1.call-update) | async-done | bytes 14155792 | tf_op jit(solution)/shard_map/all_gather | solution.py:438
  147.9 4.7 %slice.93.w_ref = bf16[3072,768]{1,0:T(8,128)(2,1)} slice(bf16[9216,768]{1,0:T(8,128)(2,1)} %all-gather.3.cloned.1.call-done.up_ref.down_ref), slice={[0:3072], [0:768]} | slice | bytes 9437184 | tf_op jit(solution)/shard_map/slice | solution.py:483
  152.7 10.4 %attend.1 = (bf16[56,768]{1,0:T(8,128)(2,1)}, bf16[912,768]{1,0:T(8,128)(2,1)}, bf16[912,768]{1,0:T(8,128)(2,1)}, f32[3,224,912]{2,1,0:T(8,128)}, bf16[56,768]{1...) custom-call(bf16[912,768]{1,0:T(8,128)(2,1)} %broadcast_select_fusion.normed_ref, ...), custom_call_target="tpu_custom_call" | custom-call | tf_op jit(solution)/shard_map/attend/pallas_call | solution.py:49
  163.1 9.5 %feed.1 = (f32[56,3072]{1,0:T(8,128)}, bf16[56,3072]{1,0:T(8,128)(2,1)}, f32[56,768]{1,0:T(8,128)}, f32[56,128]{1,0:T(8,128)}, bf16[56,768]{1,0:T(8,128)(2,1)}) custom-call(bf16[56,768]{1,0:T(8,128)(2,1)} %get-tuple-element.49.nm_ref, f32[56,768]{1,0:T(8,128)} %get-tuple-element.50.hidden_ref, ...), custom_call_target="tpu_custom_call" | custom-call | tf_op jit(solution)/shard_map/feed/pallas_call | solution.py:492
  175.1 3.4 collective-permute-start.6
  182.8 2.6 collective-permute-start.7
  189.8 3.5 collective-permute-done.8
  194.9 3.8 %collective-permute-done.4 = bf16[224,768]{1,0:T(8,128)(2,1)S(1)} collective-permute-done((bf16[224,768]{1,0:T(8,128)(2,1)S(1)}, bf16[224,768]{1,0:T(8,128)(2,1)S(1)}, u32[]{:S(2)}, u32[]{:S(2)}) %collective-permute-start.4) | collective-permute-done | bytes 344096 | tf_op jit(solution)/shard_map/ppermute | solution.py:367
  203.3 4.7 %loss.1 = (f32[56,768]{1,0:T(8,128)}, bf16[56,768]{1,0:T(8,128)(2,1)}) custom-call(bf16[896,768]{1,0:T(8,128)(2,1)} %copy-done.5, bf16[384,768]{1,0:T(8,128)(2,1)} %copy-done.13, f32[896,1]{1,0:T(8,128)} %constant.145.clone.row_bias_ref, f32[1,384]{1,0:T(1,128)} %constant.146.clone.col_bias_ref, bf16[56,768]{1,0:T(8,128)(2,1)} %get-tuple-element.51.emb_ref, ...), custom_call_target="tpu_custom_call" | custom-call | tf_op jit(solution)/shard_map/loss/pallas_call | solution.py:49
  208.0 9.8 %feed_back.1 = (bf16[56,3072]{1,0:T(8,128)(2,1)}, f32[56,768]{1,0:T(8,128)}, bf16[56,768]{1,0:T(8,128)(2,1)}, f32[8,768]{1,0:T(8,128)}) custom-call(bf16[56,768]{1,0:T(8,128)(2,1)} %get-tuple-element.54.branch_ref, f32[56,768]{1,0:T(8,128)} %get-tuple-element.55.grad_ref, f32[56,768]{1,0:T(8,128)} %get-tuple-element.50.hidden_ref, ...), custom_call_target="tpu_custom_call" | custom-call | tf_op jit(solution)/shard_map/feed_back/pallas_call | solution.py:532
  217.8 22.4 %attend_back.1 = (bf16[56,768]{1,0:T(8,128)(2,1)}, bf16[56,768]{1,0:T(8,128)(2,1)}, bf16[3,16,224]{2,1,0:T(8,128)(2,1)}, bf16[3,16,224]{2,1,0:T(8,128)(2,1)}, bf...) custom-call(bf16[56,768]{1,0:T(8,128)(2,1)} %get-tuple-element.59.mixed_ref, ...), custom_call_target="tpu_custom_call" | custom-call | tf_op jit(solution)/shard_map/attend_back/pallas_call | solution.py:49
  243.2 4.2 %collective-permute-done.13 = bf16[3,16,224]{2,1,0:T(8,128)(2,1)S(1)} collective-permute-done((bf16[3,16,224]{2,1,0:T(8,128)(2,1)S(1)}, bf16[3,16,224]{2,1,0:T(8,128)(2,1)S(1)}, u32[]{:S(2)}, u32[]{:S(2)}) %collective-permute-start.13) | collective-permute-done | bytes 21536 | tf_op jit(solution)/shard_map/ppermute | solution.py:575
  248.0 6.4 %key_grad.1 = f32[768,768]{1,0:T(8,128)} custom-call(bf16[3,16,224]{2,1,0:T(8,128)(2,1)} %broadcast_select_fusion.3.compact_ref, bf16[56,768]{1,0:T(8,128)(2,1)} %get-tuple-element.92.factor_ref, bf16[912,768]{1,0:T(8,128)(2,1)} %get-tuple-element.43.normed_ref, bf16[912,16]{1,0:T(8,128)(2,1)} %constant.148.clone.fold_ref.spread_ref, ...), custom_call_target="tpu_custom_call" | custom-call | tf_op jit(solution)/shard_map/key_grad/pallas_call | solution.py:49
  254.5 1.9 slice_select_fusion
  267.0 7.8 %collective-permute-done.11 = bf16[56,3072]{1,0:T(8,128)(2,1)} collective-permute-done((bf16[56,3072]{1,0:T(8,128)(2,1)S(1)}, bf16[56,3072]{1,0:T(8,128)(2,1)}, u32[]{:S(2)}, u32[]{:S(2)}) %collective-permute-start.11) | collective-permute-done | bytes 344096 | tf_op jit(solution)/shard_map/ppermute | solution.py:576
  276.7 7.3 %collective-permute-done.15 = f32[192,768]{1,0:T(8,128)S(1)} collective-permute-done((f32[192,768]{1,0:T(8,128)S(1)}, f32[192,768]{1,0:T(8,128)S(1)}, u32[]{:S(2)}, u32[]{:S(2)}) %collective-permute-start.15) | collective-permute-done | bytes 589856 | tf_op jit(solution)/shard_map/ppermute | solution.py:367
  286.3 3.8 %all-to-all-start = ((bf16[16,56,288]{2,1,0:T(8,128)(2,1)}), bf16[16,56,288]{2,1,0:T(8,128)(2,1)S(1)}, u32[]{:S(2)}, u32[]{:S(2)}) async-start(bf16[16,56,288]{2,1,0:T(8,128)(2,1)} %bitcast.31), calls=%async_computation | async-start | bytes 1376256 | tf_op jit(solution)/shard_map/all_to_all | solution.py:589
  290.1 15.7 %collective-permute-done.16 = f32[96,768]{1,0:T(8,128)S(1)} collective-permute-done((f32[96,768]{1,0:T(8,128)S(1)}, f32[96,768]{1,0:T(8,128)S(1)}, u32[]{:S(2)}, u32[]{:S(2)}) %collective-permute-start.16) | collective-permute-done | bytes 294944 | tf_op jit(solution)/shard_map/ppermute | solution.py:367
  307.2 9.4 %collective-permute-done.17 = f32[48,768]{1,0:T(8,128)S(1)} collective-permute-done((f32[48,768]{1,0:T(8,128)S(1)}, f32[48,768]{1,0:T(8,128)S(1)}, u32[]{:S(2)}, u32[]{:S(2)}) %collective-permute-start.17) | collective-permute-done | bytes 147488 | tf_op jit(solution)/shard_map/ppermute | solution.py:367
  323.1 4.9 %collective-permute-start.22 = (f32[48,768]{1,0:T(8,128)}, f32[48,768]{1,0:T(8,128)}, u32[]{:S(2)}, u32[]{:S(2)}) collective-permute-start(f32[48,768]{1,0:T(8,128)} %get-tuple-element.85), channel_id=1, source_target_pairs={{0,2},{6,3},{3,4},{20,5},{17,6},{23,7}} | collective-permute-start | bytes 442376 | tf_op jit(solution)/shard_map/ppermute | solution.py:615
  330.2 4.8 %owner.1 = (f32[288,768]{1,0:T(8,128)}, f32[1,768]{1,0:T(1,128)}) custom-call(s32[6]{0:T(128)} %stack.31.info_ref, bf16[896,288]{1,0:T(8,128)(2,1)} %bitcast.32, bf16[3,896,768]{2,1,0:T(8,128)(2,1)} %all-gather.5.cloned.1.call-done.b0_ref.b1_ref, bf16[3,896,768]{2,1,0:T(8,128)(2,1)} %all-gather.5.cloned.1.call-done.b0_ref.b1_ref), custom_call_target="tpu_custom_call" | custom-call | tf_op jit(solution)/shard_map/owner/pallas_call | solution.py:635
  340.6 1.9 collective-permute-done.25
  343.4 2.9 collective-permute-done.26
  346.3 2.5 collective-permute-start.27
  358.9 3.2 multiply_add_fusion
  (206 shorter events, 73.8 us)
Async XLA Ops:
  7.2 140.8 %all-gather.3.cloned.1.call-start = ((), (), s32[]{:S(2)}) async-start(), calls=%async_computation.1 | async-start | bytes 15040512 | tf_op jit(solution)/shard_map/all_gather | solution.py:438
  8.5 6.9 %collective-permute-start.1 = (bf16[288,768]{1,0:T(8,128)(2,1)S(1)}, bf16[288,768]{1,0:T(8,128)(2,1)S(1)}, u32[]{:S(2)}, u32[]{:S(2)}) collective-permute-start(bf16[288,768]{1,0:T(8,128)(2,1)S(1)} %convert_element_type.19), channel_id=1, source_target_pairs={{1,16},{3,17},{5,18},{7,19},{9,20},{11,21},{13,22},{15,23},{17,24}... | collective-permute-start | bytes 1327112 | tf_op jit(solution)/shard_map/ppermute | solution.py:436
  9.2 23.6 %collective-permute-start = (bf16[288,768]{1,0:T(8,128)(2,1)S(1)}, bf16[288,768]{1,0:T(8,128)(2,1)}, u32[]{:S(2)}, u32[]{:S(2)}) collective-permute-start(bf16[288,768]{1,0:T(8,128)(2,1)S(1)} %convert_element_type.19), channel_id=1, source_target_pairs={{0,16},{2,17},{4,18},{6,19},{8,20},{10,21},{12,22},{14,23},{16,24}... | collective-permute-start | bytes 1327112 | tf_op jit(solution)/shard_map/ppermute | solution.py:435
  35.0 294.4 %all-gather.5.cloned.1.call-start = ((), (), s32[]{:S(2)}) async-start(), calls=%async_computation.2 | async-start | bytes 4386816 | tf_op jit(solution)/shard_map/all_gather | solution.py:593
  172.6 7.1 %collective-permute-start.2 = (bf16[56,768]{1,0:T(8,128)(2,1)}, bf16[56,768]{1,0:T(8,128)(2,1)S(1)}, u32[]{:S(2)}, u32[]{:S(2)}) collective-permute-start(bf16[56,768]{1,0:T(8,128)(2,1)} %get-tuple-element.51.emb_ref), channel_id=1, source_target_pairs={{0,8},{1,9},{2,10},{3,11},{4,12},{5,13},{6,14},{7,15},{8,0},{9,1},... | collective-permute-start | bytes 258056 | tf_op jit(solution)/shard_map/ppermute | solution.py:367
  175.1 7.8 %collective-permute-start.6 = (bf16[24,768]{1,0:T(8,128)(2,1)S(1)}, bf16[24,768]{1,0:T(8,128)(2,1)S(1)}, u32[]{:S(2)}, u32[]{:S(2)}) collective-permute-start(bf16[24,768]{1,0:T(8,128)(2,1)S(1)} %maximum_maximum_fusion), channel_id=1, source_target_pairs={{0,16},{1,17},{2,18},{3,19},{4,20},{5,21},{6,22},{7,23},{8,24},{9,... | collective-permute-start | bytes 110600 | tf_op jit(solution)/shard_map/ppermute | solution.py:513
  180.6 6.8 %collective-permute-start.3 = (bf16[112,768]{1,0:T(8,128)(2,1)S(1)}, bf16[112,768]{1,0:T(8,128)(2,1)S(1)}, u32[]{:S(2)}, u32[]{:S(2)}) collective-permute-start(bf16[112,768]{1,0:T(8,128)(2,1)S(1)} %pad_maximum_fusion.6), channel_id=1, source_target_pairs={{0,4},{1,5},{2,6},{3,7},{4,0},{5,1},{6,2},{7,3},{8,12},{9,13},{10,... | collective-permute-start | bytes 516104 | tf_op jit(solution)/shard_map/ppermute | solution.py:367
  181.5 58.6 %collective-permute-start.12 = (bf16[56,2304]{1,0:T(8,128)(2,1)S(1)}, bf16[56,2304]{1,0:T(8,128)(2,1)S(1)}, u32[]{:S(2)}, u32[]{:S(2)}) collective-permute-start(bf16[56,2304]{1,0:T(8,128)(2,1)S(1)} %pad_maximum_fusion.4), channel_id=1, source_target_pairs={{16,0},{17,1},{18,2},{19,3},{20,4},{21,5},{22,6},{23,7},{24,8},{25... | collective-permute-start | bytes 774152 | tf_op jit(solution)/shard_map/ppermute | solution.py:572
  182.8 6.0 %collective-permute-start.7 = (bf16[24,768]{1,0:T(8,128)(2,1)S(1)}, bf16[24,768]{1,0:T(8,128)(2,1)S(1)}, u32[]{:S(2)}, u32[]{:S(2)}) collective-permute-start(bf16[24,768]{1,0:T(8,128)(2,1)S(1)} %collective-permute-done.6), channel_id=1, source_target_pairs={{0,8},{1,9},{2,10},{3,11},{4,12},{5,13},{6,14},{7,15},{8,0},{9,1},... | collective-permute-start | bytes 110600 | tf_op jit(solution)/shard_map/ppermute | solution.py:367
  188.3 10.4 %collective-permute-start.4 = (bf16[224,768]{1,0:T(8,128)(2,1)S(1)}, bf16[224,768]{1,0:T(8,128)(2,1)S(1)}, u32[]{:S(2)}, u32[]{:S(2)}) collective-permute-start(bf16[224,768]{1,0:T(8,128)(2,1)S(1)} %pad_maximum_fusion.1), channel_id=1, source_target_pairs={{0,2},{1,3},{2,0},{3,1},{4,6},{5,7},{6,4},{7,5},{8,10},{9,11},{10,... | collective-permute-start | bytes 1032200 | tf_op jit(solution)/shard_map/ppermute | solution.py:367
  188.9 4.4 %collective-permute-start.8 = (bf16[48,768]{1,0:T(8,128)(2,1)S(1)}, bf16[48,768]{1,0:T(8,128)(2,1)S(1)}, u32[]{:S(2)}, u32[]{:S(2)}) collective-permute-start(bf16[48,768]{1,0:T(8,128)(2,1)S(1)} %pad_maximum_fusion.8), channel_id=1, source_target_pairs={{0,4},{1,5},{2,6},{3,7},{4,0},{5,1},{6,2},{7,3},{8,12},{9,13},{10,... | collective-permute-start | bytes 221192 | tf_op jit(solution)/shard_map/ppermute | solution.py:367
  193.3 6.9 %collective-permute-start.9 = (bf16[96,768]{1,0:T(8,128)(2,1)S(1)}, bf16[96,768]{1,0:T(8,128)(2,1)S(1)}, u32[]{:S(2)}, u32[]{:S(2)}) collective-permute-start(bf16[96,768]{1,0:T(8,128)(2,1)S(1)} %pad_maximum_fusion.7), channel_id=1, source_target_pairs={{0,2},{1,3},{2,0},{3,1},{4,6},{5,7},{6,4},{7,5},{8,10},{9,11},{10,... | collective-permute-start | bytes 442376 | tf_op jit(solution)/shard_map/ppermute | solution.py:367
  198.8 3.3 collective-permute-start.5
  200.3 1.6 collective-permute-start.10
  241.7 5.7 %collective-permute-start.13 = (bf16[3,16,224]{2,1,0:T(8,128)(2,1)S(1)}, bf16[3,16,224]{2,1,0:T(8,128)(2,1)S(1)}, u32[]{:S(2)}, u32[]{:S(2)}) collective-permute-start(bf16[3,16,224]{2,1,0:T(8,128)(2,1)S(1)} %copy-done.31), channel_id=1, source_target_pairs={{16,0},{17,1},{18,2},{19,3},{20,4},{21,5},{22,6},{23,7},{24,8},{25... | collective-permute-start | bytes 64520 | tf_op jit(solution)/shard_map/ppermute | solution.py:575
  256.4 3.0 collective-permute-start.14
  261.1 22.9 %collective-permute-start.15 = (f32[192,768]{1,0:T(8,128)S(1)}, f32[192,768]{1,0:T(8,128)S(1)}, u32[]{:S(2)}, u32[]{:S(2)}) collective-permute-start(f32[192,768]{1,0:T(8,128)S(1)} %slice_select_fusion.1), channel_id=1, source_target_pairs={{0,2},{1,3},{2,0},{3,1},{4,6},{5,7},{6,4},{7,5},{8,10},{9,11},{10,... | collective-permute-start | bytes 1769480 | tf_op jit(solution)/shard_map/ppermute | solution.py:367
  261.9 12.9 %collective-permute-start.11 = (bf16[56,3072]{1,0:T(8,128)(2,1)S(1)}, bf16[56,3072]{1,0:T(8,128)(2,1)}, u32[]{:S(2)}, u32[]{:S(2)}) collective-permute-start(bf16[56,3072]{1,0:T(8,128)(2,1)S(1)} %pad_maximum_fusion.2), channel_id=1, source_target_pairs={{16,0},{17,1},{18,2},{19,3},{20,4},{21,5},{22,6},{23,7},{24,8},{25... | collective-permute-start | bytes 1032200 | tf_op jit(solution)/shard_map/ppermute | solution.py:576
  265.7 52.1 %collective-permute-start.29 = (bf16[864,384]{1,0:T(8,128)(2,1)}, bf16[864,384]{1,0:T(8,128)(2,1)S(1)}, u32[]{:S(2)}, u32[]{:S(2)}) collective-permute-start(bf16[864,384]{1,0:T(8,128)(2,1)} %get-tuple-element.75), channel_id=1, source_target_pairs={{16,0},{17,1},{18,2},{19,3},{20,4},{21,5},{22,6},{23,7},{24,8},{25... | collective-permute-start | bytes 1990664 | tf_op jit(solution)/shard_map/ppermute | solution.py:579
  284.1 21.7 %collective-permute-start.16 = (f32[96,768]{1,0:T(8,128)S(1)}, f32[96,768]{1,0:T(8,128)S(1)}, u32[]{:S(2)}, u32[]{:S(2)}) collective-permute-start(f32[96,768]{1,0:T(8,128)S(1)} %slice_select_fusion.2), channel_id=1, source_target_pairs={{0,4},{1,5},{2,6},{3,7},{4,0},{5,1},{6,2},{7,3},{8,12},{9,13},{10,... | collective-permute-start | bytes 884744 | tf_op jit(solution)/shard_map/ppermute | solution.py:367
  286.3 43.0 %all-to-all-start = ((bf16[16,56,288]{2,1,0:T(8,128)(2,1)}), bf16[16,56,288]{2,1,0:T(8,128)(2,1)S(1)}, u32[]{:S(2)}, u32[]{:S(2)}) async-start(bf16[16,56,288]{2,1,0:T(8,128)(2,1)} %bitcast.31), calls=%async_computation | async-start | bytes 1376256 | tf_op jit(solution)/shard_map/all_to_all | solution.py:589
  305.9 10.7 %collective-permute-start.17 = (f32[48,768]{1,0:T(8,128)S(1)}, f32[48,768]{1,0:T(8,128)S(1)}, u32[]{:S(2)}, u32[]{:S(2)}) collective-permute-start(f32[48,768]{1,0:T(8,128)S(1)} %slice_select_fusion.3), channel_id=1, source_target_pairs={{0,8},{1,9},{2,10},{3,11},{4,12},{5,13},{6,14},{7,15},{8,0},{9,1},... | collective-permute-start | bytes 442376 | tf_op jit(solution)/shard_map/ppermute | solution.py:367
  317.2 10.8 %collective-permute-start.18 = (f32[48,768]{1,0:T(8,128)}, f32[48,768]{1,0:T(8,128)S(1)}, u32[]{:S(2)}, u32[]{:S(2)}) collective-permute-start(f32[48,768]{1,0:T(8,128)} %get-tuple-element.85), channel_id=1, source_target_pairs={{4,3},{1,4},{7,5},{18,6},{21,7}} | collective-permute-start | bytes 442376 | tf_op jit(solution)/shard_map/ppermute | solution.py:615
  319.1 17.5 %collective-permute-start.19 = (f32[48,768]{1,0:T(8,128)}, f32[48,768]{1,0:T(8,128)}, u32[]{:S(2)}, u32[]{:S(2)}) collective-permute-start(f32[48,768]{1,0:T(8,128)} %get-tuple-element.85), channel_id=1, source_target_pairs={{12,3},{9,4},{15,5},{26,6},{29,7}} | collective-permute-start | bytes 442376 | tf_op jit(solution)/shard_map/ppermute | solution.py:615
  320.5 19.2 %collective-permute-start.20 = (f32[48,768]{1,0:T(8,128)}, f32[48,768]{1,0:T(8,128)}, u32[]{:S(2)}, u32[]{:S(2)}) collective-permute-start(f32[48,768]{1,0:T(8,128)} %get-tuple-element.85), channel_id=1, source_target_pairs={{2,3},{5,4},{16,5},{22,6},{19,7}} | collective-permute-start | bytes 442376 | tf_op jit(solution)/shard_map/ppermute | solution.py:615
  321.8 20.7 %collective-permute-start.21 = (f32[48,768]{1,0:T(8,128)}, f32[48,768]{1,0:T(8,128)}, u32[]{:S(2)}, u32[]{:S(2)}) collective-permute-start(f32[48,768]{1,0:T(8,128)} %get-tuple-element.85), channel_id=1, source_target_pairs={{10,3},{13,4},{24,5},{30,6},{27,7}} | collective-permute-start | bytes 442376 | tf_op jit(solution)/shard_map/ppermute | solution.py:615
  323.1 25.7 %collective-permute-start.22 = (f32[48,768]{1,0:T(8,128)}, f32[48,768]{1,0:T(8,128)}, u32[]{:S(2)}, u32[]{:S(2)}) collective-permute-start(f32[48,768]{1,0:T(8,128)} %get-tuple-element.85), channel_id=1, source_target_pairs={{0,2},{6,3},{3,4},{20,5},{17,6},{23,7}} | collective-permute-start | bytes 442376 | tf_op jit(solution)/shard_map/ppermute | solution.py:615
  328.0 24.2 %collective-permute-start.23 = (f32[48,768]{1,0:T(8,128)}, f32[48,768]{1,0:T(8,128)}, u32[]{:S(2)}, u32[]{:S(2)}) collective-permute-start(f32[48,768]{1,0:T(8,128)} %get-tuple-element.85), channel_id=1, source_target_pairs={{8,2},{14,3},{11,4},{28,5},{25,6},{31,7}} | collective-permute-start | bytes 442376 | tf_op jit(solution)/shard_map/ppermute | solution.py:615
  338.6 3.9 %collective-permute-start.25 = (f32[8,768]{1,0:T(8,128)S(1)}, f32[8,768]{1,0:T(8,128)S(1)}, u32[]{:S(2)}, u32[]{:S(2)}) collective-permute-start(f32[8,768]{1,0:T(8,128)S(1)} %fusion.8), channel_id=1, source_target_pairs={{0,2},{1,3},{2,0},{3,1},{4,6},{5,7},{6,4},{7,5},{8,10},{9,11},{10,... | collective-permute-start | bytes 73736 | tf_op jit(solution)/shard_map/ppermute | solution.py:367
  342.5 3.8 %collective-permute-start.26 = (f32[8,768]{1,0:T(8,128)S(1)}, f32[8,768]{1,0:T(8,128)S(1)}, u32[]{:S(2)}, u32[]{:S(2)}) collective-permute-start(f32[8,768]{1,0:T(8,128)S(1)} %add.142), channel_id=1, source_target_pairs={{0,4},{1,5},{2,6},{3,7},{4,0},{5,1},{6,2},{7,3},{8,12},{9,13},{10,... | collective-permute-start | bytes 73736 | tf_op jit(solution)/shard_map/ppermute | solution.py:367
  346.3 4.7 %collective-permute-start.27 = (f32[8,768]{1,0:T(8,128)S(1)}, f32[8,768]{1,0:T(8,128)S(1)}, u32[]{:S(2)}, u32[]{:S(2)}) collective-permute-start(f32[8,768]{1,0:T(8,128)S(1)} %add.143), channel_id=1, source_target_pairs={{0,8},{1,9},{2,10},{3,11},{4,12},{5,13},{6,14},{7,15},{8,0},{9,1},... | collective-permute-start | bytes 73736 | tf_op jit(solution)/shard_map/ppermute | solution.py:367
  351.1 3.8 %collective-permute-start.28 = (f32[8,768]{1,0:T(8,128)S(1)}, f32[8,768]{1,0:T(8,128)S(1)}, u32[]{:S(2)}, u32[]{:S(2)}) collective-permute-start(f32[8,768]{1,0:T(8,128)S(1)} %add.144), channel_id=1, source_target_pairs={{0,16},{16,0},{1,17},{17,1},{2,18},{18,2},{3,19},{19,3},{4,20},{20... | collective-permute-start | bytes 73736 | tf_op jit(solution)/shard_map/ppermute | solution.py:367
  (34 other events, 405.1 us)
Sparse Core Ops, SparseCore 0:
  35.1 112.7 all-gather.2
  241.8 61.5 all-gather.4

commit v2 on v1

--- a/solution.py
+++ b/solution.py
@@ -22,6 +22,8 @@
 GELU_A = 0.044715
 GELU_C = math.sqrt(2.0 / math.pi)
 
+POS_TEXT, POS_IMAGE, LOW, HIGH, PLACE, COUNT_PLACE, SLOT, REAL = range(8)
+
 f32 = jnp.float32
 bf16 = jnp.bfloat16
 
@@ -44,12 +46,24 @@
     return lax.dot_general(left, right, (((0,), (0,)), ((), ())), preferred_element_type=f32)
 
 
-def call(kernel, outs, *args, scratch=(), name=None, flops=0):
+def call(kernel, outs, *args, scratch=(), name=None, weights=None, smem=None):
     whole = pl.BlockSpec(memory_space=pltpu.VMEM)
+    specs = [whole] * len(args)
+    if smem is not None:
+        specs = [pl.BlockSpec(memory_space=pltpu.SMEM)] + specs
+        args = (smem, *args)
+    if weights is not None:
+        parts, table = weights
+        specs = (
+            [pl.BlockSpec(memory_space=pltpu.SMEM)]
+            + [pl.BlockSpec(memory_space=pltpu.HBM)] * len(parts)
+            + specs
+        )
+        args = (table, *parts, *args)
     return pl.pallas_call(
         kernel,
         out_shape=outs,
-        in_specs=[whole] * len(args),
+        in_specs=specs,
         out_specs=jax.tree.map(lambda _: whole, outs),
         scratch_shapes=list(scratch),
         name=name,
@@ -102,31 +116,58 @@
     return pl.ds(pl.multiple_of(base + index * 256, 256), 256)
 
 
-def rows_kernel(step, x_ref, pos_ref, norms_ref, normed_ref, npool_ref, xpool_ref):
-    gain, offset = norms_ref[0:1, :], norms_ref[1:2, :]
-
-    @pl.loop(0, x_ref.shape[0] // step)
+def rows_kernel(
+    step, text_ref, captions_ref, images_ref, facts_ref, norms_t_ref, norms_i_ref,
+    normed_t_ref, normed_ref, npool_t_ref, npool_ref, xpool_ref, facts_out_ref, norms_ref,
+):
+    facts_out_ref[...] = facts_ref[...]
+    norms_ref[...] = jnp.where(text_ref[0] == 1, norms_t_ref[...], norms_i_ref[...])
+
+    def pooled(x_ref, fact, from_ref, to_ref):
+        count = to_ref.shape[0]
+        pick = (
+            lax.broadcasted_iota(jnp.int32, (count, x_ref.shape[0]), 1)
+            == facts_ref[:, fact : fact + 1]
+        ).astype(bf16)
+        to_ref[...] = dot_nn(pick, from_ref[...]).astype(bf16)
+        xpool_ref[...] = dot_nn(pick, x_ref[...])
+
+    @pl.loop(0, captions_ref.shape[0] // step)
     def _(i):
         here = pl.ds(pl.multiple_of(i * step, step), step)
-        unit, _ = normalize(x_ref[here, :].astype(f32))
-        normed_ref[here, :] = (unit * gain + offset).astype(bf16)
-
-    count = npool_ref.shape[0]
-    pick = (
-        lax.broadcasted_iota(jnp.int32, (count, x_ref.shape[0]), 1) == pos_ref[...]
-    ).astype(bf16)
-    npool_ref[...] = dot_nn(pick, normed_ref[...]).astype(bf16)
-    xpool_ref[...] = dot_nn(pick, x_ref[...])
-
-
-def attend_kernel(
-    normed_ref, npool_ref, xpool_ref, norms_ref, low_ref, high_ref, w_ref,
-    q_ref, k_ref, v_ref, probs_ref, att_ref, hidden_ref, nm_ref,
-):
+        unit, _ = normalize(captions_ref[here, :].astype(f32))
+        normed_t_ref[here, :] = (unit * norms_t_ref[0:1, :] + norms_t_ref[1:2, :]).astype(bf16)
+
+    pooled(captions_ref, POS_TEXT, normed_t_ref, npool_t_ref)
+
+    @pl.when(text_ref[0] == 1)
+    def _():
+        normed_ref[...] = normed_t_ref[...]
+        npool_ref[...] = npool_t_ref[...]
+
+    @pl.when(text_ref[0] == 0)
+    def _():
+        @pl.loop(0, images_ref.shape[0] // step)
+        def _(i):
+            here = pl.ds(pl.multiple_of(i * step, step), step)
+            unit, _ = normalize(images_ref[here, :].astype(f32))
+            normed_ref[here, :] = (unit * norms_i_ref[0:1, :] + norms_i_ref[1:2, :]).astype(bf16)
+
+        pooled(images_ref, POS_IMAGE, normed_ref, npool_ref)
+
+
+def attend_kernel(parts, table_ref, *refs):
+    part_refs = refs[:parts]
+    (
+        normed_ref, npool_ref, xpool_ref, norms_ref, facts_ref,
+        q_ref, k_ref, v_ref, probs_ref, att_ref, hidden_ref, nm_ref, w_ref, sems,
+    ) = refs[parts:]
     count, features = npool_ref.shape
+    for wait in fetch(table_ref, part_refs, 0, 4 * features, w_ref, sems):
+        wait()
     total = normed_ref.shape[0]
     keys = lax.broadcasted_iota(jnp.int32, (count, total), 1)
-    allowed = ((keys >= low_ref[...]) & (keys < high_ref[...]))[None]
+    allowed = ((keys >= facts_ref[:, LOW : LOW + 1]) & (keys < facts_ref[:, HIGH : HIGH + 1]))[None]
 
     @pl.loop(0, features // 256)
     def _(i):
@@ -158,37 +199,37 @@
     return 0.5 * (1.0 + tanh), tanh
 
 
-def feed_kernel(
-    nm_ref, hidden_ref, up_ref, down_ref,
-    pre_ref, act_ref, pooled_ref, inverse_ref, emb_ref, total_ref,
-):
-    step = pl.program_id(0)
-    pre = dot_nt(nm_ref[...], up_ref[...])
-    pre_ref[...] = pre
-    act = (pre * gelu_parts(pre)[0]).astype(bf16)
-    act_ref[...] = act
-    part = dot_nn(act, down_ref[...])
-
-    @pl.when(step == 0)
-    def _():
-        total_ref[...] = part
-
-    @pl.when(step > 0)
-    def _():
-        total_ref[...] += part
-
-    @pl.when(step == pl.num_programs(0) - 1)
-    def _():
-        pooled = hidden_ref[...] + total_ref[...]
-        inverse = lax.rsqrt(jnp.sum(pooled * pooled, axis=-1, keepdims=True) + EPSILON)
-        pooled_ref[...] = pooled
-        inverse_ref[...] = jnp.broadcast_to(inverse, inverse_ref.shape)
-        emb_ref[...] = (pooled * inverse).astype(bf16)
+def feed_kernel(parts, first, skip, block, table_ref, *refs):
+    part_refs = refs[:parts]
+    (
+        nm_ref, hidden_ref, pre_ref, act_ref, pooled_ref, inverse_ref, emb_ref, w_ref, total_ref, sems,
+    ) = refs[parts:]
+    units = pre_ref.shape[1]
+    for wait in fetch(table_ref, part_refs, first, w_ref.shape[0], w_ref, sems):
+        wait()
+    total_ref[...] = hidden_ref[...]
+
+    @pl.loop(0, units // block)
+    def _(i):
+        here = pl.ds(pl.multiple_of(i * block, block), block)
+        pre = dot_nt(nm_ref[...], w_ref[pl.ds(pl.multiple_of(skip + i * block, 64), block), :])
+        pre_ref[:, here] = pre
+        act = (pre * gelu_parts(pre)[0]).astype(bf16)
+        act_ref[:, here] = act
+        total_ref[...] += dot_nn(
+            act, w_ref[pl.ds(pl.multiple_of(skip + units + i * block, 64), block), :]
+        )
+
+    pooled = total_ref[...]
+    inverse = lax.rsqrt(jnp.sum(pooled * pooled, axis=-1, keepdims=True) + EPSILON)
+    pooled_ref[...] = pooled
+    inverse_ref[...] = jnp.broadcast_to(inverse, inverse_ref.shape)
+    emb_ref[...] = (pooled * inverse).astype(bf16)
 
 
 def loss_kernel(
     chunk, slots, text_ref, img_ref, row_bias_ref, col_bias_ref, emb_ref, pooled_ref, inverse_ref,
-    place_ref, count_place_ref, slot_ref, real_ref, grad_ref, branch_ref,
+    facts_ref, grad_ref, branch_ref,
 ):
     images = img_ref.shape[0]
     count = emb_ref.shape[0]
@@ -217,13 +258,13 @@
     by_row = row_exp / jnp.sum(row_exp, axis=1, keepdims=True)
     by_column = jnp.exp(masked - column_lse)
     columns = lax.broadcasted_iota(jnp.int32, (count, images), 1)
-    target = (columns == place_ref[...]).astype(f32)
-    listed = dot_nn((columns == count_place_ref[...]).astype(bf16), img_ref[...])
-    at = lax.broadcasted_iota(jnp.int32, listed.shape, 1) == slot_ref[...]
+    target = (columns == facts_ref[:, PLACE : PLACE + 1]).astype(f32)
+    listed = dot_nn((columns == facts_ref[:, COUNT_PLACE : COUNT_PLACE + 1]).astype(bf16), img_ref[...])
+    at = lax.broadcasted_iota(jnp.int32, listed.shape, 1) == facts_ref[:, SLOT : SLOT + 1]
     named = jnp.maximum(jnp.sum(jnp.where(at, listed, 0.0), axis=1, keepdims=True), 1.0)
     grad_logits = 0.5 * (by_row - target) + 0.5 * (by_column - target / named)
     scaled = jnp.where(
-        (col_bias_ref[...] == 0.0) & (real_ref[...] > 0.0), LOGIT_SCALE * grad_logits, 0.0
+        (col_bias_ref[...] == 0.0) & (facts_ref[:, REAL : REAL + 1] > 0), LOGIT_SCALE * grad_logits, 0.0
     ).astype(bf16)
     grad_embed = dot_nn(scaled, img_ref[...])
     pooled = pooled_ref[...]
@@ -234,46 +275,53 @@
     branch_ref[...] = grad_pooled.astype(bf16)
 
 
-def feed_back_kernel(
-    branch_ref, grad_ref, hidden_ref, norms_ref, pre_ref, up_ref, down_ref,
-    gpre_ref, ghidden_ref, mixed_ref, sums_ref, total_ref,
-):
-    step = pl.program_id(0)
-    pre = pre_ref[...]
-    cdf, tanh = gelu_parts(pre)
-    slope = cdf + pre * 0.5 * (1.0 - tanh * tanh) * GELU_C * (1.0 + 3.0 * GELU_A * pre * pre)
-    grad_act = dot_nt(branch_ref[...], down_ref[...]).astype(bf16)
-    gpre = (grad_act.astype(f32) * slope).astype(bf16)
-    gpre_ref[...] = gpre
-    part = dot_nn(gpre, up_ref[...])
-
-    @pl.when(step == 0)
-    def _():
-        total_ref[...] = part
-
-    @pl.when(step > 0)
-    def _():
-        total_ref[...] += part
-
-    @pl.when(step == pl.num_programs(0) - 1)
-    def _():
-        grad = total_ref[...]
-        pulled, by_gain = norm_pull(grad, hidden_ref[...], norms_ref[2:3, :])
-        ghidden = grad_ref[...] + pulled
-        ghidden_ref[...] = ghidden
-        mixed_ref[...] = ghidden.astype(bf16)
-        sums_ref[...] = jnp.zeros_like(sums_ref)
-        sums_ref[2:3, :] = jnp.sum(by_gain, axis=0, keepdims=True)
-        sums_ref[3:4, :] = jnp.sum(grad, axis=0, keepdims=True)
-
-
-def attend_back_kernel(
-    step, half, mixed_ref, ghidden_ref, probs_ref, q_ref, k_ref, v_ref, x_ref, pos_ref, norms_ref,
-    sums_in_ref, fold_ref, w_ref,
-    gatt_ref, gq_ref, craw_ref, cprob_ref, left_ref, right_ref, sums_ref, grad_ref,
-):
-    count, features = mixed_ref.shape
-    gatt_ref[...] = dot_nn(mixed_ref[...], w_ref[pl.ds(3 * features, features), :]).astype(bf16)
+def feed_back_kernel(parts, first, skip, block, table_ref, *refs):
+    part_refs = refs[:parts]
+    (
+        branch_ref, grad_ref, hidden_ref, norms_ref, pre_ref,
+        gpre_ref, ghidden_ref, mixed_ref, sums_ref, gatt_ref, w_ref, total_ref, sems,
+    ) = refs[parts:]
+    units = pre_ref.shape[1]
+    features = branch_ref.shape[1]
+    for wait in fetch(table_ref, part_refs, first, w_ref.shape[0], w_ref, sems):
+        wait()
+    total_ref[...] = jnp.zeros_like(total_ref)
+
+    @pl.loop(0, units // block)
+    def _(i):
+        here = pl.ds(pl.multiple_of(i * block, block), block)
+        pre = pre_ref[:, here]
+        cdf, tanh = gelu_parts(pre)
+        slope = cdf + pre * 0.5 * (1.0 - tanh * tanh) * GELU_C * (1.0 + 3.0 * GELU_A * pre * pre)
+        grad_act = dot_nt(
+            branch_ref[...], w_ref[pl.ds(pl.multiple_of(skip + units + i * block, 64), block), :]
+        ).astype(bf16)
+        gpre = (grad_act.astype(f32) * slope).astype(bf16)
+        gpre_ref[:, here] = gpre
+        total_ref[...] += dot_nn(gpre, w_ref[pl.ds(pl.multiple_of(skip + i * block, 64), block), :])
+
+    grad = total_ref[...]
+    pulled, by_gain = norm_pull(grad, hidden_ref[...], norms_ref[2:3, :])
+    ghidden = grad_ref[...] + pulled
+    mixed = ghidden.astype(bf16)
+    ghidden_ref[...] = ghidden
+    mixed_ref[...] = mixed
+    gatt_ref[...] = dot_nn(mixed, w_ref[pl.ds(skip - features, features), :]).astype(bf16)
+    sums_ref[...] = jnp.zeros_like(sums_ref)
+    sums_ref[2:3, :] = jnp.sum(by_gain, axis=0, keepdims=True)
+    sums_ref[3:4, :] = jnp.sum(grad, axis=0, keepdims=True)
+
+
+def attend_back_kernel(parts, step, half, table_ref, *refs):
+    part_refs = refs[:parts]
+    (
+        gatt_ref, ghidden_ref, probs_ref, q_ref, k_ref, v_ref, x_ref, facts_ref, norms_ref,
+        sums_in_ref, fold_ref,
+        gq_ref, craw_ref, cprob_ref, left_ref, right_ref, sums_ref, grad_ref, w_ref, sems,
+    ) = refs[parts:]
+    count, features = gatt_ref.shape
+    for wait in fetch(table_ref, part_refs, 0, 3 * features, w_ref, sems):
+        wait()
 
     @pl.loop(0, features // 256)
     def _(i):
@@ -316,7 +364,8 @@
         dgain, doffset = carry
         here = pl.ds(pl.multiple_of(j * step, step), step)
         pick = (
-            lax.broadcasted_iota(jnp.int32, (step, count), 0) + j * step == pos_ref[...]
+            lax.broadcasted_iota(jnp.int32, (step, count), 0) + j * step
+            == facts_ref[POS_TEXT : POS_TEXT + 1, :]
         ).astype(f32)
         grad = grad_ref[here, :] + dot_nn(pick, gpool, precision=lax.Precision.HIGHEST)
         pulled, by_gain = norm_pull(grad, x_ref[here, :].astype(f32), gain)
@@ -365,6 +414,121 @@
 
 def swapped(block, axis, bit):
     return lax.ppermute(block, axis, [(i, i ^ bit) for i in range(lax.axis_size(axis))])
+
+
+UNITS = 16
+
+
+def units_gathered(low_shard, image_weights, text, prepare):
+    n = lax.axis_size("dp")
+    chips = n // 2
+    steps = chips // 2
+    index = lax.axis_index("dp")
+    core = index % 2
+    other_core = [(i, i ^ 1) for i in range(n)]
+    order = list(range(0, chips, 2)) + list(range(1, chips, 2))[::-1]
+    seat_of = np.zeros(chips, np.int32)
+    seat_of[order] = np.arange(chips)
+    route = []
+    for s in range(chips):
+        route.append((2 * order[s], 2 * order[(s + 1) % chips]))
+        route.append((2 * order[s] + 1, 2 * order[s - 1] + 1))
+
+    def pair(own, other):
+        return jnp.where(
+            core == 0,
+            jnp.concatenate([own, other], axis=0),
+            jnp.concatenate([other, own], axis=0),
+        )
+
+    def swap(block):
+        return lax.ppermute(block, "dp", other_core)
+
+    def onward(block):
+        return lax.ppermute(block, "dp", route)
+
+    def half_of(block):
+        size = block.shape[0] // 2
+        return lax.dynamic_slice_in_dim(block, core * size, size, axis=0)
+
+    high = swap(low_shard)
+    image = swap(image_weights)
+    b_part = jnp.where(text, pair(low_shard, high), jnp.where(core == 0, image, image_weights))
+    low_shard, image, image_weights, b_part = lax.optimization_barrier(
+        (low_shard, image, image_weights, b_part)
+    )
+    over = lax.ppermute(low_shard, "tower", [(0, 1)])
+    low = swap(over)
+    a_part = jnp.where(text, pair(over, low), jnp.where(core == 0, image_weights, image))
+
+    unit = np.arange(UNITS)
+    part = jnp.where(text, unit // chips, unit % 2)
+    far = (seat_of[None] - seat_of[:, None]) % chips
+    own_far = jnp.sum(
+        jnp.where(jnp.arange(chips)[None] == index // 2, jnp.asarray(far), 0), axis=1
+    )
+    far = jnp.where(text, jnp.tile(own_far, 2), jnp.repeat(own_far, 2))
+    step = jnp.minimum(far, chips - far)
+    from_other = (far < steps) == (core == 1)
+    table = jnp.where(
+        far == 0,
+        part,
+        jnp.where(
+            far == steps,
+            4 * steps - 2 + 2 * part + core,
+            4 * step - 2 + part + 2 * from_other,
+        ),
+    ).astype(jnp.int32)
+
+    parts = [a_part, b_part]
+    sent_a, sent_b = a_part, b_part
+    prepared = prepare(b_part)
+    for step in range(1, steps):
+        sent_b = onward(sent_b)
+        if step == 1:
+            sent_a, sent_b = lax.optimization_barrier((sent_a, sent_b))
+        elif step == 2:
+            sent_a, prepared, table = lax.optimization_barrier((sent_a, prepared, table))
+        sent_a = onward(sent_a)
+        parts += [sent_a, sent_b, swap(sent_a), swap(sent_b)]
+    last_b = onward(half_of(sent_b))
+    last_a = onward(half_of(sent_a))
+    parts += [last_a, swap(last_a), last_b, swap(last_b)]
+    return parts, table, prepared
+
+
+def fetch(table_ref, part_refs, first, rows, to_ref, sems):
+    size = part_refs[0].shape[0]
+    half = size // 2
+    whole = [p for p in part_refs if p.shape[0] == size]
+    halves = part_refs[len(whole) :]
+    waits = []
+    for u in range(-(-rows // size)):
+        taken = min(size, rows - u * size)
+
+        def copy(from_ref, at, count, u=u):
+            return pltpu.make_async_copy(
+                from_ref.at[pl.ds(0, count), :], to_ref.at[pl.ds(u * size + at, count), :], sems.at[u]
+            )
+
+        for j, part_ref in enumerate(whole):
+
+            @pl.when(table_ref[first + u] == j)
+            def _(part_ref=part_ref):
+                copy(part_ref, 0, taken).start()
+
+        for j in range(len(halves)):
+
+            @pl.when(table_ref[first + u] == len(whole) + j)
+            def _(j=j):
+                mine, other = halves[j // 2 * 2], halves[j // 2 * 2 + 1]
+                upper, lower = (mine, other) if j % 2 == 0 else (other, mine)
+                copy(upper, 0, min(half, taken)).start()
+                if taken > half:
+                    copy(lower, half, taken - half).start()
+
+        waits.append(copy(whole[0], 0, taken).wait)
+    return waits
 
 
 def gathered(block, axis):
@@ -431,45 +595,76 @@
     total = round_up(max(text_rows, imgs * img_rows), 48)
     wide = GROUP * count
 
-    low_shard = weights.astype(bf16)
-    even = lax.ppermute(low_shard, both, [(2 * k, n + k) for k in range(n)])
-    odd = lax.ppermute(low_shard, both, [(2 * k + 1, n + k) for k in range(n)])
-    shard = jnp.where(text, jnp.concatenate([even, odd], axis=0), image_weights)
-    packed = lax.all_gather(shard, "dp", axis=0, tiled=True)
+    def mine(of_text, of_image):
+        return jnp.where(text, of_text, of_image)
+
+    def padded_to(values, fill):
+        return jnp.pad(values, (0, count - values.shape[0]), constant_values=fill)
 
     def padded(rows):
         return jnp.pad(rows.reshape(-1, features), ((0, total - rows.shape[0] * rows.shape[1]), (0, 0)))
 
-    caption_x = padded(captions)
-    lengths = jnp.sum((token_ids != 0).astype(jnp.int32), axis=1)
-    start_t = jnp.arange(caps, dtype=jnp.int32) * length
-    start_i = jnp.arange(imgs, dtype=jnp.int32) * img_rows
-
-    def column(values, fill):
-        return jnp.pad(values, (0, count - values.shape[0]), constant_values=fill)[:, None]
-
-    low_t, high_t, pos_t = column(start_t, 0), column(start_t + lengths, 1), column(start_t + lengths - 1, 0)
-    low_i, high_i, pos_i = column(start_i, 0), column(start_i + img_rows, 1), column(start_i, 0)
-    rows_out = (
-        sds((total, features), bf16),
-        sds((count, features), bf16),
-        sds((count, features), f32),
-    )
-    normed_t, npool_t, xpool_t = call(
-        partial(rows_kernel, 48), rows_out, caption_x, pos_t, norm_params, name="rows"
-    )
-    normed_i, npool_i, xpool_i = call(
-        partial(rows_kernel, 48), rows_out, padded(images), pos_i, image_norms, name="rows"
-    )
-
-    def mine(of_text, of_image):
-        return jnp.where(text, of_text, of_image)
-
-    normed, npool, xpool = mine(normed_t, normed_i), mine(npool_t, npool_i), mine(xpool_t, xpool_i)
-    norms = mine(norm_params, image_norms)
+    img_slots = round_up(imgs + 1, 8)
+
+    def prepare(ready):
+        caption_in, image_in, ids, named, tallies, _ = lax.optimization_barrier(
+            (captions, images, token_ids, matches, counts, ready)
+        )
+        caption_x = padded(caption_in)
+        lengths = jnp.sum((ids != 0).astype(jnp.int32), axis=1)
+        start_t = jnp.arange(caps, dtype=jnp.int32) * length
+        start_i = jnp.arange(imgs, dtype=jnp.int32) * img_rows
+        pos_t = start_t + lengths - 1
+        owner_place = place_in_gathered(named // imgs, "dp")
+        columns = [
+            padded_to(pos_t, 0),
+            padded_to(start_i, 0),
+            mine(padded_to(start_t, 0), padded_to(start_i, 0)),
+            mine(padded_to(start_t + lengths, 1), padded_to(start_i + img_rows, 1)),
+            padded_to(owner_place * img_slots + named % imgs, 0),
+            padded_to(owner_place * img_slots + imgs, 0),
+            padded_to(named % imgs, 0),
+            jnp.asarray(np.arange(count) < caps, jnp.int32),
+        ]
+        facts = jnp.stack(columns, axis=0)
+        table = jnp.pad(facts.T, ((0, 0), (0, 128 - len(columns))))
+        rows = call(
+            partial(rows_kernel, 48),
+            (
+                sds((total, features), bf16),
+                sds((total, features), bf16),
+                sds((count, features), bf16),
+                sds((count, features), bf16),
+                sds((count, features), f32),
+                sds((count, 128), jnp.int32),
+                sds((4, features), f32),
+            ),
+            caption_x, padded(image_in), table, norm_params, image_norms,
+            smem=text.astype(jnp.int32)[None],
+            name="rows",
+        )
+        count_row = jnp.pad(tallies.astype(bf16), (0, features - imgs))[None]
+        return caption_x, facts, rows, count_row
+
+    low_shard = weights.astype(bf16)
+    if n == UNITS:
+        parts, table, prepared = units_gathered(low_shard, image_weights, text, prepare)
+    else:
+        even = lax.ppermute(low_shard, both, [(2 * k, n + k) for k in range(n)])
+        odd = lax.ppermute(low_shard, both, [(2 * k + 1, n + k) for k in range(n)])
+        shard = jnp.where(text, jnp.concatenate([even, odd], axis=0), image_weights)
+        packed = lax.all_gather(shard, "dp", axis=0, tiled=True)
+        parts = jnp.split(packed, UNITS, axis=0)
+        table = jnp.arange(UNITS, dtype=jnp.int32)
+        prepared = prepare(shard)
+    caption_x, facts, rows, count_row = prepared
+    normed_t, normed, npool_t, npool, xpool, facts_by_row, norms = rows
+    part_rows = all_rows // UNITS
+    feed_part = 4 * features // part_rows
+    feed_skip = 4 * features - feed_part * part_rows
 
     queries, key_rows, values, probs, attended, hidden, normed_mid = call(
-        attend_kernel,
+        partial(attend_kernel, len(parts)),
         (
             sds((count, features), bf16),
             sds((total, features), bf16),
@@ -479,45 +674,41 @@
             sds((count, features), f32),
             sds((count, features), bf16),
         ),
-        normed, npool, xpool, norms, mine(low_t, low_i), mine(high_t, high_i),
-        packed[: 4 * features],
+        normed, npool, xpool, norms, facts_by_row,
+        scratch=[
+            pltpu.VMEM((4 * features, features), bf16),
+            pltpu.SemaphoreType.DMA((-(-4 * features // part_rows),)),
+        ],
+        weights=(parts, table),
         name="attend",
     )
+    feed_rows = 2 * hidden_units + feed_skip
     block = hidden_units // 8
-    up_at, down_at = 4 * features // block, (4 * features + hidden_units) // block
-    fixed = pl.BlockSpec((count, features), lambda i: (0, 0))
-    up_spec = pl.BlockSpec((block, features), lambda i: (up_at + i, 0))
-    down_spec = pl.BlockSpec((block, features), lambda i: (down_at + i, 0))
-    slab = pl.BlockSpec((count, block), lambda i: (0, i))
-    pre_act, activated, pooled, inverse, emb = pl.pallas_call(
-        feed_kernel,
-        grid=(8,),
-        in_specs=[fixed, fixed, up_spec, down_spec],
-        out_specs=(slab, slab, fixed, pl.BlockSpec((count, 128), lambda i: (0, 0)), fixed),
-        out_shape=(
+    pre_act, activated, pooled, inverse, emb = call(
+        partial(feed_kernel, len(parts), feed_part, feed_skip, block),
+        (
             sds((count, hidden_units), f32),
             sds((count, hidden_units), bf16),
             sds((count, features), f32),
             sds((count, 128), f32),
             sds((count, features), bf16),
         ),
-        scratch_shapes=[pltpu.VMEM((count, features), f32)],
+        normed_mid, hidden,
+        scratch=[
+            pltpu.VMEM((feed_rows, features), bf16),
+            pltpu.VMEM((count, features), f32),
+            pltpu.SemaphoreType.DMA((-(-feed_rows // part_rows),)),
+        ],
+        weights=(parts, table),
         name="feed",
-    )(normed_mid, hidden, packed, packed)
-
-    img_slots = round_up(imgs + 1, 8)
-    count_row = jnp.pad(counts.astype(bf16), (0, features - imgs))[None]
+    )
+
     image_block = jnp.concatenate(
         [emb[:imgs], count_row, jnp.zeros((img_slots - imgs - 1, features), bf16)], axis=0
     )
     crossed = lax.ppermute(image_block, "tower", [(0, 1)])
     all_text = gathered(emb, "dp")
     all_images = gathered(crossed, "dp")
-    owner_place = place_in_gathered(matches // imgs, "dp")
-    place = column(owner_place * img_slots + matches % imgs, 0)
-    count_place = column(owner_place * img_slots + imgs, 0)
-    slot = column(matches % imgs, 0)
-    real = (np.arange(count) < caps).astype(np.float32)[:, None]
     row_bias = np.tile(np.where(np.arange(count) < caps, 0.0, MASKED), n)[:, None]
     col_bias = np.tile(np.where(np.arange(img_slots) < imgs, 0.0, MASKED), n)[None]
     chunk = count * min(8, n)
@@ -525,35 +716,38 @@
         partial(loss_kernel, chunk, imgs),
         (sds((count, features), f32), sds((count, features), bf16)),
         all_text, all_images, jnp.asarray(row_bias, f32), jnp.asarray(col_bias, f32),
-        emb, pooled, inverse, place, count_place, slot, jnp.asarray(real),
+        emb, pooled, inverse, facts_by_row,
         name="loss",
     )
 
-    grad_pre, grad_hidden, grad_mixed, sums = pl.pallas_call(
-        feed_back_kernel,
-        grid=(8,),
-        in_specs=[
-            fixed, fixed, fixed, pl.BlockSpec((4, features), lambda i: (0, 0)), slab,
-            up_spec, down_spec,
-        ],
-        out_specs=(slab, fixed, fixed, pl.BlockSpec((8, features), lambda i: (0, 0))),
-        out_shape=(
+    back_part = 3 * features // part_rows
+    back_skip = 4 * features - back_part * part_rows
+    back_rows = 2 * hidden_units + back_skip
+    grad_pre, grad_hidden, grad_mixed, sums, grad_att = call(
+        partial(feed_back_kernel, len(parts), back_part, back_skip, block),
+        (
             sds((count, hidden_units), bf16),
             sds((count, features), f32),
             sds((count, features), bf16),
             sds((8, features), f32),
+            sds((count, features), bf16),
         ),
-        scratch_shapes=[pltpu.VMEM((count, features), f32)],
+        grad_branch, grad_rows, hidden, norms, pre_act,
+        scratch=[
+            pltpu.VMEM((back_rows, features), bf16),
+            pltpu.VMEM((count, features), f32),
+            pltpu.SemaphoreType.DMA((-(-back_rows // part_rows),)),
+        ],
+        weights=(parts, table),
         name="feed_back",
-    )(grad_branch, grad_rows, hidden, norms, pre_act, packed, packed)
+    )
     half = features // 2
     groups = features // 256
     fold = (np.arange(total)[:, None] % length == np.arange(length)[None]).astype(np.float32)
     fold = jnp.asarray(fold, bf16)
-    grad_att, grad_q, compact_raw, compact_prob, left, right, sums = call(
-        partial(attend_back_kernel, 48, half),
+    grad_q, compact_raw, compact_prob, left, right, sums = call(
+        partial(attend_back_kernel, len(parts), 48, half),
         (
-            sds((count, features), bf16),
             sds((count, features), bf16),
             sds((groups, length, wide), bf16),
             sds((groups, length, wide), bf16),
@@ -561,9 +755,14 @@
             sds((text_rows, features - half), f32),
             sds((8, features), f32),
         ),
-        grad_mixed, grad_hidden, probs, queries, key_rows, values, caption_x,
-        pos_t.reshape(1, count), norms, sums, fold, packed[: 4 * features],
-        scratch=[pltpu.VMEM((total, features), f32)],
+        grad_att, grad_hidden, probs, queries, key_rows, values, caption_x,
+        facts, norms, sums, fold,
+        scratch=[
+            pltpu.VMEM((total, features), f32),
+            pltpu.VMEM((3 * features, features), bf16),
+            pltpu.SemaphoreType.DMA((-(-3 * features // part_rows),)),
+        ],
+        weights=(parts, table),
         name="attend_back",
     )
 

time: 372 us -> 313 us (0.84)
  waiting for transfers between devices: 168 us -> 97.1 us
  starting transfers between devices: 43.4 us -> 60.2 us
    all_gather x1 -> x0, waiting for transfers between devices: 83.4 us -> none  [local(): packed = lax.all_gather(shard, 'dp', axis=0, tiled=True)]
    ppermute x2 -> x20, waiting for transfers between devices: 17.4 us -> 39.2 us  [the longest x8 32.4 us: onward(): return lax.ppermute(block, 'dp', route)]
    ppermute x2 -> x20, starting transfers between devices: 6.91 us -> 19.2 us  [the longest x8 12.8 us: onward(): return lax.ppermute(block, 'dp', route)]
    ppermute x17, waiting for transfers between devices: 55 us -> 44.3 us  [swapped(): lax.ppermute(block, axis, [(i, i ^ bit) for i in range(lax.axis_size(axis...]
    select_n x8 -> x3, other arithmetic: 7.85 us -> 1.45 us  [mine(): return jnp.where(text, of_text, of_image)]
    ppermute x17, starting transfers between devices: 13.1 us -> 18.5 us  [swapped(): lax.ppermute(block, axis, [(i, i ^ bit) for i in range(lax.axis_size(axis...]
    slice x1 -> x0, local copies, waits for them, and re-layouts: 4.73 us -> none  [local(): packed[:4 * features]]
    unnamed x79 -> x102, local copies, waits for them, and re-layouts: 7.01 us -> 9.56 us
  transfers between devices with their start and end apart: 33 -> 50, of which waited for: 19 -> 24; matrix products, arithmetic and copies ran while one was open for 11% -> 13% of each run, Pallas kernels for 17% -> 20%
where the time goes in v2:
time: 313 us; the launch traced here: 312 us
  waiting for transfers between devices  97.1 us (31%)
  Pallas kernels  83.7 us (27%)
  starting transfers between devices  60.2 us (19%)
  local copies, waits for them, and re-layouts  27.6 us (9%)
  other arithmetic  25.6 us (8%)
  between operations  17.4 us (6%)
    pallas_call x7, Pallas kernels, call(): pl.pallas_call(kernel, out_shape=outs, in_specs=specs, out_specs=jax.tree...  78.9 us
    ppermute x17, waiting for transfers between devices, swapped(): lax.ppermute(block, axis, [(i, i ^ bit) for i in range(lax.axis_size(axis...  44.3 us
    ppermute x8, waiting for transfers between devices, onward(): return lax.ppermute(block, 'dp', route)  32.4 us
    ppermute x17, starting transfers between devices, swapped(): lax.ppermute(block, axis, [(i, i ^ bit) for i in range(lax.axis_size(axis...  18.5 us
    ppermute x8, starting transfers between devices, onward(): return lax.ppermute(block, 'dp', route)  12.8 us
    ppermute x6, starting transfers between devices, local(): placed.append(lax.ppermute(kv_share, both, route))  11.4 us
    unnamed x102, local copies, waits for them, and re-layouts  9.56 us
    ppermute x1, waiting for transfers between devices, local(): lax.ppermute(jnp.concatenate([grad_q, grad_mixed, grad_pre[:, :lower]], a...  8.34 us
  transfers between devices with their start and end apart: 50, of which 24 were waited for; matrix products, arithmetic and copies ran while one was open for 13% of the time, Pallas kernels for 20%

profile of v2, /device:TPU:0, one launch (start us, length us, event | category | flops | bytes accessed | tf_op | source)
XLA Modules:
  0.0 311.6 jit_solution(10522406748044958099)
XLA Ops:
  11.7 4.6 %collective-permute-start.2 = (bf16[288,768]{1,0:T(8,128)(2,1)S(1)}, bf16[288,768]{1,0:T(8,128)(2,1)S(1)}, u32[]{:S(2)}, u32[]{:S(2)}) collective-permute-start(bf16[288,768]{1,0:T(8,128)(2,1)S(1)} %convert_element_type.20), channel_id=1, source_target_pairs={{0,16},{1,17},{2,18},{3,19},{4,20},{5,21},{6,22},{7,23},{8,24},{9,... | collective-permute-start | bytes 1327112 | tf_op jit(solution)/shard_map/ppermute | solution.py:460
  20.5 5.7 %collective-permute-done.2 = bf16[288,768]{1,0:T(8,128)(2,1)S(1)} collective-permute-done((bf16[288,768]{1,0:T(8,128)(2,1)S(1)}, bf16[288,768]{1,0:T(8,128)(2,1)S(1)}, u32[]{:S(2)}, u32[]{:S(2)}) %collective-permute-start.2) | collective-permute-done | bytes 442400 | tf_op jit(solution)/shard_map/ppermute | solution.py:460
  33.0 3.0 reshape.47
  36.0 2.6 pad.43.captions_ref.refs_24_
  40.6 12.3 %rows.1 = (bf16[912,768]{1,0:T(8,128)(2,1)}, bf16[912,768]{1,0:T(8,128)(2,1)}, bf16[56,768]{1,0:T(8,128)(2,1)}, bf16[56,768]{1,0:T(8,128)(2,1)}, f32[56,768]{1,0...) custom-call(s32[1]{0:T(128)} %bitcast.12.text_ref, bf16[912,768]{1,0:T(8,128)(2,1)} %pad.43.captions_ref.refs_24_, ...), custom_call_target="tpu_custom_call" | custom-call | tf_op jit(solution)/shard_map/rows/pallas_call | solution.py:63
  56.1 10.0 %collective-permute-done.8.refs_6_ = bf16[576,768]{1,0:T(8,128)(2,1)} collective-permute-done((bf16[576,768]{1,0:T(8,128)(2,1)S(1)}, bf16[576,768]{1,0:T(8,128)(2,1)}, u32[]{:S(2)}, u32[]{:S(2)}) %collective-permute-start.8) | collective-permute-done | bytes 884768 | tf_op jit(solution)/shard_map/ppermute | solution.py:448
  68.2 7.3 %collective-permute-done.13.refs_11_ = bf16[576,768]{1,0:T(8,128)(2,1)S(1)} collective-permute-done((bf16[576,768]{1,0:T(8,128)(2,1)}, bf16[576,768]{1,0:T(8,128)(2,1)S(1)}, u32[]{:S(2)}, u32[]{:S(2)}) %collective-permute-start.13) | collective-permute-done | bytes 884768 | tf_op jit(solution)/shard_map/ppermute | solution.py:448
  77.2 7.8 %collective-permute-done.12.refs_10_ = bf16[576,768]{1,0:T(8,128)(2,1)S(1)} collective-permute-done((bf16[576,768]{1,0:T(8,128)(2,1)}, bf16[576,768]{1,0:T(8,128)(2,1)S(1)}, u32[]{:S(2)}, u32[]{:S(2)}) %collective-permute-start.12) | collective-permute-done | bytes 884768 | tf_op jit(solution)/shard_map/ppermute | solution.py:448
  87.2 2.5 collective-permute-done.18.refs_16_
  89.7 4.7 %collective-permute-done.16.refs_14_ = bf16[288,768]{1,0:T(8,128)(2,1)S(1)} collective-permute-done((bf16[288,768]{1,0:T(8,128)(2,1)S(1)}, bf16[288,768]{1,0:T(8,128)(2,1)S(1)}, u32[]{:S(2)}, u32[]{:S(2)}) %collective-permute-start.16) | collective-permute-done | bytes 442400 | tf_op jit(solution)/shard_map/ppermute | solution.py:448
  96.7 11.1 %attend.1 = (bf16[56,768]{1,0:T(8,128)(2,1)}, bf16[912,768]{1,0:T(8,128)(2,1)}, bf16[912,768]{1,0:T(8,128)(2,1)}, f32[3,224,912]{2,1,0:T(8,128)}, bf16[56,768]{1...) custom-call(s32[16]{0:T(128)} %compare_select_fusion.2.table_ref, bf16[576,768]{1,0:T(8,128)(2,1)} %copy-done.1, ...), custom_call_target="tpu_custom_call" | custom-call | tf_op jit(solution)/shard_map/attend/pallas_call | solution.py:63
  107.8 10.5 %feed.1 = (f32[56,3072]{1,0:T(8,128)}, bf16[56,3072]{1,0:T(8,128)(2,1)}, f32[56,768]{1,0:T(8,128)}, f32[56,128]{1,0:T(8,128)}, bf16[56,768]{1,0:T(8,128)(2,1)}) custom-call(s32[16]{0:T(128)} %compare_select_fusion.2.table_ref, bf16[576,768]{1,0:T(8,128)(2,1)} %copy-done.1, bf16[576,768]{1,0:T(8,128)(2,1)} %copy-done, bf16[576,768]{1,0:T(8,128)(2,1)} %copy-done.6, ...), custom_call_target="tpu_custom_call" | custom-call | tf_op jit(solution)/shard_map/feed/pallas_call | solution.py:63
  118.3 2.6 collective-permute-start.20
  123.2 3.0 collective-permute-done.20
  129.6 3.1 collective-permute-start.25
  136.5 2.6 collective-permute-done.26
  141.1 3.4 %collective-permute-done.22 = bf16[224,768]{1,0:T(8,128)(2,1)S(1)} collective-permute-done((bf16[224,768]{1,0:T(8,128)(2,1)S(1)}, bf16[224,768]{1,0:T(8,128)(2,1)S(1)}, u32[]{:S(2)}, u32[]{:S(2)}) %collective-permute-start.22) | collective-permute-done | bytes 344096 | tf_op jit(solution)/shard_map/ppermute | solution.py:416
  149.0 4.6 %loss.1 = (f32[56,768]{1,0:T(8,128)}, bf16[56,768]{1,0:T(8,128)(2,1)}) custom-call(bf16[896,768]{1,0:T(8,128)(2,1)} %copy-done.19, bf16[384,768]{1,0:T(8,128)(2,1)} %copy-done.25, f32[896,1]{1,0:T(8,128)} %constant.184.clone.row_bias_ref, f32[1,384]{1,0:T(1,128)} %constant.185.clone.col_bias_ref, bf16[56,768]{1,0:T(8,128)(2,1)} %get-tuple-element.94.emb_ref, ...), custom_call_target="tpu_custom_call" | custom-call | tf_op jit(solution)/shard_map/loss/pallas_call | solution.py:63
  153.6 11.4 %feed_back.1 = (bf16[56,3072]{1,0:T(8,128)(2,1)}, f32[56,768]{1,0:T(8,128)}, bf16[56,768]{1,0:T(8,128)(2,1)}, f32[8,768]{1,0:T(8,128)}, bf16[56,768]{1,0:T(8,128)(2,1)}) custom-call(s32[16]{0:T(128)} %compare_select_fusion.2.table_ref, bf16[576,768]{1,0:T(8,128)(2,1)} %copy-done.1, bf16[576,768]{1,0:T(8,128)(2,1)} %copy-done, bf16[576,768]{1,0:T(8,128)(2,1)} %copy-done.6, ...), custom_call_target="tpu_custom_call" | custom-call | tf_op jit(solution)/shard_map/feed_back/pallas_call | solution.py:63
  166.5 22.6 %attend_back.1 = (bf16[56,768]{1,0:T(8,128)(2,1)}, bf16[3,16,224]{2,1,0:T(8,128)(2,1)}, bf16[3,16,224]{2,1,0:T(8,128)(2,1)}, bf16[864,384]{1,0:T(8,128)(2,1)}, f32[864,384]{1,0:T(8,128)}, /*index=5*/f32[8,768]{1,0:T(8,128)}) custom-call(s32[16]{0:T(128)} %compare_select_fusion.2.table_ref, bf16[576,768]{1,0:T(8,128)(2,1)} %copy-done.1, ...), custom_call_target="tpu_custom_call" | custom-call | tf_op jit(solution)/shard_map/attend_back/pallas_call | solution.py:63
  190.4 5.1 %collective-permute-done.31 = bf16[3,16,224]{2,1,0:T(8,128)(2,1)S(1)} collective-permute-done((bf16[3,16,224]{2,1,0:T(8,128)(2,1)}, bf16[3,16,224]{2,1,0:T(8,128)(2,1)S(1)}, u32[]{:S(2)}, u32[]{:S(2)}) %collective-permute-start.31) | collective-permute-done | bytes 21536 | tf_op jit(solution)/shard_map/ppermute | solution.py:774
  196.2 6.3 %key_grad.1 = f32[768,768]{1,0:T(8,128)} custom-call(bf16[3,16,224]{2,1,0:T(8,128)(2,1)} %broadcast_select_fusion.compact_ref, bf16[56,768]{1,0:T(8,128)(2,1)} %get-tuple-element.140.factor_ref, bf16[912,768]{1,0:T(8,128)(2,1)} %get-tuple-element.119.normed_ref, bf16[912,16]{1,0:T(8,128)(2,1)} %constant.186.clone.refs_28_.spread_ref, ...), custom_call_target="tpu_custom_call" | custom-call | tf_op jit(solution)/shard_map/key_grad/pallas_call | solution.py:63
  202.5 1.9 slice_select_fusion
  214.5 8.3 %collective-permute-done.29 = bf16[56,3072]{1,0:T(8,128)(2,1)} collective-permute-done((bf16[56,3072]{1,0:T(8,128)(2,1)S(1)}, bf16[56,3072]{1,0:T(8,128)(2,1)}, u32[]{:S(2)}, u32[]{:S(2)}) %collective-permute-start.29) | collective-permute-done | bytes 344096 | tf_op jit(solution)/shard_map/ppermute | solution.py:775
  227.9 4.5 %all-to-all-start = ((bf16[16,56,288]{2,1,0:T(8,128)(2,1)}), bf16[16,56,288]{2,1,0:T(8,128)(2,1)S(1)}, u32[]{:S(2)}, u32[]{:S(2)}) async-start(bf16[16,56,288]{2,1,0:T(8,128)(2,1)} %bitcast.31), calls=%async_computation | async-start | bytes 1376256 | tf_op jit(solution)/shard_map/all_to_all | solution.py:788
  233.1 2.3 collective-permute-start.35
  235.9 21.5 %collective-permute-done.35 = f32[48,768]{1,0:T(8,128)S(1)} collective-permute-done((f32[48,768]{1,0:T(8,128)S(1)}, f32[48,768]{1,0:T(8,128)S(1)}, u32[]{:S(2)}, u32[]{:S(2)}) %collective-permute-start.35) | collective-permute-done | bytes 147488 | tf_op jit(solution)/shard_map/ppermute | solution.py:416
  264.0 5.5 %collective-permute-start.40 = (f32[48,768]{1,0:T(8,128)}, f32[48,768]{1,0:T(8,128)}, u32[]{:S(2)}, u32[]{:S(2)}) collective-permute-start(f32[48,768]{1,0:T(8,128)} %get-tuple-element.133), channel_id=1, source_target_pairs={{0,2},{6,3},{3,4},{20,5},{17,6},{23,7}} | collective-permute-start | bytes 442376 | tf_op jit(solution)/shard_map/ppermute | solution.py:814
  271.7 4.8 %owner.1 = (f32[288,768]{1,0:T(8,128)}, f32[1,768]{1,0:T(1,128)}) custom-call(s32[6]{0:T(128)} %stack.58.info_ref, bf16[896,288]{1,0:T(8,128)(2,1)} %bitcast.32, bf16[3,896,768]{2,1,0:T(8,128)(2,1)} %all-gather.2.cloned.1.call-done.b0_ref.b1_ref, bf16[3,896,768]{2,1,0:T(8,128)(2,1)} %all-gather.2.cloned.1.call-done.b0_ref.b1_ref), custom_call_target="tpu_custom_call" | custom-call | tf_op jit(solution)/shard_map/owner/pallas_call | solution.py:834
  284.9 2.9 collective-permute-done.44
  287.8 2.5 collective-permute-start.45
  300.4 3.2 %multiply_add_fusion = (f32[288,768]{1,0:T(8,128)}, f32[288,768]{1,0:T(8,128)}, f32[288,768]{1,0:T(8,128)}, f32[288,768]{1,0:T(8,128)}) fusion(f32[288,768]{1,0:T(8,128)S(1)} %copy-done.21, f32[288,768]{1,0:T(8,128)S(1)} %copy-done.16, f32[288,768]{1,0:T(8,128)S(1)} %copy-done.22, f32[]{:T(128)S(6)} %min.7, f32[288,768]{1,0:T(8,128)} %get-tuple-element.116, ...), kind=kLoop, calls=%fused_computation.7 | loop fusion | flops 2875392 | bytes 7962628 | tf_op jit(solution)/shard_map/add | solution.py:865
  (261 shorter events, 89.7 us)
Async XLA Ops:
  7.2 263.7 %all-gather.2.cloned.1.call-start = ((), (), s32[]{:S(2)}) async-start(), calls=%async_computation.1 | async-start | bytes 4386816 | tf_op jit(solution)/shard_map/all_gather | solution.py:792
  11.7 14.5 %collective-permute-start.2 = (bf16[288,768]{1,0:T(8,128)(2,1)S(1)}, bf16[288,768]{1,0:T(8,128)(2,1)S(1)}, u32[]{:S(2)}, u32[]{:S(2)}) collective-permute-start(bf16[288,768]{1,0:T(8,128)(2,1)S(1)} %convert_element_type.20), channel_id=1, source_target_pairs={{0,16},{1,17},{2,18},{3,19},{4,20},{5,21},{6,22},{7,23},{8,24},{9,... | collective-permute-start | bytes 1327112 | tf_op jit(solution)/shard_map/ppermute | solution.py:460
  16.4 13.2 %collective-permute-start.4 = (bf16[576,768]{1,0:T(8,128)(2,1)S(1)}, bf16[576,768]{1,0:T(8,128)(2,1)S(1)}, u32[]{:S(2)}, u32[]{:S(2)}) collective-permute-start(bf16[576,768]{1,0:T(8,128)(2,1)S(1)} %fusion.refs_1_), channel_id=1, source_target_pairs={{0,4},{1,3},{4,8},{5,1},{8,12},{9,5},{12,14},{13,9},{14,10},{15,13... | collective-permute-start | bytes 2654216 | tf_op jit(solution)/shard_map/ppermute | solution.py:448
  29.7 23.2 %collective-permute-start.5 = (bf16[576,768]{1,0:T(8,128)(2,1)S(1)}, bf16[576,768]{1,0:T(8,128)(2,1)S(1)}, u32[]{:S(2)}, u32[]{:S(2)}) collective-permute-start(bf16[576,768]{1,0:T(8,128)(2,1)S(1)} %fusion.1.refs_0_), channel_id=1, source_target_pairs={{0,4},{1,3},{4,8},{5,1},{8,12},{9,5},{12,14},{13,9},{14,10},{15,13... | collective-permute-start | bytes 2654216 | tf_op jit(solution)/shard_map/ppermute | solution.py:448
  31.4 23.2 %collective-permute-start.9 = (bf16[576,768]{1,0:T(8,128)(2,1)S(1)}, bf16[576,768]{1,0:T(8,128)(2,1)}, u32[]{:S(2)}, u32[]{:S(2)}) collective-permute-start(bf16[576,768]{1,0:T(8,128)(2,1)S(1)} %collective-permute-done.4.refs_3_), channel_id=1, source_target_pairs={{0,4},{1,3},{4,8},{5,1},{8,12},{9,5},{12,14},{13,9},{14,10},{15,13... | collective-permute-start | bytes 2654216 | tf_op jit(solution)/shard_map/ppermute | solution.py:448
  52.9 13.2 %collective-permute-start.8 = (bf16[576,768]{1,0:T(8,128)(2,1)S(1)}, bf16[576,768]{1,0:T(8,128)(2,1)}, u32[]{:S(2)}, u32[]{:S(2)}) collective-permute-start(bf16[576,768]{1,0:T(8,128)(2,1)S(1)} %collective-permute-done.5.refs_2_), channel_id=1, source_target_pairs={{0,4},{1,3},{4,8},{5,1},{8,12},{9,5},{12,14},{13,9},{14,10},{15,13... | collective-permute-start | bytes 2654216 | tf_op jit(solution)/shard_map/ppermute | solution.py:448
  54.5 20.9 %collective-permute-start.13 = (bf16[576,768]{1,0:T(8,128)(2,1)}, bf16[576,768]{1,0:T(8,128)(2,1)S(1)}, u32[]{:S(2)}, u32[]{:S(2)}) collective-permute-start(bf16[576,768]{1,0:T(8,128)(2,1)} %collective-permute-done.9.refs_7_), channel_id=1, source_target_pairs={{0,4},{1,3},{4,8},{5,1},{8,12},{9,5},{12,14},{13,9},{14,10},{15,13... | collective-permute-start | bytes 2654216 | tf_op jit(solution)/shard_map/ppermute | solution.py:448
  66.1 18.9 %collective-permute-start.12 = (bf16[576,768]{1,0:T(8,128)(2,1)}, bf16[576,768]{1,0:T(8,128)(2,1)S(1)}, u32[]{:S(2)}, u32[]{:S(2)}) collective-permute-start(bf16[576,768]{1,0:T(8,128)(2,1)} %collective-permute-done.8.refs_6_), channel_id=1, source_target_pairs={{0,4},{1,3},{4,8},{5,1},{8,12},{9,5},{12,14},{13,9},{14,10},{15,13... | collective-permute-start | bytes 2654216 | tf_op jit(solution)/shard_map/ppermute | solution.py:448
  67.7 17.3 %collective-permute-start.7 = (bf16[576,768]{1,0:T(8,128)(2,1)S(1)}, bf16[576,768]{1,0:T(8,128)(2,1)}, u32[]{:S(2)}, u32[]{:S(2)}) collective-permute-start(bf16[576,768]{1,0:T(8,128)(2,1)S(1)} %collective-permute-done.4.refs_3_), channel_id=1, source_target_pairs={{0,1},{1,0},{2,3},{3,2},{4,5},{5,4},{6,7},{7,6},{8,9},{9,8},{10,11... | collective-permute-start | bytes 2654216 | tf_op jit(solution)/shard_map/ppermute | solution.py:445
  67.7 17.9 %collective-permute-start.6 = (bf16[576,768]{1,0:T(8,128)(2,1)S(1)}, bf16[576,768]{1,0:T(8,128)(2,1)}, u32[]{:S(2)}, u32[]{:S(2)}) collective-permute-start(bf16[576,768]{1,0:T(8,128)(2,1)S(1)} %collective-permute-done.5.refs_2_), channel_id=1, source_target_pairs={{0,1},{1,0},{2,3},{3,2},{4,5},{5,4},{6,7},{7,6},{8,9},{9,8},{10,11... | collective-permute-start | bytes 2654216 | tf_op jit(solution)/shard_map/ppermute | solution.py:445
  68.2 19.0 %collective-permute-start.11 = (bf16[576,768]{1,0:T(8,128)(2,1)}, bf16[576,768]{1,0:T(8,128)(2,1)}, u32[]{:S(2)}, u32[]{:S(2)}) collective-permute-start(bf16[576,768]{1,0:T(8,128)(2,1)} %collective-permute-done.9.refs_7_), channel_id=1, source_target_pairs={{0,1},{1,0},{2,3},{3,2},{4,5},{5,4},{6,7},{7,6},{8,9},{9,8},{10,11... | collective-permute-start | bytes 2654216 | tf_op jit(solution)/shard_map/ppermute | solution.py:445
  75.5 14.2 %collective-permute-start.18 = (bf16[288,768]{1,0:T(8,128)(2,1)S(1)}, bf16[288,768]{1,0:T(8,128)(2,1)S(1)}, u32[]{:S(2)}, u32[]{:S(2)}) collective-permute-start(bf16[288,768]{1,0:T(8,128)(2,1)S(1)} %constant_dynamic-slice_fusion), channel_id=1, source_target_pairs={{0,4},{1,3},{4,8},{5,1},{8,12},{9,5},{12,14},{13,9},{14,10},{15,13... | collective-permute-start | bytes 1327112 | tf_op jit(solution)/shard_map/ppermute | solution.py:448
  85.0 9.6 %collective-permute-start.10 = (bf16[576,768]{1,0:T(8,128)(2,1)}, bf16[576,768]{1,0:T(8,128)(2,1)S(1)}, u32[]{:S(2)}, u32[]{:S(2)}) collective-permute-start(bf16[576,768]{1,0:T(8,128)(2,1)} %collective-permute-done.8.refs_6_), channel_id=1, source_target_pairs={{0,1},{1,0},{2,3},{3,2},{4,5},{5,4},{6,7},{7,6},{8,9},{9,8},{10,11... | collective-permute-start | bytes 2654216 | tf_op jit(solution)/shard_map/ppermute | solution.py:445
  85.0 9.5 %collective-permute-start.15 = (bf16[576,768]{1,0:T(8,128)(2,1)S(1)}, bf16[576,768]{1,0:T(8,128)(2,1)S(1)}, u32[]{:S(2)}, u32[]{:S(2)}) collective-permute-start(bf16[576,768]{1,0:T(8,128)(2,1)S(1)} %collective-permute-done.13.refs_11_), channel_id=1, source_target_pairs={{0,1},{1,0},{2,3},{3,2},{4,5},{5,4},{6,7},{7,6},{8,9},{9,8},{10,11... | collective-permute-start | bytes 2654216 | tf_op jit(solution)/shard_map/ppermute | solution.py:445
  85.6 8.9 %collective-permute-start.16 = (bf16[288,768]{1,0:T(8,128)(2,1)S(1)}, bf16[288,768]{1,0:T(8,128)(2,1)S(1)}, u32[]{:S(2)}, u32[]{:S(2)}) collective-permute-start(bf16[288,768]{1,0:T(8,128)(2,1)S(1)} %constant_dynamic-slice_fusion.1), channel_id=1, source_target_pairs={{0,4},{1,3},{4,8},{5,1},{8,12},{9,5},{12,14},{13,9},{14,10},{15,13... | collective-permute-start | bytes 1327112 | tf_op jit(solution)/shard_map/ppermute | solution.py:448
  87.2 7.4 %collective-permute-start.14 = (bf16[576,768]{1,0:T(8,128)(2,1)S(1)}, bf16[576,768]{1,0:T(8,128)(2,1)S(1)}, u32[]{:S(2)}, u32[]{:S(2)}) collective-permute-start(bf16[576,768]{1,0:T(8,128)(2,1)S(1)} %collective-permute-done.12.refs_10_), channel_id=1, source_target_pairs={{0,1},{1,0},{2,3},{3,2},{4,5},{5,4},{6,7},{7,6},{8,9},{9,8},{10,11... | collective-permute-start | bytes 2654216 | tf_op jit(solution)/shard_map/ppermute | solution.py:445
  118.3 7.9 %collective-permute-start.20 = (bf16[56,768]{1,0:T(8,128)(2,1)}, bf16[56,768]{1,0:T(8,128)(2,1)S(1)}, u32[]{:S(2)}, u32[]{:S(2)}) collective-permute-start(bf16[56,768]{1,0:T(8,128)(2,1)} %get-tuple-element.94.emb_ref), channel_id=1, source_target_pairs={{0,8},{1,9},{2,10},{3,11},{4,12},{5,13},{6,14},{7,15},{8,0},{9,1},... | collective-permute-start | bytes 258056 | tf_op jit(solution)/shard_map/ppermute | solution.py:416
  121.9 7.7 %collective-permute-start.24 = (bf16[24,768]{1,0:T(8,128)(2,1)S(1)}, bf16[24,768]{1,0:T(8,128)(2,1)S(1)}, u32[]{:S(2)}, u32[]{:S(2)}) collective-permute-start(bf16[24,768]{1,0:T(8,128)(2,1)S(1)} %maximum_maximum_fusion), channel_id=1, source_target_pairs={{0,16},{1,17},{2,18},{3,19},{4,20},{5,21},{6,22},{7,23},{8,24},{9,... | collective-permute-start | bytes 110600 | tf_op jit(solution)/shard_map/ppermute | solution.py:709
  128.1 36.9 %collective-permute-start.30 = (bf16[56,2304]{1,0:T(8,128)(2,1)S(1)}, bf16[56,2304]{1,0:T(8,128)(2,1)S(1)}, u32[]{:S(2)}, u32[]{:S(2)}) collective-permute-start(bf16[56,2304]{1,0:T(8,128)(2,1)S(1)} %pad_maximum_fusion.4), channel_id=1, source_target_pairs={{16,0},{17,1},{18,2},{19,3},{20,4},{21,5},{22,6},{23,7},{24,8},{25... | collective-permute-start | bytes 774152 | tf_op jit(solution)/shard_map/ppermute | solution.py:771
  134.5 10.0 %collective-permute-start.22 = (bf16[224,768]{1,0:T(8,128)(2,1)S(1)}, bf16[224,768]{1,0:T(8,128)(2,1)S(1)}, u32[]{:S(2)}, u32[]{:S(2)}) collective-permute-start(bf16[224,768]{1,0:T(8,128)(2,1)S(1)} %pad_maximum_fusion.1), channel_id=1, source_target_pairs={{0,2},{1,3},{2,0},{3,1},{4,6},{5,7},{6,4},{7,5},{8,10},{9,11},{10,... | collective-permute-start | bytes 1032200 | tf_op jit(solution)/shard_map/ppermute | solution.py:416
  209.1 15.6 %collective-permute-start.33 = (f32[192,768]{1,0:T(8,128)S(1)}, f32[192,768]{1,0:T(8,128)S(1)}, u32[]{:S(2)}, u32[]{:S(2)}) collective-permute-start(f32[192,768]{1,0:T(8,128)S(1)} %slice_select_fusion.1), channel_id=1, source_target_pairs={{0,2},{1,3},{2,0},{3,1},{4,6},{5,7},{6,4},{7,5},{8,10},{9,11},{10,... | collective-permute-start | bytes 1769480 | tf_op jit(solution)/shard_map/ppermute | solution.py:416
  209.9 12.9 %collective-permute-start.29 = (bf16[56,3072]{1,0:T(8,128)(2,1)S(1)}, bf16[56,3072]{1,0:T(8,128)(2,1)}, u32[]{:S(2)}, u32[]{:S(2)}) collective-permute-start(bf16[56,3072]{1,0:T(8,128)(2,1)S(1)} %pad_maximum_fusion.2), channel_id=1, source_target_pairs={{16,0},{17,1},{18,2},{19,3},{20,4},{21,5},{22,6},{23,7},{24,8},{25... | collective-permute-start | bytes 1032200 | tf_op jit(solution)/shard_map/ppermute | solution.py:775
  213.2 45.6 %collective-permute-start.47 = (bf16[864,384]{1,0:T(8,128)(2,1)}, bf16[864,384]{1,0:T(8,128)(2,1)S(1)}, u32[]{:S(2)}, u32[]{:S(2)}) collective-permute-start(bf16[864,384]{1,0:T(8,128)(2,1)} %get-tuple-element.123), channel_id=1, source_target_pairs={{16,0},{17,1},{18,2},{19,3},{20,4},{21,5},{22,6},{23,7},{24,8},{25... | collective-permute-start | bytes 1990664 | tf_op jit(solution)/shard_map/ppermute | solution.py:778
  224.9 8.1 %collective-permute-start.34 = (f32[96,768]{1,0:T(8,128)S(1)}, f32[96,768]{1,0:T(8,128)S(1)}, u32[]{:S(2)}, u32[]{:S(2)}) collective-permute-start(f32[96,768]{1,0:T(8,128)S(1)} %slice_select_fusion.2), channel_id=1, source_target_pairs={{0,4},{1,5},{2,6},{3,7},{4,0},{5,1},{6,2},{7,3},{8,12},{9,13},{10,... | collective-permute-start | bytes 884744 | tf_op jit(solution)/shard_map/ppermute | solution.py:416
  227.9 43.0 %all-to-all-start = ((bf16[16,56,288]{2,1,0:T(8,128)(2,1)}), bf16[16,56,288]{2,1,0:T(8,128)(2,1)S(1)}, u32[]{:S(2)}, u32[]{:S(2)}) async-start(bf16[16,56,288]{2,1,0:T(8,128)(2,1)} %bitcast.31), calls=%async_computation | async-start | bytes 1376256 | tf_op jit(solution)/shard_map/all_to_all | solution.py:788
  233.1 24.4 %collective-permute-start.35 = (f32[48,768]{1,0:T(8,128)S(1)}, f32[48,768]{1,0:T(8,128)S(1)}, u32[]{:S(2)}, u32[]{:S(2)}) collective-permute-start(f32[48,768]{1,0:T(8,128)S(1)} %slice_select_fusion.3), channel_id=1, source_target_pairs={{0,8},{1,9},{2,10},{3,11},{4,12},{5,13},{6,14},{7,15},{8,0},{9,1},... | collective-permute-start | bytes 442376 | tf_op jit(solution)/shard_map/ppermute | solution.py:416
  258.2 11.4 %collective-permute-start.36 = (f32[48,768]{1,0:T(8,128)}, f32[48,768]{1,0:T(8,128)S(1)}, u32[]{:S(2)}, u32[]{:S(2)}) collective-permute-start(f32[48,768]{1,0:T(8,128)} %get-tuple-element.133), channel_id=1, source_target_pairs={{4,3},{1,4},{7,5},{18,6},{21,7}} | collective-permute-start | bytes 442376 | tf_op jit(solution)/shard_map/ppermute | solution.py:814
  260.1 18.0 %collective-permute-start.37 = (f32[48,768]{1,0:T(8,128)}, f32[48,768]{1,0:T(8,128)}, u32[]{:S(2)}, u32[]{:S(2)}) collective-permute-start(f32[48,768]{1,0:T(8,128)} %get-tuple-element.133), channel_id=1, source_target_pairs={{12,3},{9,4},{15,5},{26,6},{29,7}} | collective-permute-start | bytes 442376 | tf_op jit(solution)/shard_map/ppermute | solution.py:814
  261.4 19.8 %collective-permute-start.38 = (f32[48,768]{1,0:T(8,128)}, f32[48,768]{1,0:T(8,128)}, u32[]{:S(2)}, u32[]{:S(2)}) collective-permute-start(f32[48,768]{1,0:T(8,128)} %get-tuple-element.133), channel_id=1, source_target_pairs={{2,3},{5,4},{16,5},{22,6},{19,7}} | collective-permute-start | bytes 442376 | tf_op jit(solution)/shard_map/ppermute | solution.py:814
  262.7 21.3 %collective-permute-start.39 = (f32[48,768]{1,0:T(8,128)}, f32[48,768]{1,0:T(8,128)}, u32[]{:S(2)}, u32[]{:S(2)}) collective-permute-start(f32[48,768]{1,0:T(8,128)} %get-tuple-element.133), channel_id=1, source_target_pairs={{10,3},{13,4},{24,5},{30,6},{27,7}} | collective-permute-start | bytes 442376 | tf_op jit(solution)/shard_map/ppermute | solution.py:814
  264.0 26.3 %collective-permute-start.40 = (f32[48,768]{1,0:T(8,128)}, f32[48,768]{1,0:T(8,128)}, u32[]{:S(2)}, u32[]{:S(2)}) collective-permute-start(f32[48,768]{1,0:T(8,128)} %get-tuple-element.133), channel_id=1, source_target_pairs={{0,2},{6,3},{3,4},{20,5},{17,6},{23,7}} | collective-permute-start | bytes 442376 | tf_op jit(solution)/shard_map/ppermute | solution.py:814
  269.5 24.2 %collective-permute-start.41 = (f32[48,768]{1,0:T(8,128)}, f32[48,768]{1,0:T(8,128)}, u32[]{:S(2)}, u32[]{:S(2)}) collective-permute-start(f32[48,768]{1,0:T(8,128)} %get-tuple-element.133), channel_id=1, source_target_pairs={{8,2},{14,3},{11,4},{28,5},{25,6},{31,7}} | collective-permute-start | bytes 442376 | tf_op jit(solution)/shard_map/ppermute | solution.py:814
  (62 other events, 491.7 us)
Sparse Core Ops, SparseCore 0:
  166.6 49.5 all-gather.1

commit v3 on v2

v3 whole, which is shorter than its diff:
```python
from functools import partial
import math

import jax
import jax.numpy as jnp
import numpy as np
from jax import lax
from jax.experimental import pallas as pl
from jax.experimental.pallas import tpu as pltpu
from jax.sharding import PartitionSpec as P

HEAD_DIM = 64
GROUP = 4

EPSILON = 1e-06
LOGIT_SCALE = 50.0
CLIP_NORM = 1.0
MOMENTUM_RATE = 0.9
DECAY_RATE = 0.0001
AVERAGE_RATE = 0.7
MASKED = -1e30
GELU_A = 0.044715
GELU_C = math.sqrt(2.0 / math.pi)

POS_TEXT, POS_IMAGE, LOW, HIGH, PLACE, COUNT_PLACE, SLOT, REAL = range(8)

f32 = jnp.float32
bf16 = jnp.bfloat16


def round_up(value, step):
    return (value + step - 1) // step * step


def dot_nn(left, right, **kw):
    return lax.dot_general(
        left, right, (((1,), (0,)), ((), ())), preferred_element_type=f32, **kw
    )


def dot_nt(left, right):
    return lax.dot_general(left, right, (((1,), (1,)), ((), ())), preferred_element_type=f32)


def dot_tn(left, right):
    return lax.dot_general(left, right, (((0,), (0,)), ((), ())), preferred_element_type=f32)


def call(
    kernel, outs, *args, scratch=(), name=None, weights=None, smem=None, micros=5, in_hbm=False,
    aliases=None,
):
    space = pl.BlockSpec(memory_space=pltpu.HBM if in_hbm else pltpu.VMEM)
    specs = [space] * len(args)
    if smem is not None:
        specs = [pl.BlockSpec(memory_space=pltpu.SMEM)] + specs
        args = (smem, *args)
    if weights is not None:
        parts, table = weights
        specs = (
            [pl.BlockSpec(memory_space=pltpu.SMEM)]
            + [pl.BlockSpec(memory_space=pltpu.HBM)] * len(parts)
            + specs
        )
        args = (table, *parts, *args)
    return pl.pallas_call(
        kernel,
        out_shape=outs,
        in_specs=specs,
        out_specs=jax.tree.map(lambda _: space, outs),
        scratch_shapes=list(scratch),
        input_output_aliases=aliases or {},
        cost_estimate=pl.CostEstimate(
            flops=micros * 1_000_000_000, bytes_accessed=micros * 2_000_000, transcendentals=0
        ),
        name=name,
    )(*args)


def sds(shape, dtype):
    return jax.ShapeDtypeStruct(shape, dtype)


def normalize(rows):
    middle = jnp.mean(rows, axis=-1, keepdims=True)
    centred = rows - middle
    spread = jnp.mean(centred * centred, axis=-1, keepdims=True)
    scale = lax.rsqrt(spread + EPSILON)
    return centred * scale, scale


def norm_pull(grad, rows, gain):
    unit, scale = normalize(rows)
    scaled = grad * gain
    pulled = scale * (
        scaled
        - jnp.mean(scaled, axis=-1, keepdims=True)
        - unit * jnp.mean(scaled * unit, axis=-1, keepdims=True)
    )
    return pulled, grad * unit


def lanes_of_heads(count):
    return lax.broadcasted_iota(jnp.int32, (count, GROUP * HEAD_DIM), 1) // HEAD_DIM


def stack_heads(block):
    lanes = lanes_of_heads(block.shape[0])
    zero = jnp.zeros_like(block)
    return jnp.concatenate([jnp.where(lanes == h, block, zero) for h in range(GROUP)], axis=0)


def unstack_heads(block):
    count = block.shape[0] // GROUP
    lanes = lanes_of_heads(count)
    total = jnp.where(lanes == 0, block[:count], 0.0)
    for h in range(1, GROUP):
        total = jnp.where(lanes == h, block[h * count : (h + 1) * count], total)
    return total


def group_slice(index, base=0):
    return pl.ds(pl.multiple_of(base + index * 256, 256), 256)


def rows_kernel(
    step, text_ref, captions_ref, images_ref, facts_ref, norms_t_ref, norms_i_ref,
    normed_t_ref, normed_ref, npool_t_ref, npool_ref, xpool_ref, facts_out_ref, norms_ref,
):
    facts_out_ref[...] = facts_ref[...]
    norms_ref[...] = jnp.where(text_ref[0] == 1, norms_t_ref[...], norms_i_ref[...])

    def pooled(x_ref, fact, from_ref, to_ref):
        count = to_ref.shape[0]
        pick = (
            lax.broadcasted_iota(jnp.int32, (count, x_ref.shape[0]), 1)
            == facts_ref[:, fact : fact + 1]
        ).astype(bf16)
        to_ref[...] = dot_nn(pick, from_ref[...]).astype(bf16)
        xpool_ref[...] = dot_nn(pick, x_ref[...])

    @pl.loop(0, captions_ref.shape[0] // step)
    def _(i):
        here = pl.ds(pl.multiple_of(i * step, step), step)
        unit, _ = normalize(captions_ref[here, :].astype(f32))
        normed_t_ref[here, :] = (unit * norms_t_ref[0:1, :] + norms_t_ref[1:2, :]).astype(bf16)

    pooled(captions_ref, POS_TEXT, normed_t_ref, npool_t_ref)

    @pl.when(text_ref[0] == 1)
    def _():
        normed_ref[...] = normed_t_ref[...]
        npool_ref[...] = npool_t_ref[...]

    @pl.when(text_ref[0] == 0)
    def _():
        @pl.loop(0, images_ref.shape[0] // step)
        def _(i):
            here = pl.ds(pl.multiple_of(i * step, step), step)
            unit, _ = normalize(images_ref[here, :].astype(f32))
            normed_ref[here, :] = (unit * norms_i_ref[0:1, :] + norms_i_ref[1:2, :]).astype(bf16)

        pooled(images_ref, POS_IMAGE, normed_ref, npool_ref)


class Waits:
    def __init__(self, waits, size):
        self.waits, self.size, self.done = waits, size, set()

    def __call__(self, low, high):
        for u in range(low // self.size, -(-high // self.size)):
            if u not in self.done:
                self.done.add(u)
                self.waits[u]()


def attend_kernel(parts, table_ref, *refs):
    part_refs = refs[:parts]
    (
        normed_ref, npool_ref, xpool_ref, norms_ref, facts_ref, fold_ref,
        q_ref, k_ref, v_ref, probs_ref, folded_ref, att_ref, hidden_ref, nm_ref, w_ref, sems,
    ) = refs[parts:]
    count, features = npool_ref.shape
    total = normed_ref.shape[0]
    need = Waits(
        fetch(table_ref, part_refs, 0, 4 * features, w_ref, sems), part_refs[0].shape[0]
    )
    keys = lax.broadcasted_iota(jnp.int32, (count, total), 1)
    allowed = ((keys >= facts_ref[:, LOW : LOW + 1]) & (keys < facts_ref[:, HIGH : HIGH + 1]))[None]
    need(0, features)
    q_ref[...] = dot_nt(npool_ref[...], w_ref[pl.ds(0, features), :]).astype(bf16)
    for to_ref, base in ((k_ref, features), (v_ref, 2 * features)):
        need(base, base + features)
        wide = features // 2

        @pl.loop(0, 2)
        def _(i, to_ref=to_ref, base=base):
            here = pl.ds(pl.multiple_of(i * wide, 128), wide)
            from_rows = pl.ds(pl.multiple_of(base + i * wide, 128), wide)
            to_ref[:, here] = dot_nt(normed_ref[...], w_ref[from_rows, :]).astype(bf16)

    @pl.loop(0, features // 256)
    def _(i):
        cols = group_slice(i)
        scores = dot_nt(stack_heads(q_ref[:, cols]), k_ref[:, cols]) * HEAD_DIM**-0.5
        scores = jnp.where(allowed, scores.reshape(GROUP, count, total), MASKED)
        exponent = jnp.exp(scores - jnp.max(scores, axis=-1, keepdims=True))
        probs = exponent / jnp.sum(exponent, axis=-1, keepdims=True)
        probs = probs.reshape(GROUP * count, total)
        probs_ref[i] = probs
        low = probs.astype(bf16)
        att_ref[:, cols] = unstack_heads(dot_nn(low, v_ref[:, cols])).astype(bf16)
        folded_ref[i] = dot_nt(fold_ref[...], low).astype(bf16)

    need(3 * features, 4 * features)
    hidden = xpool_ref[...] + dot_nt(
        att_ref[...], w_ref[pl.ds(3 * features, features), :]
    )
    hidden_ref[...] = hidden
    unit, _ = normalize(hidden)
    nm_ref[...] = (unit * norms_ref[2:3, :] + norms_ref[3:4, :]).astype(bf16)


def gelu_parts(pre):
    tanh = jnp.tanh(GELU_C * (pre + GELU_A * pre * pre * pre))
    return 0.5 * (1.0 + tanh), tanh


def feed_kernel(parts, first, skip, blocks, images, table_ref, *refs):
    part_refs = refs[:parts]
    (
        text_ref, nm_ref, hidden_ref, count_ref,
        pre_ref, act_ref, pooled_ref, inverse_ref, emb_ref, w_ref, total_ref, sems,
    ) = refs[parts:]
    units = pre_ref.shape[1]
    block = units // blocks
    need = Waits(
        fetch(table_ref, part_refs, first, w_ref.shape[0], w_ref, sems), part_refs[0].shape[0]
    )
    for i in range(blocks):
        here = pl.ds(i * block, block)
        up, down = skip + i * block, skip + units + i * block
        need(up, up + block)
        pre = dot_nt(nm_ref[...], w_ref[pl.ds(up, block), :])
        pre_ref[:, here] = pre
        act = (pre * gelu_parts(pre)[0]).astype(bf16)
        act_ref[:, here] = act
        need(down, down + block)
        part = dot_nn(act, w_ref[pl.ds(down, block), :])
        total_ref[...] = part + (hidden_ref[...] if i == 0 else total_ref[...])

    need(0, w_ref.shape[0])
    pooled = total_ref[...]
    inverse = lax.rsqrt(jnp.sum(pooled * pooled, axis=-1, keepdims=True) + EPSILON)
    pooled_ref[...] = pooled
    inverse_ref[...] = jnp.broadcast_to(inverse, inverse_ref.shape)
    emb = pooled * inverse
    counted = (lax.broadcasted_iota(jnp.int32, emb.shape, 0) == images) & (text_ref[0] == 0)
    emb_ref[...] = jnp.where(counted, count_ref[...], emb).astype(bf16)


def loss_kernel(
    chunk, text_a_ref, text_b_ref, img_a_ref, img_b_ref, row_bias_ref, col_bias_ref,
    emb_ref, pooled_ref, inverse_ref, facts_ref, grad_ref, branch_ref, img_ref,
):
    images = img_ref.shape[0]
    count = emb_ref.shape[0]
    img_ref[pl.ds(0, images // 2), :] = img_a_ref[...]
    img_ref[pl.ds(images // 2, images // 2), :] = img_b_ref[...]
    top, acc = jnp.full((1, images), MASKED, f32), jnp.zeros((1, images), f32)
    for text_ref in (text_a_ref, text_b_ref):

        def body(j, carry, text_ref=text_ref):
            top, acc = carry
            here = pl.ds(pl.multiple_of(j * chunk, 8), chunk)
            logits = LOGIT_SCALE * dot_nt(text_ref[here, :], img_ref[...]) + row_bias_ref[...]
            higher = jnp.maximum(top, jnp.max(logits, axis=0, keepdims=True))
            acc = acc * jnp.exp(top - higher) + jnp.sum(
                jnp.exp(logits - higher), axis=0, keepdims=True
            )
            return higher, acc

        top, acc = lax.fori_loop(0, text_ref.shape[0] // chunk, body, (top, acc))

    column_lse = top + jnp.log(acc)
    logits = LOGIT_SCALE * dot_nt(emb_ref[...], img_ref[...])
    masked = logits + col_bias_ref[...]
    row_top = jnp.max(masked, axis=1, keepdims=True)
    row_exp = jnp.exp(masked - row_top)
    by_row = row_exp / jnp.sum(row_exp, axis=1, keepdims=True)
    by_column = jnp.exp(masked - column_lse)
    columns = lax.broadcasted_iota(jnp.int32, (count, images), 1)
    target = (columns == facts_ref[:, PLACE : PLACE + 1]).astype(f32)
    listed = dot_nn((columns == facts_ref[:, COUNT_PLACE : COUNT_PLACE + 1]).astype(bf16), img_ref[...])
    at = lax.broadcasted_iota(jnp.int32, listed.shape, 1) == facts_ref[:, SLOT : SLOT + 1]
    named = jnp.maximum(jnp.sum(jnp.where(at, listed, 0.0), axis=1, keepdims=True), 1.0)
    grad_logits = 0.5 * (by_row - target) + 0.5 * (by_column - target / named)
    scaled = jnp.where(
        (col_bias_ref[...] == 0.0) & (facts_ref[:, REAL : REAL + 1] > 0), LOGIT_SCALE * grad_logits, 0.0
    ).astype(bf16)
    grad_embed = dot_nn(scaled, img_ref[...])
    pooled = pooled_ref[...]
    inverse = inverse_ref[:, 0:1]
    projection = jnp.sum(pooled * grad_embed, axis=-1, keepdims=True)
    grad_pooled = inverse * grad_embed - inverse * inverse * inverse * projection * pooled
    grad_ref[...] = grad_pooled
    branch_ref[...] = grad_pooled.astype(bf16)


def feed_back_kernel(parts, first, skip, blocks, table_ref, *refs):
    part_refs = refs[:parts]
    (
        branch_ref, grad_ref, hidden_ref, norms_ref, pre_ref,
        gpre_ref, ghidden_ref, mixed_ref, sums_ref, gatt_ref, w_ref, total_ref, sems,
    ) = refs[parts:]
    units = pre_ref.shape[1]
    features = branch_ref.shape[1]
    block = units // blocks
    need = Waits(
        fetch(table_ref, part_refs, first, w_ref.shape[0], w_ref, sems), part_refs[0].shape[0]
    )
    for i in range(blocks):
        here = pl.ds(i * block, block)
        up, down = skip + i * block, skip + units + i * block
        pre = pre_ref[:, here]
        cdf, tanh = gelu_parts(pre)
        slope = cdf + pre * 0.5 * (1.0 - tanh * tanh) * GELU_C * (1.0 + 3.0 * GELU_A * pre * pre)
        need(down, down + block)
        grad_act = dot_nt(branch_ref[...], w_ref[pl.ds(down, block), :]).astype(bf16)
        gpre = (grad_act.astype(f32) * slope).astype(bf16)
        gpre_ref[:, here] = gpre
        need(up, up + block)
        part = dot_nn(gpre, w_ref[pl.ds(up, block), :])
        total_ref[...] = part if i == 0 else part + total_ref[...]

    need(0, w_ref.shape[0])
    grad = total_ref[...]
    pulled, by_gain = norm_pull(grad, hidden_ref[...], norms_ref[2:3, :])
    ghidden = grad_ref[...] + pulled
    mixed = ghidden.astype(bf16)
    ghidden_ref[...] = ghidden
    mixed_ref[...] = mixed
    gatt_ref[...] = dot_nn(mixed, w_ref[pl.ds(skip - features, features), :]).astype(bf16)
    sums_ref[...] = jnp.zeros_like(sums_ref)
    sums_ref[2:3, :] = jnp.sum(by_gain, axis=0, keepdims=True)
    sums_ref[3:4, :] = jnp.sum(grad, axis=0, keepdims=True)


def three_parts(value):
    high = value.astype(bf16)
    rest = value - high.astype(f32)
    middle = rest.astype(bf16)
    low = (rest - middle.astype(f32)).astype(bf16)
    return jnp.concatenate([high, middle, low], axis=0)


def attend_back_kernel(parts, step, half, table_ref, *refs):
    part_refs = refs[:parts]
    (
        text_ref, gatt_ref, ghidden_ref, probs_ref, q_ref, k_ref, v_ref, x_ref, normed_ref, facts_ref,
        norms_ref, sums_in_ref,
        gq_ref, left_ref, right_ref, sums_ref, key_ref, joined_ref, grad_ref, w_ref, sems,
    ) = refs[parts:]
    count, features = gatt_ref.shape

    @pl.when(text_ref[0] == 1)
    def _():
        need = Waits(
            fetch(table_ref, part_refs, 0, 3 * features, w_ref, sems), part_refs[0].shape[0]
        )

        @pl.loop(0, features // 256)
        def _(i):
            cols = group_slice(i)
            gatt = stack_heads(gatt_ref[:, cols])
            queries = stack_heads(q_ref[:, cols])
            key_rows, values = k_ref[:, cols], v_ref[:, cols]
            probs = probs_ref[i]
            grad_probs = dot_nt(gatt, values)
            mean = jnp.sum(probs * grad_probs, axis=-1, keepdims=True)
            raw = (probs * (grad_probs - mean) * HEAD_DIM**-0.5).astype(bf16)
            gq_ref[:, cols] = unstack_heads(dot_nn(raw, key_rows)).astype(bf16)
            joined_ref[:, cols] = dot_tn(raw, queries).astype(bf16)
            joined_ref[:, group_slice(i, features)] = dot_tn(probs.astype(bf16), gatt).astype(bf16)

        need(0, 3 * features)
        gpool = dot_nn(gq_ref[...], w_ref[pl.ds(0, features), :])
        extra = jnp.concatenate([three_parts(gpool), three_parts(ghidden_ref[...])], axis=1)
        gain = norms_ref[0:1, :]
        places = facts_ref[POS_TEXT : POS_TEXT + 1, :]
        places = jnp.concatenate([places, places, places], axis=1)

        def body(j, carry):
            dgain, doffset = carry
            here = pl.ds(pl.multiple_of(j * step, 16), step)
            pick = (
                lax.broadcasted_iota(jnp.int32, (step, 3 * count), 0) + j * step == places
            ).astype(bf16)
            added = dot_nn(pick, extra)
            grad = (
                dot_nn(joined_ref[here, :], w_ref[pl.ds(features, 2 * features), :])
                + added[:, :features]
            )
            pulled, by_gain = norm_pull(grad, x_ref[here, :].astype(f32), gain)
            pulled = pulled + added[:, features:]
            left_ref[here, :] = pulled[:, :half].astype(bf16)
            right_ref[here, :] = pulled[:, half:]
            return (
                dgain + jnp.sum(by_gain, axis=0, keepdims=True),
                doffset + jnp.sum(grad, axis=0, keepdims=True),
            )

        none = jnp.zeros((1, features), f32)
        dgain, doffset = lax.fori_loop(0, left_ref.shape[0] // step, body, (none, none))
        sums_ref[...] = sums_in_ref[...]
        sums_ref[0:1, :] = dgain
        sums_ref[1:2, :] = doffset

        @pl.loop(0, features // 256)
        def _(i):
            key_ref[group_slice(i), :] = dot_tn(joined_ref[:, group_slice(i)], normed_ref[...])


def value_grad_kernel(
    text_ref, folded_hbm, factor_hbm, normed_hbm, spread_hbm, row_hbm, col_hbm, _, out_hbm,
    folded_ref, factor_ref, normed_ref, spread_ref, row_ref, col_ref, out_ref, sems,
):
    features = factor_ref.shape[1]

    @pl.when(text_ref[0] == 0)
    def _():
        moves = [
            pltpu.make_async_copy(from_hbm, to_ref, sems.at[i])
            for i, (from_hbm, to_ref) in enumerate(
                (
                    (folded_hbm, folded_ref), (factor_hbm, factor_ref), (normed_hbm, normed_ref),
                    (spread_hbm, spread_ref), (row_hbm, row_ref), (col_hbm, col_ref),
                )
            )
        ]
        for move in moves:
            move.start()
        for move in moves:
            move.wait()

        @pl.loop(0, features // 256)
        def _(i):
            factor = stack_heads(factor_ref[:, group_slice(i)])
            wide = dot_nn(spread_ref[...], folded_ref[i])
            wide = jnp.where(row_ref[...] == col_ref[...], wide, 0.0).astype(bf16)
            joined = dot_nn(wide, factor).astype(bf16)
            out_ref[group_slice(i), :] = dot_tn(joined, normed_ref[...])

        pltpu.sync_copy(out_ref, out_hbm)


def pack_kernel(lower, text_ref, pre_ref, act_ref, query_ref, late_ref, out_ref):
    features = query_ref.shape[1]
    own = out_ref.shape[2]

    def fill(pieces):
        start = 0
        for ref, first, size in pieces:
            at = start
            while at < start + size:
                to = at % own
                taken = min(own - to, start + size - at)
                from_lane = first + at - start
                out_ref[at // own, :, to : to + taken] = ref[:, from_lane : from_lane + taken]
                at += taken
            start += size

    @pl.when(text_ref[0] == 1)
    def _():
        fill([(pre_ref, lower, pre_ref.shape[1] - lower), (act_ref, 0, act_ref.shape[1])])

    @pl.when(text_ref[0] == 0)
    def _():
        first, last = features // own, 3 * features // own
        out_ref[first : last + 1] = jnp.zeros((last + 1 - first,) + out_ref.shape[1:], bf16)
        fill([(query_ref, 0, features)])
        start = 3 * features
        at = 0
        while at < features + lower:
            to = (start + at) % own
            taken = min(own - to, features + lower - at)
            out_ref[(start + at) // own, :, to : to + taken] = late_ref[:, at : at + taken]
            at += taken


def owner_kernel(info_ref, a_ref, b0_ref, b1_ref, sums_ref, out_ref, stats_ref):
    rows = lax.broadcasted_iota(jnp.int32, out_ref.shape, 0)
    edge = info_ref[2]
    out_ref[...] = dot_tn(a_ref[...], b0_ref[0])

    @pl.when(edge < out_ref.shape[0])
    def _():
        out_ref[...] = jnp.where(rows < edge, out_ref[...], dot_tn(a_ref[...], b1_ref[0]))

    place = rows + info_ref[3]
    grad = jnp.where((place < info_ref[4]) | (place >= info_ref[5]), out_ref[...], 0.0)
    out_ref[...] = grad
    at = lax.broadcasted_iota(jnp.int32, stats_ref.shape, 0)
    known = jnp.where((at < 4) & (info_ref[6] == 1), sums_ref[...], 0.0)
    stats_ref[...] = jnp.where(at == 4, jnp.sum(grad * grad, axis=0, keepdims=True), known)


def update_kernel(
    step_rate, slots, stats_ref, own_ref, *refs,
):
    placed_refs = refs[:slots]
    (
        weights_ref, momentum_ref, averages_ref, norms_ref, norm_momentum_ref, norm_averages_ref,
        grads_ref, new_weights_ref, new_momentum_ref, new_averages_ref,
        norm_grads_ref, new_norms_ref, new_norm_momentum_ref, new_norm_averages_ref, norm_ref,
    ) = refs[slots:]
    sums = stats_ref[0:4, :]
    total = jnp.sum(stats_ref[4:5, :], axis=1, keepdims=True) + jnp.sum(
        jnp.sum(sums * sums, axis=1, keepdims=True), axis=0, keepdims=True
    )
    grad_norm = jnp.sqrt(total)
    factor = jnp.minimum(1.0, CLIP_NORM / (grad_norm + 1e-06))
    norm_ref[...] = grad_norm

    def moved(grad, decayed, old, old_momentum, old_average):
        new_momentum = MOMENTUM_RATE * old_momentum + decayed
        new = old - step_rate * (decayed + MOMENTUM_RATE * new_momentum)
        return new, new_momentum, AVERAGE_RATE * old_average + (1.0 - AVERAGE_RATE) * new

    grad = sums * factor
    norm_grads_ref[...] = grad
    new_norms_ref[...], new_norm_momentum_ref[...], new_norm_averages_ref[...] = moved(
        grad, grad, norms_ref[...], norm_momentum_ref[...], norm_averages_ref[...]
    )
    size = own_ref.shape[0] // slots
    for s, placed_ref in enumerate(placed_refs):
        here = slice(s * size, (s + 1) * size)
        grad = (own_ref[here, :] + placed_ref[...]) * factor
        grads_ref[here, :] = grad
        old = weights_ref[here, :]
        new_weights_ref[here, :], new_momentum_ref[here, :], new_averages_ref[here, :] = moved(
            grad, grad + DECAY_RATE * old, old, momentum_ref[here, :], averages_ref[here, :]
        )


def bits_of(axis):
    size = lax.axis_size(axis)
    return [1 << b for b in range(size.bit_length() - 1)]


def swapped(block, axis, bit):
    return lax.ppermute(block, axis, [(i, i ^ bit) for i in range(lax.axis_size(axis))])


UNITS = 16


def units_gathered(low_shard, image_weights, text, prepare):
    n = lax.axis_size("dp")
    chips = n // 2
    steps = chips // 2
    index = lax.axis_index("dp")
    core = index % 2
    other_core = [(i, i ^ 1) for i in range(n)]
    order = list(range(0, chips, 2)) + list(range(1, chips, 2))[::-1]
    seat_of = np.zeros(chips, np.int32)
    seat_of[order] = np.arange(chips)
    route = []
    for s in range(chips):
        route.append((2 * order[s], 2 * order[(s + 1) % chips]))
        route.append((2 * order[s] + 1, 2 * order[s - 1] + 1))

    def pair(own, other):
        return jnp.where(
            core == 0,
            jnp.concatenate([own, other], axis=0),
            jnp.concatenate([other, own], axis=0),
        )

    def swap(block):
        return lax.ppermute(block, "dp", other_core)

    def onward(block):
        return lax.ppermute(block, "dp", route)

    def half_of(block):
        size = block.shape[0] // 2
        return lax.dynamic_slice_in_dim(block, core * size, size, axis=0)

    high = swap(low_shard)
    image = swap(image_weights)
    b_part = jnp.where(text, pair(low_shard, high), jnp.where(core == 0, image, image_weights))
    low_shard, image, image_weights, b_part = lax.optimization_barrier(
        (low_shard, image, image_weights, b_part)
    )
    over = lax.ppermute(low_shard, "tower", [(0, 1)])
    low = swap(over)
    a_part = jnp.where(text, pair(over, low), jnp.where(core == 0, image_weights, image))

    unit = np.arange(UNITS)
    part = jnp.where(text, unit // chips, unit % 2)
    far = (seat_of[None] - seat_of[:, None]) % chips
    own_far = jnp.sum(
        jnp.where(jnp.arange(chips)[None] == index // 2, jnp.asarray(far), 0), axis=1
    )
    far = jnp.where(text, jnp.tile(own_far, 2), jnp.repeat(own_far, 2))
    step = jnp.minimum(far, chips - far)
    from_other = (far < steps) == (core == 1)
    table = jnp.where(
        far == 0,
        part,
        jnp.where(
            far == steps,
            4 * steps - 2 + 2 * part + core,
            4 * step - 2 + part + 2 * from_other,
        ),
    ).astype(jnp.int32)

    parts = [a_part, b_part]
    sent_a, sent_b = a_part, b_part
    prepared = prepare(b_part)
    for step in range(1, steps):
        sent_b = onward(sent_b)
        if step == 1:
            sent_a, sent_b = lax.optimization_barrier((sent_a, sent_b))
        elif step == 2:
            sent_a, prepared, table = lax.optimization_barrier((sent_a, prepared, table))
        sent_a = onward(sent_a)
        parts += [sent_a, sent_b, swap(sent_a), swap(sent_b)]
    last_b = onward(half_of(sent_b))
    last_a = onward(half_of(sent_a))
    parts += [last_a, swap(last_a), last_b, swap(last_b)]
    return parts, table, prepared


def fetch(table_ref, part_refs, first, rows, to_ref, sems):
    size = part_refs[0].shape[0]
    half = size // 2
    whole = [p for p in part_refs if p.shape[0] == size]
    halves = part_refs[len(whole) :]
    waits = []
    for u in range(-(-rows // size)):
        taken = min(size, rows - u * size)

        def copy(from_ref, at, count, u=u):
            return pltpu.make_async_copy(
                from_ref.at[pl.ds(0, count), :], to_ref.at[pl.ds(u * size + at, count), :], sems.at[u]
            )

        for j, part_ref in enumerate(whole):

            @pl.when(table_ref[first + u] == j)
            def _(part_ref=part_ref):
                copy(part_ref, 0, taken).start()

        for j in range(len(halves)):

            @pl.when(table_ref[first + u] == len(whole) + j)
            def _(j=j):
                mine, other = halves[j // 2 * 2], halves[j // 2 * 2 + 1]
                upper, lower = (mine, other) if j % 2 == 0 else (other, mine)
                copy(upper, 0, min(half, taken)).start()
                if taken > half:
                    copy(lower, half, taken - half).start()

        waits.append(copy(whole[0], 0, taken).wait)
    return waits


def stages_of(axis):
    size = lax.axis_size(axis)
    if size == 16:
        return [(4, 8), (2,), (1,)]
    return [(bit,) for bit in reversed(bits_of(axis))]


def gather_stage(block, axis, stage):
    blocks = [block]
    for bit in range(1, 1 << len(stage)):
        other = sum(b for s, b in enumerate(stage) if bit >> s & 1)
        blocks.append(swapped(block, axis, other))
    return blocks


def place_in_gathered(device, axis):
    other = lax.axis_index(axis) ^ device
    order = [bit for stage in stages_of(axis) for bit in stage]
    return sum(((other & bit) // bit) << s for s, bit in enumerate(order))


def share_step(block, axis, bit, others=()):
    levels = lax.axis_size(axis).bit_length() - 1
    dim = levels - bit.bit_length()
    mine = ((lax.axis_index(axis) & bit) != 0).astype(jnp.int32)
    kept = lax.dynamic_slice_in_dim(block, mine, 1, axis=dim)
    sent = lax.dynamic_slice_in_dim(block, 1 - mine, 1, axis=dim)
    received, others = lax.optimization_barrier((swapped(sent, axis, bit), others))
    return kept + received, others


def summed(block, others):
    size = lax.axis_size("dp")
    if size != 16:
        for axis in ("dp", "tower"):
            for bit in bits_of(axis):
                block = block + swapped(block, axis, bit)
        return block, others
    across = [(t * size + i, (1 - t) * size + (i ^ 2)) for t in range(2) for i in range(size)]
    block = (block + lax.ppermute(block, "tower", [(0, 1), (1, 0)])) + (
        swapped(block, "dp", 2) + lax.ppermute(block, ("tower", "dp"), across)
    )
    block = (block + swapped(block, "dp", 4)) + (
        swapped(block, "dp", 8) + swapped(block, "dp", 12)
    )
    other, others = lax.optimization_barrier((swapped(block, "dp", 1), others))
    return block + other, others


def local(
    images,
    captions,
    token_ids,
    counts,
    matches,
    image_weights,
    image_norms,
    weights,
    norm_params,
    momentum,
    norm_momentum,
    averages,
    norm_averages,
):
    text = lax.axis_index("tower") == 1
    index = lax.axis_index("dp")
    n = lax.axis_size("dp")
    both = ("tower", "dp")
    caps, length, features = captions.shape
    imgs, img_rows = images.shape[:2]
    text_rows = caps * length
    own_rows = weights.shape[0]
    all_rows = 2 * n * own_rows
    hidden_units = (all_rows - 4 * features) // 2
    count = round_up(max(caps, imgs), 8)
    total = round_up(max(text_rows, imgs * img_rows), 48)
    wide = GROUP * count

    def mine(of_text, of_image):
        return jnp.where(text, of_text, of_image)

    def padded_to(values, fill):
        return jnp.pad(values, (0, count - values.shape[0]), constant_values=fill)

    def padded(rows):
        return jnp.pad(rows.reshape(-1, features), ((0, total - rows.shape[0] * rows.shape[1]), (0, 0)))

    img_slots = round_up(imgs + 1, 8)

    def prepare(ready):
        caption_in, image_in, ids, named, tallies, _ = lax.optimization_barrier(
            (captions, images, token_ids, matches, counts, ready)
        )
        caption_x = padded(caption_in)
        lengths = jnp.sum((ids != 0).astype(jnp.int32), axis=1)
        start_t = jnp.arange(caps, dtype=jnp.int32) * length
        start_i = jnp.arange(imgs, dtype=jnp.int32) * img_rows
        pos_t = start_t + lengths - 1
        owner_place = place_in_gathered(named // imgs, "dp")
        columns = [
            padded_to(pos_t, 0),
            padded_to(start_i, 0),
            mine(padded_to(start_t, 0), padded_to(start_i, 0)),
            mine(padded_to(start_t + lengths, 1), padded_to(start_i + img_rows, 1)),
            padded_to(owner_place * img_slots + named % imgs, 0),
            padded_to(owner_place * img_slots + imgs, 0),
            padded_to(named % imgs, 0),
            jnp.asarray(np.arange(count) < caps, jnp.int32),
        ]
        facts = jnp.stack(columns, axis=0)
        table = jnp.pad(facts.T, ((0, 0), (0, 128 - len(columns))))
        rows = call(
            partial(rows_kernel, 48),
            (
                sds((total, features), bf16),
                sds((total, features), bf16),
                sds((count, features), bf16),
                sds((count, features), bf16),
                sds((count, features), f32),
                sds((count, 128), jnp.int32),
                sds((4, features), f32),
            ),
            caption_x, padded(image_in), table, norm_params, image_norms,
            smem=text.astype(jnp.int32)[None],
            name="rows",
        )
        first_row = (lax.axis_index("tower") * n + index) * own_rows
        last_row = first_row + own_rows - 1
        up_row, down_row = 4 * features, 4 * features + hidden_units

        def other_of(row):
            in_low = jnp.where(row < 3 * features, 0, jnp.where(row < up_row, 1, 2))
            return jnp.where(row >= down_row, 0, in_low)

        edge = jnp.int32(own_rows)
        for boundary in (features, 3 * features, up_row, down_row):
            inside = (boundary > first_row) & (boundary <= last_row)
            edge = jnp.where(inside, boundary - first_row, edge)
        info = jnp.stack(
            [
                other_of(first_row), other_of(last_row), edge, first_row,
                jnp.int32(features), jnp.int32(3 * features), text.astype(jnp.int32),
            ]
        ).astype(jnp.int32)
        count_row = jnp.pad(tallies.astype(f32), (0, features - imgs))[None]
        return caption_x, facts, rows, count_row, info

    low_shard = weights.astype(bf16)
    if n == UNITS:
        parts, table, prepared = units_gathered(low_shard, image_weights, text, prepare)
    else:
        even = lax.ppermute(low_shard, both, [(2 * k, n + k) for k in range(n)])
        odd = lax.ppermute(low_shard, both, [(2 * k + 1, n + k) for k in range(n)])
        shard = jnp.where(text, jnp.concatenate([even, odd], axis=0), image_weights)
        packed = lax.all_gather(shard, "dp", axis=0, tiled=True)
        parts = jnp.split(packed, UNITS, axis=0)
        table = jnp.arange(UNITS, dtype=jnp.int32)
        prepared = prepare(shard)
    caption_x, facts, rows, count_row, info = prepared
    normed_t, normed, npool_t, npool, xpool, facts_by_row, norms = rows
    part_rows = all_rows // UNITS
    feed_part = 4 * features // part_rows
    feed_skip = 4 * features - feed_part * part_rows

    flag = text.astype(jnp.int32)[None]
    groups = features // 256
    fold = np.arange(length)[:, None] == np.arange(total)[None] % length
    weights_of = (parts, table)

    def loads(rows):
        return [
            pltpu.VMEM((rows, features), bf16),
            pltpu.SemaphoreType.DMA((-(-rows // part_rows),)),
        ]

    queries, key_rows, values, probs, folded, attended, hidden, normed_mid = call(
        partial(attend_kernel, len(parts)),
        (
            sds((count, features), bf16),
            sds((total, features), bf16),
            sds((total, features), bf16),
            sds((groups, wide, total), f32),
            sds((groups, length, wide), bf16),
            sds((count, features), bf16),
            sds((count, features), f32),
            sds((count, features), bf16),
        ),
        normed, npool, xpool, norms, facts_by_row, jnp.asarray(fold, bf16),
        scratch=loads(4 * features),
        weights=weights_of,
        micros=10,
        name="attend",
    )
    to_image = [(1, 0)]
    early_x = lax.ppermute(jnp.concatenate([attended, normed_mid], axis=1), "tower", to_image)
    folded_x = lax.ppermute(folded, "tower", to_image)
    feed_rows = 2 * hidden_units + feed_skip
    total_scratch = pltpu.VMEM((count, features), f32)

    def feed_scratch(rows):
        weights_at, sems = loads(rows)
        return [weights_at, total_scratch, sems]

    pre_act, activated, pooled, inverse, emb = call(
        partial(feed_kernel, len(parts), feed_part, feed_skip, 2, imgs),
        (
            sds((count, hidden_units), f32),
            sds((count, hidden_units), bf16),
            sds((count, features), f32),
            sds((count, 128), f32),
            sds((count, features), bf16),
        ),
        normed_mid, hidden, count_row,
        smem=flag,
        scratch=feed_scratch(feed_rows),
        weights=weights_of,
        micros=6,
        name="feed",
    )

    emb, early_x, folded_x = lax.optimization_barrier((emb, early_x, folded_x))

    stages = stages_of("dp")
    blocks = gather_stage(emb, "dp", stages[0])
    all_images = lax.ppermute(
        jnp.concatenate([b[:img_slots] for b in blocks], axis=0), "tower", [(0, 1)]
    )
    all_text = jnp.concatenate(blocks, axis=0)
    for stage in stages[1:-1]:
        all_text = jnp.concatenate(gather_stage(all_text, "dp", stage), axis=0)
        all_images = jnp.concatenate(gather_stage(all_images, "dp", stage), axis=0)
    all_text = gather_stage(all_text, "dp", stages[-1])
    all_images = gather_stage(all_images, "dp", stages[-1])
    chunk = count * min(8, n // 2)
    row_bias = np.tile(np.where(np.arange(count) < caps, 0.0, MASKED), chunk // count)[:, None]
    col_bias = np.tile(np.where(np.arange(img_slots) < imgs, 0.0, MASKED), n)[None]
    grad_rows, grad_branch = call(
        partial(loss_kernel, chunk),
        (sds((count, features), f32), sds((count, features), bf16)),
        *all_text, *all_images, jnp.asarray(row_bias, f32), jnp.asarray(col_bias, f32),
        emb, pooled, inverse, facts_by_row,
        scratch=[pltpu.VMEM((n * img_slots, features), bf16)],
        name="loss",
    )
    attended_x, mid_x = early_x[:, :features], early_x[:, features:]
    others = jnp.stack(
        [mine(grad_branch, npool_t), mine(grad_branch, attended_x), mine(normed_mid, mid_x)]
    )
    others, grad_branch = lax.optimization_barrier((others, grad_branch))
    others = lax.all_gather(others, "dp", axis=1, tiled=True)

    back_part = 3 * features // part_rows
    back_skip = 4 * features - back_part * part_rows
    back_rows = 2 * hidden_units + back_skip
    grad_pre, grad_hidden, grad_mixed, sums, grad_att = call(
        partial(feed_back_kernel, len(parts), back_part, back_skip, 2),
        (
            sds((count, hidden_units), bf16),
            sds((count, features), f32),
            sds((count, features), bf16),
            sds((8, features), f32),
            sds((count, features), bf16),
        ),
        grad_branch, grad_rows, hidden, norms, pre_act,
        scratch=feed_scratch(back_rows),
        weights=weights_of,
        micros=7,
        name="feed_back",
    )
    lower = all_rows // 2 - 4 * features
    grad_att_x = lax.ppermute(grad_att, "tower", to_image)
    late_x = lax.ppermute(
        jnp.concatenate([grad_mixed, grad_pre[:, :lower]], axis=1), "tower", to_image
    )

    half = features // 2
    step = max(
        s for s in range(16, 305, 16) if text_rows % s == 0
    )
    grad_q, left, right, sums, key_part = call(
        partial(attend_back_kernel, len(parts), step, half),
        (
            sds((count, features), bf16),
            sds((text_rows, half), bf16),
            sds((text_rows, features - half), f32),
            sds((8, features), f32),
            sds((features, features), f32),
        ),
        grad_att, grad_hidden, probs, queries, key_rows, values, caption_x, normed_t, facts, norms,
        sums,
        smem=flag,
        scratch=[
            pltpu.VMEM((total, 2 * features), bf16),
            pltpu.VMEM((8, 128), f32),
            *loads(3 * features),
        ],
        weights=weights_of,
        micros=16,
        name="attend_back",
    )
    grad_q, key_part, grad_att_x, late_x = lax.optimization_barrier(
        (grad_q, key_part, grad_att_x, late_x)
    )
    grad_q_x = lax.ppermute(grad_q, "tower", to_image)

    spread = jnp.asarray(fold.T, bf16)
    row_cap = jnp.asarray(np.arange(total)[:, None] // length, jnp.int32)
    col_cap = jnp.asarray(np.tile(np.arange(count), GROUP)[None], jnp.int32)
    value_in = (folded_x, grad_att_x, normed_t, spread, row_cap, col_cap)
    kv_part = call(
        value_grad_kernel,
        sds((features, features), f32),
        *value_in, key_part,
        smem=flag,
        in_hbm=True,
        aliases={len(value_in) + 1: 0},
        scratch=[
            *[pltpu.VMEM(v.shape, v.dtype) for v in value_in],
            pltpu.VMEM((features, features), f32),
            pltpu.SemaphoreType.DMA((len(value_in),)),
        ],
        name="value_grad",
    )
    share_rows = features // n
    half_share = share_rows // 2
    bits = bits_of("dp")
    kv_part = kv_part.reshape((2,) * len(bits) + (share_rows, features))
    kv_part, _ = share_step(kv_part, "dp", bits[0])
    grad_q_x, late_x, left, kv_part = lax.optimization_barrier((grad_q_x, late_x, left, kv_part))
    upper, under = kv_part[..., :half_share, :], kv_part[..., half_share:, :]
    upper_order, under_order = bits[1:], bits[2:-1] + bits[1:2] + bits[-1:]
    columns = call(
        partial(pack_kernel, lower),
        sds((n, count, own_rows), bf16),
        grad_pre, activated, grad_q_x, late_x,
        smem=flag,
        micros=2,
        name="pack",
    )
    upper, columns = share_step(upper, "dp", upper_order[0], columns)
    under, _ = share_step(under, "dp", under_order[0])
    left_x = lax.ppermute(left, "tower", to_image)
    input_grad = jnp.where(text, right, left_x.astype(f32)).reshape(caps, length, half)
    for up_bit, under_bit in zip(upper_order[1:-1], under_order[1:-1]):
        upper, input_grad = share_step(upper, "dp", up_bit, input_grad)
        under, _ = share_step(under, "dp", under_bit)

    own_columns = lax.all_to_all(columns, "dp", 0, 0, tiled=True)
    whole = lambda shape: pl.BlockSpec(shape, lambda i, s: (0, 0))
    own_grads, stats = pl.pallas_call(
        owner_kernel,
        grid_spec=pltpu.PrefetchScalarGridSpec(
            num_scalar_prefetch=1,
            grid=(1,),
            in_specs=[
                whole((n * count, own_rows)),
                pl.BlockSpec((1, n * count, features), lambda i, s: (s[0], 0, 0)),
                pl.BlockSpec((1, n * count, features), lambda i, s: (s[1], 0, 0)),
                whole((8, features)),
            ],
            out_specs=(whole((own_rows, features)), whole((8, features))),
        ),
        out_shape=(sds((own_rows, features), f32), sds((8, features), f32)),
        cost_estimate=pl.CostEstimate(
            flops=4_000_000_000, bytes_accessed=8_000_000, transcendentals=0
        ),
        name="owner",
    )(
        info, own_columns.reshape(n * count, own_rows), others, others, sums,
    )
    upper, (own_grads, stats) = share_step(upper, "dp", upper_order[-1], (own_grads, stats))
    under, _ = share_step(under, "dp", under_order[-1])
    kv_share = jnp.concatenate([upper, under], axis=-2).reshape(share_rows, features)

    core = index % 2
    kv_other = swapped(kv_share, "dp", 1)
    kv_pair = jnp.where(
        core == 0,
        jnp.concatenate([kv_share, kv_other], axis=0),
        jnp.concatenate([kv_other, kv_share], axis=0),
    )
    slots = own_rows // (2 * share_rows)
    placed = []
    for s in range(slots):
        route = []
        for owner in range(2 * n):
            row = owner * own_rows + 2 * s * share_rows
            if features <= row < 2 * features:
                route.append((n + (row - features) // share_rows + s % 2, owner))
            elif 2 * features <= row < 3 * features:
                route.append(((row - 2 * features) // share_rows + s % 2, owner))
        placed.append(lax.ppermute(kv_pair, both, route))
    kv_square = jnp.sum(kv_share * kv_share, axis=0)
    stats = stats + jnp.where(jnp.arange(8)[:, None] == 4, kv_square[None], 0.0)
    stats, placed = summed(stats, placed)
    rows_f32, small_f32 = sds((own_rows, features), f32), sds((4, features), f32)
    (
        grads, new_weights, new_momentum, new_averages,
        norm_grads, new_norm_params, new_norm_momentum, new_norm_averages, grad_norm,
    ) = call(
        partial(update_kernel, 0.4 * math.sqrt(all_rows), slots),
        (
            rows_f32, rows_f32, rows_f32, rows_f32,
            small_f32, small_f32, small_f32, small_f32, sds((1, 1), f32),
        ),
        stats, own_grads, *placed, weights, momentum, averages,
        norm_params, norm_momentum, norm_averages,
        name="update",
    )
    grad_norm = grad_norm.reshape(())
    return (
        grads,
        norm_grads,
        input_grad,
        new_weights,
        new_momentum,
        new_averages,
        new_norm_params,
        new_norm_momentum,
        new_norm_averages,
        grad_norm,
    )


def solution(mesh):
    return jax.shard_map(
        local,
        mesh=mesh,
        in_specs=(
            P("dp", None, None),
            P("dp", None, None),
            P("dp", None),
            P("dp"),
            P("dp"),
            P("dp", None),
            P(),
            P(("tower", "dp"), None),
            P(),
            P(("tower", "dp"), None),
            P(),
            P(("tower", "dp"), None),
            P(),
        ),
        out_specs=(
            P(("tower", "dp"), None),
            P(),
            P("dp", None, "tower"),
            P(("tower", "dp"), None),
            P(("tower", "dp"), None),
            P(("tower", "dp"), None),
            P(),
            P(),
            P(),
            P(),
        ),
        check_vma=False,
    )
```

time: 313 us -> 277 us (0.88)
  Pallas kernels: 83.7 us -> 68.7 us
  other arithmetic: 25.6 us -> 14.9 us
  waiting for transfers between devices: 97.1 us -> 87.8 us
  local copies, waits for them, and re-layouts: 27.6 us -> 18.5 us
  starting transfers between devices: 60.2 us -> 68.4 us
    pallas_call x7 -> x9, Pallas kernels: 78.9 us -> 64.3 us  [call(): pl.pallas_call(kernel, out_shape=outs, in_specs=specs, out_specs=jax.tree...]
    ppermute x17 -> x20, starting transfers between devices: 18.5 us -> 26.6 us  [swapped(): lax.ppermute(block, axis, [(i, i ^ bit) for i in range(lax.axis_size(axis...]
    ppermute x17 -> x20, waiting for transfers between devices: 44.3 us -> 36.3 us  [swapped(): lax.ppermute(block, axis, [(i, i ^ bit) for i in range(lax.axis_size(axis...]
    ppermute x10 -> x11, waiting for transfers between devices: 13.5 us -> 9.22 us  [the longest x1 3.09 us: local(): lax.ppermute(jnp.concatenate([grad_mixed, grad_pre[:, :lower]], axis=1),...]
    add x11, other arithmetic: 7.84 us -> 3.9 us  [the longest x7 1.57 us: share_step(): return (kept + received, others)]
    select_n x8 -> x1, other arithmetic: 3.49 us -> 0.02 us  [local(): jnp.where(core == 0, jnp.concatenate([kv_share, kv_other], axis=0), jnp.c...]
    unnamed x102 -> x76, local copies, waits for them, and re-layouts: 9.56 us -> 6.72 us
    ppermute x10 -> x11, starting transfers between devices: 16.8 us -> 14.8 us  [the longest x1 4.76 us: local(): lax.ppermute(jnp.concatenate([b[:img_slots] for b in blocks], axis=0), 't...]
  transfers between devices with their start and end apart: 50 -> 54, of which waited for: 24 -> 26; matrix products, arithmetic and copies ran while one was open for 13% -> 8% of each run, Pallas kernels for 20% -> 17%
where the time goes in v3:
time: 277 us; the launch traced here: 273 us
  waiting for transfers between devices  87.8 us (32%)
  Pallas kernels  68.7 us (25%)
  starting transfers between devices  68.4 us (25%)
  local copies, waits for them, and re-layouts  18.5 us (7%)
  other arithmetic  14.9 us (5%)
  between operations  14.8 us (5%)
    pallas_call x9, Pallas kernels, call(): pl.pallas_call(kernel, out_shape=outs, in_specs=specs, out_specs=jax.tree...  64.3 us
    ppermute x20, waiting for transfers between devices, swapped(): lax.ppermute(block, axis, [(i, i ^ bit) for i in range(lax.axis_size(axis...  36.3 us
    ppermute x8, waiting for transfers between devices, onward(): return lax.ppermute(block, 'dp', route)  34.5 us
    ppermute x20, starting transfers between devices, swapped(): lax.ppermute(block, axis, [(i, i ^ bit) for i in range(lax.axis_size(axis...  26.6 us
    ppermute x8, starting transfers between devices, onward(): return lax.ppermute(block, 'dp', route)  12.7 us
    ppermute x1, waiting for transfers between devices, units_gathered(): over = lax.ppermute(low_shard, 'tower', [(0, 1)])  7.05 us
    unnamed x76, local copies, waits for them, and re-layouts  6.72 us
    all_to_all x1, starting transfers between devices, local(): own_columns = lax.all_to_all(columns, 'dp', 0, 0, tiled=True)  5.9 us
  transfers between devices with their start and end apart: 54, of which 26 were waited for; matrix products, arithmetic and copies ran while one was open for 8% of the time, Pallas kernels for 17%

profile of v3, /device:TPU:0, one launch (start us, length us, event | category | flops | bytes accessed | tf_op | source)
XLA Modules:
  0.0 273.1 jit_solution(9510295887106212850)
XLA Ops:
  12.2 5.3 %collective-permute-start.2 = (bf16[288,768]{1,0:T(8,128)(2,1)S(1)}, bf16[288,768]{1,0:T(8,128)(2,1)}, u32[]{:S(2)}, u32[]{:S(2)}) collective-permute-start(bf16[288,768]{1,0:T(8,128)(2,1)S(1)} %convert_element_type.37), channel_id=1, source_target_pairs={{0,16},{1,17},{2,18},{3,19},{4,20},{5,21},{6,22},{7,23},{8,24},{9,... | collective-permute-start | bytes 1327112 | tf_op jit(solution)/shard_map/ppermute | solution.py:596
  19.7 7.0 %collective-permute-done.2 = bf16[288,768]{1,0:T(8,128)(2,1)} collective-permute-done((bf16[288,768]{1,0:T(8,128)(2,1)S(1)}, bf16[288,768]{1,0:T(8,128)(2,1)}, u32[]{:S(2)}, u32[]{:S(2)}) %collective-permute-start.2) | collective-permute-done | bytes 442400 | tf_op jit(solution)/shard_map/ppermute | solution.py:596
  29.0 2.6 pad.43.captions_ref.refs_25_
  38.8 12.2 %rows.1 = (bf16[912,768]{1,0:T(8,128)(2,1)}, bf16[912,768]{1,0:T(8,128)(2,1)}, bf16[56,768]{1,0:T(8,128)(2,1)}, bf16[56,768]{1,0:T(8,128)(2,1)}, f32[56,768]{1,0...) custom-call(s32[1]{0:T(128)} %bitcast.8.text_ref.refs_18_, bf16[912,768]{1,0:T(8,128)(2,1)} %pad.43.captions_ref.refs_25_, ...), custom_call_target="tpu_custom_call" | custom-call | flops 5000000000 | bytes 10000000 | tf_op jit(solution)/shard_map/rows/pallas_call | solution.py:66
  53.2 4.2 %collective-permute-done.9.refs_7_ = bf16[576,768]{1,0:T(8,128)(2,1)S(1)} collective-permute-done((bf16[576,768]{1,0:T(8,128)(2,1)}, bf16[576,768]{1,0:T(8,128)(2,1)S(1)}, u32[]{:S(2)}, u32[]{:S(2)}) %collective-permute-start.9) | collective-permute-done | bytes 884768 | tf_op jit(solution)/shard_map/ppermute | solution.py:584
  58.9 8.0 %collective-permute-done.8.refs_6_ = bf16[576,768]{1,0:T(8,128)(2,1)} collective-permute-done((bf16[576,768]{1,0:T(8,128)(2,1)}, bf16[576,768]{1,0:T(8,128)(2,1)}, u32[]{:S(2)}, u32[]{:S(2)}) %collective-permute-start.8) | collective-permute-done | bytes 884768 | tf_op jit(solution)/shard_map/ppermute | solution.py:584
  69.0 7.3 %collective-permute-done.13.refs_11_ = bf16[576,768]{1,0:T(8,128)(2,1)S(1)} collective-permute-done((bf16[576,768]{1,0:T(8,128)(2,1)S(1)}, bf16[576,768]{1,0:T(8,128)(2,1)S(1)}, u32[]{:S(2)}, u32[]{:S(2)}) %collective-permute-start.13) | collective-permute-done | bytes 884768 | tf_op jit(solution)/shard_map/ppermute | solution.py:584
  78.0 7.8 %collective-permute-done.12.refs_10_ = bf16[576,768]{1,0:T(8,128)(2,1)S(1)} collective-permute-done((bf16[576,768]{1,0:T(8,128)(2,1)}, bf16[576,768]{1,0:T(8,128)(2,1)S(1)}, u32[]{:S(2)}, u32[]{:S(2)}) %collective-permute-start.12) | collective-permute-done | bytes 884768 | tf_op jit(solution)/shard_map/ppermute | solution.py:584
  88.0 2.5 collective-permute-done.18.refs_16_
  90.5 4.7 %collective-permute-done.16.refs_14_ = bf16[288,768]{1,0:T(8,128)(2,1)S(1)} collective-permute-done((bf16[288,768]{1,0:T(8,128)(2,1)S(1)}, bf16[288,768]{1,0:T(8,128)(2,1)S(1)}, u32[]{:S(2)}, u32[]{:S(2)}) %collective-permute-start.16) | collective-permute-done | bytes 442400 | tf_op jit(solution)/shard_map/ppermute | solution.py:584
  97.8 12.5 %attend.1 = (bf16[56,768]{1,0:T(8,128)(2,1)}, bf16[912,768]{1,0:T(8,128)(2,1)}, bf16[912,768]{1,0:T(8,128)(2,1)}, f32[3,224,912]{2,1,0:T(8,128)}, bf16[3,16,224]...) custom-call(s32[16]{0:T(128)} %compare_select_fusion.2.table_ref, ...), custom_call_target="tpu_custom_call" | custom-call | flops 10000000000 | bytes 20000000 | tf_op jit(solution)/shard_map/attend/pallas_call | solution.py:66
  113.8 7.1 %feed.1 = (f32[56,3072]{1,0:T(8,128)}, bf16[56,3072]{1,0:T(8,128)(2,1)}, f32[56,768]{1,0:T(8,128)}, f32[56,128]{1,0:T(8,128)}, bf16[56,768]{1,0:T(8,128)(2,1)}) custom-call(s32[16]{0:T(128)} %compare_select_fusion.2.table_ref, bf16[576,768]{1,0:T(8,128)(2,1)} %copy-done.3, bf16[576,768]{1,0:T(8,128)(2,1)} %fusion.refs_1_, ...), custom_call_target="tpu_custom_call" | custom-call | flops 6000000000 | bytes 12000000 | tf_op jit(solution)/shard_map/feed/pallas_call | solution.py:66
  122.6 2.6 collective-permute-start.23
  127.1 5.5 %collective-permute-done.23 = bf16[56,768]{1,0:T(8,128)(2,1)S(1)} collective-permute-done((bf16[56,768]{1,0:T(8,128)(2,1)}, bf16[56,768]{1,0:T(8,128)(2,1)S(1)}, u32[]{:S(2)}, u32[]{:S(2)}) %collective-permute-start.23) | collective-permute-done | bytes 86048 | tf_op jit(solution)/shard_map/ppermute | solution.py:552
  135.2 4.8 %collective-permute-start.27 = (bf16[96,768]{1,0:T(8,128)(2,1)S(1)}, bf16[96,768]{1,0:T(8,128)(2,1)S(1)}, u32[]{:S(2)}, u32[]{:S(2)}) collective-permute-start(bf16[96,768]{1,0:T(8,128)(2,1)S(1)} %pad_maximum_fusion.4), channel_id=1, source_target_pairs={{0,16},{1,17},{2,18},{3,19},{4,20},{5,21},{6,22},{7,23},{8,24},{9,... | collective-permute-start | bytes 442376 | tf_op jit(solution)/shard_map/ppermute | solution.py:894
  143.8 4.6 %collective-permute-done.28 = bf16[96,768]{1,0:T(8,128)(2,1)S(1)} collective-permute-done((bf16[96,768]{1,0:T(8,128)(2,1)S(1)}, bf16[96,768]{1,0:T(8,128)(2,1)S(1)}, u32[]{:S(2)}, u32[]{:S(2)}) %collective-permute-start.28) | collective-permute-done | bytes 147488 | tf_op jit(solution)/shard_map/ppermute | solution.py:552
  151.1 4.0 %loss.1 = (f32[56,768]{1,0:T(8,128)}, bf16[56,768]{1,0:T(8,128)(2,1)}) custom-call(bf16[448,768]{1,0:T(8,128)(2,1)} %copy-done.11, bf16[448,768]{1,0:T(8,128)(2,1)} %copy-done.22, bf16[192,768]{1,0:T(8,128)(2,1)} %copy-done.9, bf16[192,768]{1,0:T(8,128)(2,1)} %copy-done.29, f32[448,1]{1,0:T(8,128)} %constant.173.clone.row_bias_ref, ...), custom_call_target="tpu_custom_call" | custom-call | flops 5000000000 | bytes 10000000 | tf_op jit(solution)/shard_map/loss/pallas_call | solution.py:66
  156.8 9.3 %feed_back.1 = (bf16[56,3072]{1,0:T(8,128)(2,1)}, f32[56,768]{1,0:T(8,128)}, bf16[56,768]{1,0:T(8,128)(2,1)}, f32[8,768]{1,0:T(8,128)}, bf16[56,768]{1,0:T(8,128)(2,1)}) custom-call(s32[16]{0:T(128)} %compare_select_fusion.2.table_ref, bf16[576,768]{1,0:T(8,128)(2,1)} %copy-done.3, bf16[576,768]{1,0:T(8,128)(2,1)} %fusion.refs_1_, ...), custom_call_target="tpu_custom_call" | custom-call | flops 7000000000 | bytes 14000000 | tf_op jit(solution)/shard_map/feed_back/pallas_call | solution.py:66
  170.6 5.9 %attend_back.1 = (bf16[56,768]{1,0:T(8,128)(2,1)}, bf16[864,384]{1,0:T(8,128)(2,1)}, f32[864,384]{1,0:T(8,128)}, f32[8,768]{1,0:T(8,128)}, f32[768,768]{1,0:T(8,128)}) custom-call(s32[16]{0:T(128)} %compare_select_fusion.2.table_ref, bf16[576,768]{1,0:T(8,128)(2,1)} %copy-done.3, bf16[576,768]{1,0:T(8,128)(2,1)} %fusion.refs_1_, ...), custom_call_target="tpu_custom_call" | custom-call | flops 16000000000 | bytes 32000000 | tf_op jit(solution)/shard_map/attend_back/pallas_call | solution.py:66
  176.5 3.1 %collective-permute-done.31.late_ref = bf16[56,2304]{1,0:T(8,128)(2,1)S(1)} collective-permute-done((bf16[56,2304]{1,0:T(8,128)(2,1)S(1)}, bf16[56,2304]{1,0:T(8,128)(2,1)S(1)}, u32[]{:S(2)}, u32[]{:S(2)}) %collective-permute-start.31) | collective-permute-done | bytes 258080 | tf_op jit(solution)/shard_map/ppermute | solution.py:941
  180.3 6.4 %value_grad.1 = f32[768,768]{1,0:T(8,128)} custom-call(s32[1]{0:T(128)} %bitcast.8.text_ref.refs_18_, bf16[3,16,224]{2,1,0:T(8,128)(2,1)} %copy-done.33, bf16[56,768]{1,0:T(8,128)(2,1)} %copy-done.31, bf16[912,768]{1,0:T(8,128)(2,1)} %get-tuple-element.148.refs_26_.normed_hbm, ...), custom_call_target="tpu_custom_call", output_to_operand_aliasing={{}: (7, {})} | custom-call | flops 5000000000 | bytes 10000000 | tf_op jit(solution)/shard_map/value_grad/pallas_call | solution.py:66
  192.7 3.0 %collective-permute-done.32.query_ref = bf16[56,768]{1,0:T(8,128)(2,1)S(1)} collective-permute-done((bf16[56,768]{1,0:T(8,128)(2,1)}, bf16[56,768]{1,0:T(8,128)(2,1)S(1)}, u32[]{:S(2)}, u32[]{:S(2)}) %collective-permute-start.32) | collective-permute-done | bytes 86048 | tf_op jit(solution)/shard_map/ppermute | solution.py:973
  197.9 2.8 %collective-permute-start.38 = (f32[2,1,2,1,24,768]{5,4,3,2,1,0:T(8,128)S(1)}, f32[2,1,2,1,24,768]{5,4,3,2,1,0:T(8,128)S(1)}, u32[]{:S(2)}, u32[]{:S(2)}) collective-permute-start(f32[2,1,2,1,24,768]{5,4,3,2,1,0:T(8,128)S(1)} %constant_dynamic-slice_fusion.1), channel_id=1, source_target_pairs={{0,4},{1,5},{2,6},{3,7},{4,0},{5,1},{6,2},{7,3},{8,12},{9,13},{10,... | collective-permute-start | bytes 884744 | tf_op jit(solution)/shard_map/ppermute | solution.py:552
  205.3 5.9 %all-to-all-start = ((bf16[16,56,288]{2,1,0:T(8,128)(2,1)}), bf16[16,56,288]{2,1,0:T(8,128)(2,1)S(1)}, u32[]{:S(2)}, u32[]{:S(2)}) async-start(bf16[16,56,288]{2,1,0:T(8,128)(2,1)} %pack.1), calls=%async_computation | async-start | bytes 1376256 | tf_op jit(solution)/shard_map/all_to_all | solution.py:1017
  213.9 8.9 %collective-permute-done.39 = f32[2,1,1,1,24,768]{5,4,3,2,1,0:T(8,128)S(1)} collective-permute-done((f32[2,1,1,1,24,768]{5,4,3,2,1,0:T(8,128)S(1)}, f32[2,1,1,1,24,768]{5,4,3,2,1,0:T(8,128)S(1)}, u32[]{:S(2)}, u32[]{:S(2)}) %collective-permute-start.39) | collective-permute-done | bytes 147488 | tf_op jit(solution)/shard_map/ppermute | solution.py:552
  224.8 2.9 %collective-permute-start.35 = (f32[2,1,1,1,24,768]{5,4,3,2,1,0:T(8,128)S(1)}, f32[2,1,1,1,24,768]{5,4,3,2,1,0:T(8,128)S(1)}, u32[]{:S(2)}, u32[]{:S(2)}) collective-permute-start(f32[2,1,1,1,24,768]{5,4,3,2,1,0:T(8,128)S(1)} %constant_dynamic-slice_fusion.3), channel_id=1, source_target_pairs={{0,4},{1,5},{2,6},{3,7},{4,0},{5,1},{6,2},{7,3},{8,12},{9,13},{10,... | collective-permute-start | bytes 442376 | tf_op jit(solution)/shard_map/ppermute | solution.py:552
  227.8 5.4 %collective-permute-done.40 = f32[1,1,1,1,24,768]{5,4,3,2,1,0:T(8,128)S(1)} collective-permute-done((f32[1,1,1,1,24,768]{5,4,3,2,1,0:T(8,128)S(1)}, f32[1,1,1,1,24,768]{5,4,3,2,1,0:T(8,128)S(1)}, u32[]{:S(2)}, u32[]{:S(2)}) %collective-permute-start.40) | collective-permute-done | bytes 73760 | tf_op jit(solution)/shard_map/ppermute | solution.py:552
  235.4 4.4 %owner.1 = (f32[288,768]{1,0:T(8,128)}, f32[8,768]{1,0:T(8,128)}) custom-call(s32[7]{0:T(128)} %stack.68.info_ref, bf16[896,288]{1,0:T(8,128)(2,1)} %bitcast.39, bf16[3,896,768]{2,1,0:T(8,128)(2,1)} %all-gather.2.cloned.1.call-done.b0_ref.b1_ref, bf16[3,896,768]{2,1,0:T(8,128)(2,1)} %all-gather.2.cloned.1.call-done.b0_ref.b1_ref, ...), custom_call_target="tpu_custom_call" | custom-call | flops 4000000000 | bytes 8000000 | tf_op jit(solution)/shard_map/owner/pallas_call | solution.py:1019
  244.7 2.9 %collective-permute-done.43 = f32[8,768]{1,0:T(8,128)S(1)} collective-permute-done((f32[8,768]{1,0:T(8,128)S(1)}, f32[8,768]{1,0:T(8,128)S(1)}, u32[]{:S(2)}, u32[]{:S(2)}) %collective-permute-start.43) | collective-permute-done | bytes 24608 | tf_op jit(solution)/shard_map/ppermute | solution.py:710
  248.4 2.9 %collective-permute-start.45 = (f32[8,768]{1,0:T(8,128)S(1)}, f32[8,768]{1,0:T(8,128)S(1)}, u32[]{:S(2)}, u32[]{:S(2)}) collective-permute-start(f32[8,768]{1,0:T(8,128)S(1)} %add_add_fusion.1), channel_id=1, source_target_pairs={{0,8},{1,9},{2,10},{3,11},{4,12},{5,13},{6,14},{7,15},{8,0},{9,1},... | collective-permute-start | bytes 73736 | tf_op jit(solution)/shard_map/ppermute | solution.py:552
  254.2 3.2 %collective-permute-start.44 = (f32[8,768]{1,0:T(8,128)S(1)}, f32[8,768]{1,0:T(8,128)S(1)}, u32[]{:S(2)}, u32[]{:S(2)}) collective-permute-start(f32[8,768]{1,0:T(8,128)S(1)} %add_add_fusion.1), channel_id=1, source_target_pairs={{0,4},{1,5},{2,6},{3,7},{4,0},{5,1},{6,2},{7,3},{8,12},{9,13},{10,... | collective-permute-start | bytes 73736 | tf_op jit(solution)/shard_map/ppermute | solution.py:552
  261.6 4.7 %update.1 = (f32[288,768]{1,0:T(8,128)}, f32[288,768]{1,0:T(8,128)}, f32[288,768]{1,0:T(8,128)}, f32[288,768]{1,0:T(8,128)}, f32[4,768]{1,0:T(4,128)}, /*index=5...) custom-call(f32[8,768]{1,0:T(8,128)} %add.211.stats_ref, ...), custom_call_target="tpu_custom_call" | custom-call | flops 5000000000 | bytes 10000000 | tf_op jit(solution)/shard_map/update/pallas_call | solution.py:66
  (232 shorter events, 83.9 us)
Async XLA Ops:
  7.2 227.4 %all-gather.2.cloned.1.call-start = ((), (), s32[]{:S(2)}) async-start(), calls=%async_computation.1 | async-start | bytes 4386816 | tf_op jit(solution)/shard_map/all_gather | solution.py:919
  12.2 14.5 %collective-permute-start.2 = (bf16[288,768]{1,0:T(8,128)(2,1)S(1)}, bf16[288,768]{1,0:T(8,128)(2,1)}, u32[]{:S(2)}, u32[]{:S(2)}) collective-permute-start(bf16[288,768]{1,0:T(8,128)(2,1)S(1)} %convert_element_type.37), channel_id=1, source_target_pairs={{0,16},{1,17},{2,18},{3,19},{4,20},{5,21},{6,22},{7,23},{8,24},{9,... | collective-permute-start | bytes 1327112 | tf_op jit(solution)/shard_map/ppermute | solution.py:596
  18.1 16.7 %collective-permute-start.4 = (bf16[576,768]{1,0:T(8,128)(2,1)}, bf16[576,768]{1,0:T(8,128)(2,1)}, u32[]{:S(2)}, u32[]{:S(2)}) collective-permute-start(bf16[576,768]{1,0:T(8,128)(2,1)} %fusion.refs_1_), channel_id=1, source_target_pairs={{0,4},{1,3},{4,8},{5,1},{8,12},{9,5},{12,14},{13,9},{14,10},{15,13... | collective-permute-start | bytes 2654216 | tf_op jit(solution)/shard_map/ppermute | solution.py:584
  34.8 16.8 %collective-permute-start.5 = (bf16[576,768]{1,0:T(8,128)(2,1)S(1)}, bf16[576,768]{1,0:T(8,128)(2,1)}, u32[]{:S(2)}, u32[]{:S(2)}) collective-permute-start(bf16[576,768]{1,0:T(8,128)(2,1)S(1)} %fusion.1.refs_0_), channel_id=1, source_target_pairs={{0,4},{1,3},{4,8},{5,1},{8,12},{9,5},{12,14},{13,9},{14,10},{15,13... | collective-permute-start | bytes 2654216 | tf_op jit(solution)/shard_map/ppermute | solution.py:584
  37.2 20.2 %collective-permute-start.9 = (bf16[576,768]{1,0:T(8,128)(2,1)}, bf16[576,768]{1,0:T(8,128)(2,1)S(1)}, u32[]{:S(2)}, u32[]{:S(2)}) collective-permute-start(bf16[576,768]{1,0:T(8,128)(2,1)} %collective-permute-done.4.refs_3_), channel_id=1, source_target_pairs={{0,4},{1,3},{4,8},{5,1},{8,12},{9,5},{12,14},{13,9},{14,10},{15,13... | collective-permute-start | bytes 2654216 | tf_op jit(solution)/shard_map/ppermute | solution.py:584
  51.6 15.3 %collective-permute-start.8 = (bf16[576,768]{1,0:T(8,128)(2,1)}, bf16[576,768]{1,0:T(8,128)(2,1)}, u32[]{:S(2)}, u32[]{:S(2)}) collective-permute-start(bf16[576,768]{1,0:T(8,128)(2,1)} %collective-permute-done.5.refs_2_), channel_id=1, source_target_pairs={{0,4},{1,3},{4,8},{5,1},{8,12},{9,5},{12,14},{13,9},{14,10},{15,13... | collective-permute-start | bytes 2654216 | tf_op jit(solution)/shard_map/ppermute | solution.py:584
  57.4 19.0 %collective-permute-start.13 = (bf16[576,768]{1,0:T(8,128)(2,1)S(1)}, bf16[576,768]{1,0:T(8,128)(2,1)S(1)}, u32[]{:S(2)}, u32[]{:S(2)}) collective-permute-start(bf16[576,768]{1,0:T(8,128)(2,1)S(1)} %collective-permute-done.9.refs_7_), channel_id=1, source_target_pairs={{0,4},{1,3},{4,8},{5,1},{8,12},{9,5},{12,14},{13,9},{14,10},{15,13... | collective-permute-start | bytes 2654216 | tf_op jit(solution)/shard_map/ppermute | solution.py:584
  67.0 18.9 %collective-permute-start.12 = (bf16[576,768]{1,0:T(8,128)(2,1)}, bf16[576,768]{1,0:T(8,128)(2,1)S(1)}, u32[]{:S(2)}, u32[]{:S(2)}) collective-permute-start(bf16[576,768]{1,0:T(8,128)(2,1)} %collective-permute-done.8.refs_6_), channel_id=1, source_target_pairs={{0,4},{1,3},{4,8},{5,1},{8,12},{9,5},{12,14},{13,9},{14,10},{15,13... | collective-permute-start | bytes 2654216 | tf_op jit(solution)/shard_map/ppermute | solution.py:584
  68.5 17.3 %collective-permute-start.7 = (bf16[576,768]{1,0:T(8,128)(2,1)}, bf16[576,768]{1,0:T(8,128)(2,1)}, u32[]{:S(2)}, u32[]{:S(2)}) collective-permute-start(bf16[576,768]{1,0:T(8,128)(2,1)} %collective-permute-done.4.refs_3_), channel_id=1, source_target_pairs={{0,1},{1,0},{2,3},{3,2},{4,5},{5,4},{6,7},{7,6},{8,9},{9,8},{10,11... | collective-permute-start | bytes 2654216 | tf_op jit(solution)/shard_map/ppermute | solution.py:581
  68.5 17.9 %collective-permute-start.6 = (bf16[576,768]{1,0:T(8,128)(2,1)}, bf16[576,768]{1,0:T(8,128)(2,1)}, u32[]{:S(2)}, u32[]{:S(2)}) collective-permute-start(bf16[576,768]{1,0:T(8,128)(2,1)} %collective-permute-done.5.refs_2_), channel_id=1, source_target_pairs={{0,1},{1,0},{2,3},{3,2},{4,5},{5,4},{6,7},{7,6},{8,9},{9,8},{10,11... | collective-permute-start | bytes 2654216 | tf_op jit(solution)/shard_map/ppermute | solution.py:581
  69.0 19.0 %collective-permute-start.11 = (bf16[576,768]{1,0:T(8,128)(2,1)S(1)}, bf16[576,768]{1,0:T(8,128)(2,1)}, u32[]{:S(2)}, u32[]{:S(2)}) collective-permute-start(bf16[576,768]{1,0:T(8,128)(2,1)S(1)} %collective-permute-done.9.refs_7_), channel_id=1, source_target_pairs={{0,1},{1,0},{2,3},{3,2},{4,5},{5,4},{6,7},{7,6},{8,9},{9,8},{10,11... | collective-permute-start | bytes 2654216 | tf_op jit(solution)/shard_map/ppermute | solution.py:581
  76.4 14.2 %collective-permute-start.18 = (bf16[288,768]{1,0:T(8,128)(2,1)S(1)}, bf16[288,768]{1,0:T(8,128)(2,1)S(1)}, u32[]{:S(2)}, u32[]{:S(2)}) collective-permute-start(bf16[288,768]{1,0:T(8,128)(2,1)S(1)} %constant_dynamic-slice_fusion.6), channel_id=1, source_target_pairs={{0,4},{1,3},{4,8},{5,1},{8,12},{9,5},{12,14},{13,9},{14,10},{15,13... | collective-permute-start | bytes 1327112 | tf_op jit(solution)/shard_map/ppermute | solution.py:584
  85.8 9.5 %collective-permute-start.10 = (bf16[576,768]{1,0:T(8,128)(2,1)}, bf16[576,768]{1,0:T(8,128)(2,1)S(1)}, u32[]{:S(2)}, u32[]{:S(2)}) collective-permute-start(bf16[576,768]{1,0:T(8,128)(2,1)} %collective-permute-done.8.refs_6_), channel_id=1, source_target_pairs={{0,1},{1,0},{2,3},{3,2},{4,5},{5,4},{6,7},{7,6},{8,9},{9,8},{10,11... | collective-permute-start | bytes 2654216 | tf_op jit(solution)/shard_map/ppermute | solution.py:581
  85.9 9.5 %collective-permute-start.15 = (bf16[576,768]{1,0:T(8,128)(2,1)S(1)}, bf16[576,768]{1,0:T(8,128)(2,1)S(1)}, u32[]{:S(2)}, u32[]{:S(2)}) collective-permute-start(bf16[576,768]{1,0:T(8,128)(2,1)S(1)} %collective-permute-done.13.refs_11_), channel_id=1, source_target_pairs={{0,1},{1,0},{2,3},{3,2},{4,5},{5,4},{6,7},{7,6},{8,9},{9,8},{10,11... | collective-permute-start | bytes 2654216 | tf_op jit(solution)/shard_map/ppermute | solution.py:581
  86.4 8.9 %collective-permute-start.16 = (bf16[288,768]{1,0:T(8,128)(2,1)S(1)}, bf16[288,768]{1,0:T(8,128)(2,1)S(1)}, u32[]{:S(2)}, u32[]{:S(2)}) collective-permute-start(bf16[288,768]{1,0:T(8,128)(2,1)S(1)} %constant_dynamic-slice_fusion.7), channel_id=1, source_target_pairs={{0,4},{1,3},{4,8},{5,1},{8,12},{9,5},{12,14},{13,9},{14,10},{15,13... | collective-permute-start | bytes 1327112 | tf_op jit(solution)/shard_map/ppermute | solution.py:584
  111.2 9.8 %collective-permute-start.20 = (bf16[56,1536]{1,0:T(8,128)(2,1)S(1)}, bf16[56,1536]{1,0:T(8,128)(2,1)S(1)}, u32[]{:S(2)}, u32[]{:S(2)}) collective-permute-start(bf16[56,1536]{1,0:T(8,128)(2,1)S(1)} %pad_maximum_fusion.3), channel_id=1, source_target_pairs={{16,0},{17,1},{18,2},{19,3},{20,4},{21,5},{22,6},{23,7},{24,8},{25... | collective-permute-start | bytes 516104 | tf_op jit(solution)/shard_map/ppermute | solution.py:864
  112.5 8.5 %collective-permute-start.21 = (bf16[3,16,224]{2,1,0:T(8,128)(2,1)}, bf16[3,16,224]{2,1,0:T(8,128)(2,1)S(1)}, u32[]{:S(2)}, u32[]{:S(2)}) collective-permute-start(bf16[3,16,224]{2,1,0:T(8,128)(2,1)} %get-tuple-element.131), channel_id=1, source_target_pairs={{16,0},{17,1},{18,2},{19,3},{20,4},{21,5},{22,6},{23,7},{24,8},{25... | collective-permute-start | bytes 64520 | tf_op jit(solution)/shard_map/ppermute | solution.py:865
  122.6 10.0 %collective-permute-start.23 = (bf16[56,768]{1,0:T(8,128)(2,1)}, bf16[56,768]{1,0:T(8,128)(2,1)S(1)}, u32[]{:S(2)}, u32[]{:S(2)}) collective-permute-start(bf16[56,768]{1,0:T(8,128)(2,1)} %get-tuple-element.132.emb_ref), channel_id=1, source_target_pairs={{0,8},{1,9},{2,10},{3,11},{4,12},{5,13},{6,14},{7,15},{8,0},{9,1},... | collective-permute-start | bytes 258056 | tf_op jit(solution)/shard_map/ppermute | solution.py:552
  133.5 8.5 %collective-permute-start.25 = (bf16[224,768]{1,0:T(8,128)(2,1)S(1)}, bf16[224,768]{1,0:T(8,128)(2,1)S(1)}, u32[]{:S(2)}, u32[]{:S(2)}) collective-permute-start(bf16[224,768]{1,0:T(8,128)(2,1)S(1)} %pad_maximum_fusion), channel_id=1, source_target_pairs={{0,2},{1,3},{2,0},{3,1},{4,6},{5,7},{6,4},{7,5},{8,10},{9,11},{10,... | collective-permute-start | bytes 1032200 | tf_op jit(solution)/shard_map/ppermute | solution.py:552
  142.1 8.0 %collective-permute-start.26 = (bf16[448,768]{1,0:T(8,128)(2,1)S(1)}, bf16[448,768]{1,0:T(8,128)(2,1)S(1)}, u32[]{:S(2)}, u32[]{:S(2)}) collective-permute-start(bf16[448,768]{1,0:T(8,128)(2,1)S(1)} %constant_dynamic-update-slice_fusion.text_a_ref), channel_id=1, source_target_pairs={{0,1},{1,0},{2,3},{3,2},{4,5},{5,4},{6,7},{7,6},{8,9},{9,8},{10,11... | collective-permute-start | bytes 2064392 | tf_op jit(solution)/shard_map/ppermute | solution.py:552
  166.1 10.4 %collective-permute-start.30 = (bf16[56,768]{1,0:T(8,128)(2,1)}, bf16[56,768]{1,0:T(8,128)(2,1)S(1)}, u32[]{:S(2)}, u32[]{:S(2)}) collective-permute-start(bf16[56,768]{1,0:T(8,128)(2,1)} %get-tuple-element.141.refs_19_), channel_id=1, source_target_pairs={{16,0},{17,1},{18,2},{19,3},{20,4},{21,5},{22,6},{23,7},{24,8},{25... | collective-permute-start | bytes 258056 | tf_op jit(solution)/shard_map/ppermute | solution.py:940
  169.3 10.3 %collective-permute-start.31 = (bf16[56,2304]{1,0:T(8,128)(2,1)S(1)}, bf16[56,2304]{1,0:T(8,128)(2,1)S(1)}, u32[]{:S(2)}, u32[]{:S(2)}) collective-permute-start(bf16[56,2304]{1,0:T(8,128)(2,1)S(1)} %pad_maximum_fusion.2), channel_id=1, source_target_pairs={{16,0},{17,1},{18,2},{19,3},{20,4},{21,5},{22,6},{23,7},{24,8},{25... | collective-permute-start | bytes 774152 | tf_op jit(solution)/shard_map/ppermute | solution.py:941
  196.4 8.9 %collective-permute-start.34 = (f32[2,2,1,1,24,768]{5,4,3,2,1,0:T(8,128)S(1)}, f32[2,2,1,1,24,768]{5,4,3,2,1,0:T(8,128)S(1)}, u32[]{:S(2)}, u32[]{:S(2)}) collective-permute-start(f32[2,2,1,1,24,768]{5,4,3,2,1,0:T(8,128)S(1)} %constant_dynamic-slice_fusion.4), channel_id=1, source_target_pairs={{0,2},{1,3},{2,0},{3,1},{4,6},{5,7},{6,4},{7,5},{8,10},{9,11},{10,... | collective-permute-start | bytes 884744 | tf_op jit(solution)/shard_map/ppermute | solution.py:552
  197.9 15.2 %collective-permute-start.38 = (f32[2,1,2,1,24,768]{5,4,3,2,1,0:T(8,128)S(1)}, f32[2,1,2,1,24,768]{5,4,3,2,1,0:T(8,128)S(1)}, u32[]{:S(2)}, u32[]{:S(2)}) collective-permute-start(f32[2,1,2,1,24,768]{5,4,3,2,1,0:T(8,128)S(1)} %constant_dynamic-slice_fusion.1), channel_id=1, source_target_pairs={{0,4},{1,5},{2,6},{3,7},{4,0},{5,1},{6,2},{7,3},{8,12},{9,13},{10,... | collective-permute-start | bytes 884744 | tf_op jit(solution)/shard_map/ppermute | solution.py:552
  200.7 32.4 %collective-permute-start.36 = (bf16[864,384]{1,0:T(8,128)(2,1)}, bf16[864,384]{1,0:T(8,128)(2,1)S(1)}, u32[]{:S(2)}, u32[]{:S(2)}) collective-permute-start(bf16[864,384]{1,0:T(8,128)(2,1)} %get-tuple-element.167), channel_id=1, source_target_pairs={{16,0},{17,1},{18,2},{19,3},{20,4},{21,5},{22,6},{23,7},{24,8},{25... | collective-permute-start | bytes 1990664 | tf_op jit(solution)/shard_map/ppermute | solution.py:1011
  205.3 29.3 %all-to-all-start = ((bf16[16,56,288]{2,1,0:T(8,128)(2,1)}), bf16[16,56,288]{2,1,0:T(8,128)(2,1)S(1)}, u32[]{:S(2)}, u32[]{:S(2)}) async-start(bf16[16,56,288]{2,1,0:T(8,128)(2,1)} %pack.1), calls=%async_computation | async-start | bytes 1376256 | tf_op jit(solution)/shard_map/all_to_all | solution.py:1017
  213.2 9.6 %collective-permute-start.39 = (f32[2,1,1,1,24,768]{5,4,3,2,1,0:T(8,128)S(1)}, f32[2,1,1,1,24,768]{5,4,3,2,1,0:T(8,128)S(1)}, u32[]{:S(2)}, u32[]{:S(2)}) collective-permute-start(f32[2,1,1,1,24,768]{5,4,3,2,1,0:T(8,128)S(1)} %constant_dynamic-slice_fusion), channel_id=1, source_target_pairs={{0,2},{1,3},{2,0},{3,1},{4,6},{5,7},{6,4},{7,5},{8,10},{9,11},{10,... | collective-permute-start | bytes 442376 | tf_op jit(solution)/shard_map/ppermute | solution.py:552
  222.8 10.3 %collective-permute-start.40 = (f32[1,1,1,1,24,768]{5,4,3,2,1,0:T(8,128)S(1)}, f32[1,1,1,1,24,768]{5,4,3,2,1,0:T(8,128)S(1)}, u32[]{:S(2)}, u32[]{:S(2)}) collective-permute-start(f32[1,1,1,1,24,768]{5,4,3,2,1,0:T(8,128)S(1)} %constant_dynamic-slice_fusion.8), channel_id=1, source_target_pairs={{0,8},{1,9},{2,10},{3,11},{4,12},{5,13},{6,14},{7,15},{8,0},{9,1},... | collective-permute-start | bytes 221192 | tf_op jit(solution)/shard_map/ppermute | solution.py:552
  224.8 9.6 %collective-permute-start.35 = (f32[2,1,1,1,24,768]{5,4,3,2,1,0:T(8,128)S(1)}, f32[2,1,1,1,24,768]{5,4,3,2,1,0:T(8,128)S(1)}, u32[]{:S(2)}, u32[]{:S(2)}) collective-permute-start(f32[2,1,1,1,24,768]{5,4,3,2,1,0:T(8,128)S(1)} %constant_dynamic-slice_fusion.3), channel_id=1, source_target_pairs={{0,4},{1,5},{2,6},{3,7},{4,0},{5,1},{6,2},{7,3},{8,12},{9,13},{10,... | collective-permute-start | bytes 442376 | tf_op jit(solution)/shard_map/ppermute | solution.py:552
  251.3 9.4 %collective-permute-start.49 = (f32[96,768]{1,0:T(8,128)S(1)}, f32[96,768]{1,0:T(8,128)S(1)}, u32[]{:S(2)}, u32[]{:S(2)}) collective-permute-start(f32[96,768]{1,0:T(8,128)S(1)} %maximum_select_fusion.2), channel_id=1, source_target_pairs={{18,3},{24,4},{30,5},{4,6},{10,7}} | collective-permute-start | bytes 884744 | tf_op jit(solution)/shard_map/ppermute | solution.py:1061
  252.0 8.7 %collective-permute-start.50 = (f32[96,768]{1,0:T(8,128)S(1)}, f32[96,768]{1,0:T(8,128)S(1)}, u32[]{:S(2)}, u32[]{:S(2)}) collective-permute-start(f32[96,768]{1,0:T(8,128)S(1)} %maximum_select_fusion.2), channel_id=1, source_target_pairs={{21,3},{27,4},{1,5},{7,6},{13,7}} | collective-permute-start | bytes 884744 | tf_op jit(solution)/shard_map/ppermute | solution.py:1061
  252.7 8.0 %collective-permute-start.51 = (f32[96,768]{1,0:T(8,128)S(1)}, f32[96,768]{1,0:T(8,128)S(1)}, u32[]{:S(2)}, u32[]{:S(2)}) collective-permute-start(f32[96,768]{1,0:T(8,128)S(1)} %maximum_select_fusion.2), channel_id=1, source_target_pairs={{16,2},{22,3},{28,4},{2,5},{8,6},{14,7}} | collective-permute-start | bytes 884744 | tf_op jit(solution)/shard_map/ppermute | solution.py:1061
  (57 other events, 351.2 us)
Sparse Core Ops, SparseCore 0:
  156.9 54.7 all-gather.1
